TPU v7x, 256 devices: a whole 4x4x8 slice. The times are simulated.
256 devices in a mesh: cls: 128 (over y, z, x), rep: 2 (over core).
Axes of the slice: x: 4, y: 4, z: 8, core: 2. Of those that a mesh axis runs over, the one named last changes fastest.
Arguments:
- queries: bfloat16 [2, 256, 768], P('rep', 'cls'), may hold values from -16 to 16
- positives: int32 [2, 256, 4], replicated, may hold values from -1 to 786431, as said below
- label_vectors: bfloat16 [786432, 768], P('cls'), may hold values from -80 to 80
- refresh_slot: int32 [], replicated, may hold values from 0 to 7
- features: bfloat16 [98304, 768], P(('cls', 'rep')), may hold values from -6 to 6
- encoder_weight: bfloat16 [768, 768], replicated, may hold values from -0.21875 to 0.21875
- encoder_gain: float32 [768], replicated, may hold values from 0.1 to 1.9
- free_vectors: bfloat16 [98304, 768], P(('cls', 'rep')), may hold values from -3 to 3
- targets: int32 [98304], replicated, may hold values from 0 to 98303, as said below
Outputs:
- loss: float32 [2, 256], P('rep', 'cls')
- query_grads: bfloat16 [2, 256, 768], P('rep', 'cls')
- refreshed_vectors: bfloat16 [98304, 768], P(('cls', 'rep'))
Inputs may be any that keep to these rules, and one draw needn't show every extreme that they name: `positives`: each row holds 1 to 4 label ids in its first places and -1 in the rest; ids may repeat within a row. `targets`: A permutation. Refreshed row t belongs to owner t // 768. The b-th aligned block of 384 entries names exactly 3 rows of every owner, all in the half b % 2 of that owner's 768 rows.
All inputs are finite; a program needn't handle non-finite values.
Results may differ from a plain program's by a relative error of at most 0.0048.
Values may be sent and summed in bfloat16 or wider, within the bound.
No kernel may reach another device: no remote copies, remote signals or barrier semaphores. Data moves between devices by JAX's collectives and lax.ppermute only.
A program may use at most 128 MiB of HBM per device.

v0:
```python
import jax
import jax.numpy as jnp
from jax import lax
from jax.sharding import Mesh
from jax.sharding import PartitionSpec as P

SLOTS = 8
CLS = ("cls_0", "cls_1", "cls_2")
CLS_REP = ("cls_0", "cls_1", "cls_2", "rep")


def from_partner(value, axis, bit):
    mask = 2**bit
    pairs = [(source, source ^ mask) for source in range(lax.axis_size(axis))]
    return lax.ppermute(value, axis, pairs)


def copy_for_each(shard, axis):
    length = lax.axis_size(axis)
    return lax.all_to_all(
        jnp.broadcast_to(shard[None], (length, *shard.shape)), axis, 0, 0, tiled=True
    )


def in_order(pieces, dim):
    dims = list(pieces.shape[1:])
    dims[dim] *= pieces.shape[0]
    return jnp.moveaxis(pieces, 0, dim).reshape(dims)


def whole_of(shard, axes, dim):
    far, near = axes
    pieces = copy_for_each(copy_for_each(shard, far), near)
    return in_order(pieces.swapaxes(0, 1).reshape(-1, *shard.shape), dim)


def taken_together(shard, axis):
    return copy_for_each(shard, axis).max(axis=0)


def over_axes(shard, axes):
    far, near = axes
    nearer = taken_together(shard, near)
    return taken_together(nearer, far)


def taken_together_2(shard, axis):
    everything = copy_for_each(shard, axis)
    return jnp.sum(everything, axis=0)


def one_axis_at_a_time(shard, axes):
    far, near = axes
    nearer = taken_together_2(shard, near)
    return taken_together_2(nearer, far)


def together(arrays, axis):
    ends = [0]
    for a in arrays:
        ends.append(ends[-1] + a.size)
    running = one_axis_at_a_time(jnp.concatenate([a.ravel() for a in arrays]), axis)
    return tuple((running[b:e].reshape(a.shape) for a, b, e in zip(arrays, ends, ends[1:])))


def split_up(shard, dim, length):
    dims = shard.shape
    pieces = shard.reshape(*dims[:dim], length, dims[dim] // length, *dims[dim + 1 :])
    return jnp.moveaxis(pieces, dim, 0)


def sum_at_owner(shard, axis, dim):
    pieces = split_up(shard, dim, lax.axis_size(axis))
    arrived = lax.all_to_all(pieces, axis, split_axis=0, concat_axis=0, tiled=True)
    return arrived.sum(axis=0)


def sum_in_two_steps(shard, axes, dim):
    far, near = axes
    pieces = split_up(shard, dim, lax.axis_size(far))
    nearer = sum_at_owner(pieces, near, dim + 1)
    arrived = lax.all_to_all(nearer, far, split_axis=0, concat_axis=0, tiled=True)
    return arrived.sum(axis=0)


def per_device(
    queries,
    positives,
    label_vectors,
    refresh_slot,
    features,
    encoder_weight,
    encoder_gain,
    free_vectors,
    targets,
):
    cls_count = lax.axis_size(CLS)
    rep_count = lax.axis_size("rep")
    cls_index = lax.axis_index(CLS)
    rep_index = lax.axis_index("rep")
    lab_rows = label_vectors.shape[0]
    feature_width = label_vectors.shape[1]
    slot_rows = lab_rows // SLOTS
    half_rows = slot_rows // rep_count
    per_owner = half_rows // cls_count
    query_rows = queries.shape[1]
    hidden = jnp.dot(features, encoder_weight, preferred_element_type=jnp.float32)
    normed = (
        hidden * lax.rsqrt(jnp.mean(hidden * hidden, axis=1, keepdims=True) + 1e-06) * encoder_gain
    )
    encoded = normed.astype(jnp.bfloat16)
    block_index = cls_index * rep_count + rep_index
    own_targets = lax.dynamic_slice_in_dim(targets, block_index * half_rows, half_rows)
    sending = encoded[jnp.argsort(own_targets)].reshape(cls_count, per_owner, feature_width)
    arrived = lax.all_to_all(sending, CLS, split_axis=0, concat_axis=0, tiled=True)
    by_source = lax.dynamic_index_in_dim(
        targets.reshape(cls_count, rep_count, half_rows), rep_index, 1, keepdims=False
    )
    row_offsets = by_source - (cls_index * slot_rows + rep_index * half_rows)
    kept_rows = (row_offsets >= 0) & (row_offsets < half_rows)
    row_keys = jnp.sort(jnp.where(kept_rows, row_offsets, half_rows), axis=1)[:, :per_owner]
    placed = arrived.reshape(half_rows, feature_width)[jnp.argsort(row_keys.reshape(-1))]
    refreshed = (free_vectors.astype(jnp.float32) + placed.astype(jnp.float32)).astype(jnp.bfloat16)
    partner = from_partner(refreshed, "rep", 0)
    first_half = jnp.where(rep_index == 0, refreshed, partner)
    second_half = jnp.where(rep_index == 0, partner, refreshed)
    fresh_block = jnp.concatenate([first_half, second_half], axis=0)
    current = lax.dynamic_update_slice(
        label_vectors, fresh_block, (refresh_slot * slot_rows, jnp.zeros((), jnp.int32))
    )
    own_queries = queries.reshape(query_rows, feature_width)
    first_label = cls_index * lab_rows
    label_ids = lax.dynamic_index_in_dim(positives, rep_index, 0, keepdims=False)
    logits = lax.dot_general(
        whole_of(own_queries, (("cls_0", "cls_1"), "cls_2"), 0),
        current,
        (((1,), (1,)), ((), ())),
        preferred_element_type=jnp.float32,
    )
    own_offset = cls_index * query_rows
    usable_count = current.shape[0]
    label_offsets = label_ids - first_label
    valid_ids = label_ids >= 0
    present = valid_ids & (label_offsets >= 0) & (label_offsets < usable_count)
    picked = jnp.take_along_axis(logits, jnp.clip(label_offsets, 0, usable_count - 1), axis=1)
    positive_part = jnp.sum(jnp.where(present, picked, 0.0), axis=1)
    local_peak = jnp.max(logits, axis=1)
    local_total = jnp.sum(jnp.exp(logits - local_peak[:, None]), axis=1)
    local_stats = (local_peak, local_total, positive_part)
    maxima = over_axes(local_stats[0], (("cls_0", "cls_1"), "cls_2"))
    exp_totals, positive_sums = together(
        (local_stats[1] * jnp.exp(local_stats[0] - maxima), local_stats[2]),
        (("cls_0", "cls_1"), "cls_2"),
    )
    log_total = maxima + jnp.log(exp_totals)
    id_count = jnp.sum(valid_ids.astype(jnp.float32), axis=1)
    loss_all = log_total - positive_sums / id_count
    inverse_count = 1.0 / id_count
    label_iota = jnp.arange(usable_count, dtype=jnp.int32)[None, :]
    target_mass = jnp.zeros(logits.shape, jnp.float32)
    for column in range(label_ids.shape[1]):
        matches = (label_offsets[:, column : column + 1] == label_iota) & present[
            :, column : column + 1
        ]
        target_mass = target_mass + jnp.where(matches, inverse_count[:, None], 0.0)
    coefficients = (jnp.exp(logits - log_total[:, None]) - target_mass).astype(jnp.bfloat16)
    own_grads = sum_in_two_steps(
        jnp.dot(coefficients, current, preferred_element_type=jnp.float32),
        (("cls_0", "cls_1"), "cls_2"),
        0,
    )
    own_loss = lax.dynamic_slice_in_dim(loss_all, own_offset, query_rows).reshape(1, query_rows)
    return (
        own_loss,
        own_grads.astype(jnp.bfloat16).reshape(1, query_rows, feature_width),
        refreshed,
    )


def solution(mesh):
    torus = Mesh(
        mesh.devices.reshape(4, 8, 4, mesh.shape["rep"]), ("cls_0", "cls_1", "cls_2", "rep")
    )
    placed = (
        P("rep", CLS, None),
        P(),
        P(CLS, None),
        P(),
        P(CLS_REP, None),
        P(),
        P(),
        P(CLS_REP, None),
        P(),
    )
    return jax.shard_map(
        per_device,
        mesh=torus,
        in_specs=placed,
        out_specs=(P("rep", CLS), P("rep", CLS, None), P(CLS_REP, None)),
        check_vma=False,
    )
```

profile of v0, /device:TPU:32, one launch (start us, length us, event | category | flops | bytes accessed | tf_op | source)
XLA Modules:
  0.0 240.9 jit_solution(14369495773253647212)
XLA Ops:
  7.2 8.1 %copy.43 = bf16[6144,768]{1,0:T(8,128)(2,1)} copy(bf16[6144,768]{1,0:T(8,128)(2,1)} %param.11) | data formatting | bytes 18874368
  15.3 3.8 %sort.39 = (s32[384]{0:T(512)}, s32[384]{0:T(512)S(1)}) sort(s32[384]{0:T(512)S(1)} %dynamic_slice.14, s32[384]{0:T(512)S(1)} %iota.11), dimensions={0}, to_apply=%region_1.0 | sort | flops 3456 | bytes 6144 | tf_op jit(solution)/shard_map/jit(argsort)/sort | solution.py:114
  19.2 0.7 multiply_reduce_fusion
  20.1 2.2 gather_fusion
  22.3 1.1 reshape.110
  23.3 15.1 %all-to-all-start = ((bf16[128,3,768]{2,1,0:T(4,128)(2,1)}), bf16[128,3,768]{2,1,0:T(4,128)(2,1)S(1)}, u32[]{:S(2)}, u32[]{:S(2)}) async-start(bf16[128,3,768]{2,1,0:T(4,128)(2,1)} %reshape.110), calls=%async_computation | async-start | bytes 1572864 | tf_op jit(solution)/shard_map/all_to_all | solution.py:115
  38.5 0.2 reshape.112
  38.8 0.2 dynamic-slice_subtract_fusion
  39.0 0.7 bitcast_select_fusion
  39.7 9.7 %sort.43.cloned.1.call-done = s32[128,384]{1,0:T(8,128)} async-done(((s32[128,384]{1,0:T(8,128)}), s32[128,384]{1,0:T(8,128)}) %sort.43.cloned.1.call-update) | async-done | bytes 196624 | tf_op jit(solution)/shard_map/jit(sort)/sort | solution.py:121
  49.4 0.8 slice.50
  50.2 0.2 reshape.113
  50.5 3.8 %sort.41 = (s32[384]{0:T(512)}, s32[384]{0:T(512)S(1)}) sort(s32[384]{0:T(512)S(1)} %reshape.113, s32[384]{0:T(512)S(1)} %iota.12), dimensions={0}, to_apply=%region_3.4 | sort | flops 3456 | bytes 6144 | tf_op jit(solution)/shard_map/jit(argsort)/sort | solution.py:122
  54.2 8.9 %all-to-all-done = bf16[128,3,768]{2,1,0:T(4,128)(2,1)S(1)} async-done(((bf16[128,3,768]{2,1,0:T(4,128)(2,1)}), bf16[128,3,768]{2,1,0:T(4,128)(2,1)S(1)}, u32[]{:S(2)}, u32[]{:S(2)}) %all-to-all-start) | async-done | bytes 589856 | tf_op jit(solution)/shard_map/all_to_all | solution.py:115
  63.1 0.7 broadcast_in_dim.89
  63.8 5.1 %all-to-all-start.1 = ((bf16[32,2,768]{2,1,0:T(2,128)(2,1)}), bf16[32,2,768]{2,1,0:T(2,128)(2,1)}, u32[]{:S(2)}, u32[]{:S(2)}) async-start(bf16[32,2,768]{2,1,0:T(2,128)(2,1)} %broadcast_in_dim.89), calls=%async_computation.1 | async-start | bytes 196608 | tf_op jit(solution)/shard_map/all_to_all | solution.py:20
  68.9 0.5 reshape.111
  69.4 2.2 gather_fusion.1
  72.0 6.4 %all-to-all-done.1 = bf16[32,2,768]{2,1,0:T(2,128)(2,1)} async-done(((bf16[32,2,768]{2,1,0:T(2,128)(2,1)}), bf16[32,2,768]{2,1,0:T(2,128)(2,1)}, u32[]{:S(2)}, u32[]{:S(2)}) %all-to-all-start.1) | async-done | bytes 98336 | tf_op jit(solution)/shard_map/all_to_all | solution.py:20
  78.4 1.8 broadcast_in_dim.90
  80.2 3.6 %all-to-all-start.2 = ((bf16[4,32,2,768]{3,2,1,0:T(2,128)(2,1)}), bf16[4,32,2,768]{3,2,1,0:T(2,128)(2,1)S(1)}, u32[]{:S(2)}, u32[]{:S(2)}) async-start(bf16[4,32,2,768]{3,2,1,0:T(2,128)(2,1)} %broadcast_in_dim.90), calls=%async_computation.2 | async-start | bytes 786432 | tf_op jit(solution)/shard_map/all_to_all | solution.py:20
  84.8 6.2 %all-to-all-done.2 = bf16[4,32,2,768]{3,2,1,0:T(2,128)(2,1)S(1)} async-done(((bf16[4,32,2,768]{3,2,1,0:T(2,128)(2,1)}), bf16[4,32,2,768]{3,2,1,0:T(2,128)(2,1)S(1)}, u32[]{:S(2)}, u32[]{:S(2)}) %all-to-all-start.2) | async-done | bytes 393248 | tf_op jit(solution)/shard_map/all_to_all | solution.py:20
  91.0 0.3 copy.20
  91.5 1.1 broadcast_select_fusion.1
  92.6 1.1 maximum_dynamic-update-slice_fusion
  93.7 9.0 %fusion.16 = (f32[256]{0:T(256)S(1)}, f32[6144,256]{1,0:T(8,128)}) fusion(bf16[6144,768]{1,0:T(8,128)(2,1)} %maximum_dynamic-update-slice_fusion, bf16[256,768]{1,0:T(8,128)(2,1)S(1)} %reshape_reshape.6), kind=kOutput, calls=%fused_computation.64 | convolution fusion | flops 2417491712 | bytes 16122880 | tf_op jit(solution)/shard_map/dot_general | solution.py:134
  102.8 0.6 broadcast_in_dim.91
  103.4 3.2 %all-to-all-start.3 = ((f32[4,1,256]{2,1,0:T(1,128)}), f32[4,1,256]{2,1,0:T(1,128)S(1)}, u32[]{:S(2)}, u32[]{:S(2)}) async-start(f32[4,1,256]{2,1,0:T(1,128)} %broadcast_in_dim.91), calls=%async_computation.3 | async-start | bytes 8192 | tf_op jit(solution)/shard_map/all_to_all | solution.py:20
  106.6 3.7 %exponential_reduce_fusion = f32[256]{0:T(256)S(1)} fusion(f32[256]{0:T(256)S(1)} %get-tuple-element.27, f32[6144,256]{1,0:T(8,128)} %get-tuple-element.28), kind=kLoop, calls=%fused_computation.8 | loop fusion | flops 3145472 | bytes 6293504 | tf_op jit(solution)/shard_map/reduce_sum | solution.py:148
  110.3 32.0 %gather_fusion.2 = f32[1024]{0:T(1024)S(1)} fusion(f32[256,6144]{0,1:T(8,128)} %bitcast.45, s32[1024]{0:T(1024)S(1)} %reshape.131), kind=kCustom, calls=%fused_computation.2 | custom fusion | bytes 16384 | tf_op jit(solution)/shard_map/jit(take_along_axis)/gather | solution.py:145
  142.4 0.6 broadcast_in_dim.92
  143.0 16.1 %all-to-all-start.4 = ((f32[32,1,256]{2,1,0:T(1,128)}), f32[32,1,256]{2,1,0:T(1,128)S(1)}, u32[]{:S(2)}, u32[]{:S(2)}) async-start(f32[32,1,256]{2,1,0:T(1,128)} %broadcast_in_dim.92), calls=%async_computation.4 | async-start | bytes 65536 | tf_op jit(solution)/shard_map/all_to_all | solution.py:20
  159.1 0.2 convert_reduce_fusion
  159.3 8.6 %all-to-all-done.4 = f32[32,1,256]{2,1,0:T(1,128)S(1)} async-done(((f32[32,1,256]{2,1,0:T(1,128)}), f32[32,1,256]{2,1,0:T(1,128)S(1)}, u32[]{:S(2)}, u32[]{:S(2)}) %all-to-all-start.4) | async-done | bytes 32800 | tf_op jit(solution)/shard_map/all_to_all | solution.py:20
  168.1 10.4 %all_to_all.49 = f32[4,1,512]{2,1,0:T(1,128)S(1)} all-to-all(f32[4,1,512]{2,1,0:T(1,128)S(1)} %broadcast_in_dim.95), channel_id=1, replica_groups=mesh['cls_0'=4,'cls_1'=8,'cls_2'=4,'rep'=2] {'cls_2'}, dimensions={0} | all-to-all | bytes 16384 | tf_op jit(solution)/shard_map/all_to_all | solution.py:20
  178.4 0.7 broadcast_in_dim.96
  179.1 4.8 %all-to-all-start.6 = ((f32[32,1,512]{2,1,0:T(1,128)}), f32[32,1,512]{2,1,0:T(1,128)S(1)}, u32[]{:S(2)}, u32[]{:S(2)}) async-start(f32[32,1,512]{2,1,0:T(1,128)} %broadcast_in_dim.96), calls=%async_computation.6 | async-start | bytes 131072 | tf_op jit(solution)/shard_map/all_to_all | solution.py:20
  183.9 0.3 slice_reduce_fusion.7
  184.2 0.3 slice_reduce_fusion.3
  184.6 8.6 %all-to-all-done.6 = f32[32,1,512]{2,1,0:T(1,128)S(1)} async-done(((f32[32,1,512]{2,1,0:T(1,128)}), f32[32,1,512]{2,1,0:T(1,128)S(1)}, u32[]{:S(2)}, u32[]{:S(2)}) %all-to-all-start.6) | async-done | bytes 65568 | tf_op jit(solution)/shard_map/all_to_all | solution.py:20
  193.3 11.4 %fusion.4 = f32[256,768]{1,0:T(8,128)S(1)} fusion(bf16[6144,768]{1,0:T(8,128)(2,1)} %maximum_dynamic-update-slice_fusion, s32[256]{0:T(256)S(1)} %get-tuple-element.10, s32[256]{0:T(256)S(1)} %get-tuple-element.8, s32[256]{0:T(256)S(1)} %get-tuple-element.9, f32[256]{0:T(256)S(1)} %get-tuple-element.24, s32[256]{0:T(256)S(1)} %get-tuple-element.7, ...), kind=kOutput, calls=%fused_computation.13 | convolution fusion | flops 2444230656 | bytes 16522240 | tf_op jit(solution)/shard_map/dot_general | solution.py:168
  204.6 0.5 reshape_reshape.7
  205.2 11.9 %all_to_all.50 = f32[4,32,2,768]{3,2,1,0:T(2,128)S(1)} all-to-all(f32[4,32,2,768]{3,2,1,0:T(2,128)S(1)} %bitcast.46), channel_id=1, replica_groups=mesh['cls_0'=4,'cls_1'=8,'cls_2'=4,'rep'=2] {'cls_2'}, dimensions={0} | all-to-all | bytes 1572864 | tf_op jit(solution)/shard_map/all_to_all | solution.py:74
  217.1 1.1 reduce_sum.78
  218.2 4.7 %all-to-all-start.8 = ((f32[32,2,768]{2,1,0:T(2,128)}), f32[32,2,768]{2,1,0:T(2,128)S(1)}, u32[]{:S(2)}, u32[]{:S(2)}) async-start(f32[32,2,768]{2,1,0:T(2,128)} %reduce_sum.78), calls=%async_computation.8 | async-start | bytes 393216 | tf_op jit(solution)/shard_map/all_to_all | solution.py:82
  222.8 0.6 dynamic-slice_bitcast_fusion
  223.4 10.0 %all-to-all-done.8 = f32[32,2,768]{2,1,0:T(2,128)S(1)} async-done(((f32[32,2,768]{2,1,0:T(2,128)}), f32[32,2,768]{2,1,0:T(2,128)S(1)}, u32[]{:S(2)}, u32[]{:S(2)}) %all-to-all-start.8) | async-done | bytes 196640 | tf_op jit(solution)/shard_map/all_to_all | solution.py:82
  233.4 0.7 reduce_sum.79
  (47 shorter events, 1.6 us)
Async XLA Ops:
  7.2 12.0 %copy-start = (bf16[768,768]{1,0:T(8,128)(2,1)S(1)}, bf16[768,768]{1,0:T(8,128)(2,1)}, u32[]{:S(2)}) copy-start(bf16[768,768]{1,0:T(8,128)(2,1)} %param.14) | copy-start | bytes 3538948
  7.2 8.1 %copy-start.4 = (s32[98304]{0:T(1024)S(1)}, s32[98304]{0:T(1024)}, u32[]{:S(2)}) copy-start(s32[98304]{0:T(1024)} %param.17) | copy-start | bytes 1179652
  7.2 12.0 %copy-start.2 = (bf16[384,768]{1,0:T(8,128)(2,1)S(1)}, bf16[384,768]{1,0:T(8,128)(2,1)}, u32[]{:S(2)}) copy-start(bf16[384,768]{1,0:T(8,128)(2,1)} %param.13) | copy-start | bytes 1769476
  7.2 12.7 %copy-start.5 = (f32[768]{0:T(1024)S(1)}, f32[768]{0:T(1024)}, u32[]{:S(2)}) copy-start(f32[768]{0:T(1024)} %param.15) | copy-start | bytes 9220
  19.9 43.2 %copy-start.6 = (bf16[1,2,768]{2,1,0:T(2,128)(2,1)S(1)}, bf16[1,2,768]{2,1,0:T(2,128)(2,1)}, u32[]{:S(2)}) copy-start(bf16[1,2,768]{2,1,0:T(2,128)(2,1)} %param.9) | copy-start | bytes 9220
  22.2 49.3 %copy-start.3 = (bf16[384,768]{1,0:T(8,128)(2,1)S(1)}, bf16[384,768]{1,0:T(8,128)(2,1)}, u32[]{:S(2)}) copy-start(bf16[384,768]{1,0:T(8,128)(2,1)} %param.16) | copy-start | bytes 1769476
  23.3 48.5 %copy-start.7 = (s32[2,256,4]{1,2,0:T(4,128)S(1)}, s32[2,256,4]{1,2,0:T(4,128)}, u32[]{:S(2)}) copy-start(s32[2,256,4]{1,2,0:T(4,128)} %param.10) | copy-start | bytes 24580
  23.3 39.8 %all-to-all-start = ((bf16[128,3,768]{2,1,0:T(4,128)(2,1)}), bf16[128,3,768]{2,1,0:T(4,128)(2,1)S(1)}, u32[]{:S(2)}, u32[]{:S(2)}) async-start(bf16[128,3,768]{2,1,0:T(4,128)(2,1)} %reshape.110), calls=%async_computation | async-start | bytes 1572864 | tf_op jit(solution)/shard_map/all_to_all | solution.py:115
  38.5 10.9 %sort.43.cloned.1.call-start = ((), (), s32[]{:S(2)}) async-start(), calls=%async_computation.9 | async-start | bytes 589856 | tf_op jit(solution)/shard_map/jit(sort)/sort | solution.py:121
  63.8 14.6 %all-to-all-start.1 = ((bf16[32,2,768]{2,1,0:T(2,128)(2,1)}), bf16[32,2,768]{2,1,0:T(2,128)(2,1)}, u32[]{:S(2)}, u32[]{:S(2)}) async-start(bf16[32,2,768]{2,1,0:T(2,128)(2,1)} %broadcast_in_dim.89), calls=%async_computation.1 | async-start | bytes 196608 | tf_op jit(solution)/shard_map/all_to_all | solution.py:20
  71.7 31.0 %copy-start.1 = (bf16[384,768]{1,0:T(8,128)(2,1)}, bf16[384,768]{1,0:T(8,128)(2,1)S(1)}, u32[]{:S(2)}) copy-start(bf16[384,768]{1,0:T(8,128)(2,1)S(1)} %add_convert_fusion) | copy-start | bytes 1769476
  71.8 19.7 %collective-permute-start = (bf16[384,768]{1,0:T(8,128)(2,1)S(1)}, bf16[384,768]{1,0:T(8,128)(2,1)}, u32[]{:S(2)}, u32[]{:S(2)}) collective-permute-start(bf16[384,768]{1,0:T(8,128)(2,1)S(1)} %add_convert_fusion), channel_id=1, source_target_pairs={{0,1},{1,0},{2,3},{3,2},{4,5},{5,4},{6,7},{7,6},{8,9},{9,8},{10,11... | collective-permute-start | bytes 1769480 | tf_op jit(solution)/shard_map/ppermute | solution.py:15
  80.2 10.8 %all-to-all-start.2 = ((bf16[4,32,2,768]{3,2,1,0:T(2,128)(2,1)}), bf16[4,32,2,768]{3,2,1,0:T(2,128)(2,1)S(1)}, u32[]{:S(2)}, u32[]{:S(2)}) async-start(bf16[4,32,2,768]{3,2,1,0:T(2,128)(2,1)} %broadcast_in_dim.90), calls=%async_computation.2 | async-start | bytes 786432 | tf_op jit(solution)/shard_map/all_to_all | solution.py:20
  103.4 39.0 %all-to-all-start.3 = ((f32[4,1,256]{2,1,0:T(1,128)}), f32[4,1,256]{2,1,0:T(1,128)S(1)}, u32[]{:S(2)}, u32[]{:S(2)}) async-start(f32[4,1,256]{2,1,0:T(1,128)} %broadcast_in_dim.91), calls=%async_computation.3 | async-start | bytes 8192 | tf_op jit(solution)/shard_map/all_to_all | solution.py:20
  143.0 24.9 %all-to-all-start.4 = ((f32[32,1,256]{2,1,0:T(1,128)}), f32[32,1,256]{2,1,0:T(1,128)S(1)}, u32[]{:S(2)}, u32[]{:S(2)}) async-start(f32[32,1,256]{2,1,0:T(1,128)} %broadcast_in_dim.92), calls=%async_computation.4 | async-start | bytes 65536 | tf_op jit(solution)/shard_map/all_to_all | solution.py:20
  179.1 14.1 %all-to-all-start.6 = ((f32[32,1,512]{2,1,0:T(1,128)}), f32[32,1,512]{2,1,0:T(1,128)S(1)}, u32[]{:S(2)}, u32[]{:S(2)}) async-start(f32[32,1,512]{2,1,0:T(1,128)} %broadcast_in_dim.96), calls=%async_computation.6 | async-start | bytes 131072 | tf_op jit(solution)/shard_map/all_to_all | solution.py:20
  218.2 15.3 %all-to-all-start.8 = ((f32[32,2,768]{2,1,0:T(2,128)}), f32[32,2,768]{2,1,0:T(2,128)S(1)}, u32[]{:S(2)}, u32[]{:S(2)}) async-start(f32[32,2,768]{2,1,0:T(2,128)} %reduce_sum.78), calls=%async_computation.8 | async-start | bytes 393216 | tf_op jit(solution)/shard_map/all_to_all | solution.py:82
Sparse Core Ops, SparseCore 0:
  42.2 6.8 sort.45.cloned.1.call-done
  (1 shorter events, 0.0 us)
where the time goes:
time: 243 us; the launch traced here: 241 us
  local copies, waits for them, and re-layouts  64.1 us (26%)
  starting transfers between devices  52.7 us (22%)
  waiting for transfers between devices  48.7 us (20%)
  blocking collectives  22.3 us (9%)
  matrix products  21.1 us (9%)
  other arithmetic  17 us (7%)
  between operations  15.1 us (6%)
    all_to_all x5, starting transfers between devices, copy_for_each(): lax.all_to_all(jnp.broadcast_to(shard[None], (length, *shard.shape)), axi...  32.8 us
    gather x3, local copies, waits for them, and re-layouts, per_device(): jnp.take_along_axis(logits, jnp.clip(label_offsets, 0, usable_count - 1),...  32.2 us
    all_to_all x5, waiting for transfers between devices, copy_for_each(): lax.all_to_all(jnp.broadcast_to(shard[None], (length, *shard.shape)), axi...  29.8 us
    all_to_all x1, starting transfers between devices, per_device(): lax.all_to_all(sending, CLS, split_axis=0, concat_axis=0, tiled=True)  15.1 us
    all_to_all x1, blocking collectives, sum_at_owner(): lax.all_to_all(pieces, axis, split_axis=0, concat_axis=0, tiled=True)  11.9 us
    dot_general x1, matrix products, per_device(): jnp.dot(coefficients, current, preferred_element_type=jnp.float32)  11.4 us
    all_to_all x1, blocking collectives, copy_for_each(): lax.all_to_all(jnp.broadcast_to(shard[None], (length, *shard.shape)), axi...  10.4 us
    all_to_all x1, waiting for transfers between devices, sum_in_two_steps(): lax.all_to_all(nearer, far, split_axis=0, concat_axis=0, tiled=True)  10 us
  transfers between devices with their start and end apart: 8, of which 6 were waited for; matrix products, arithmetic and copies ran while one was open for 20% of the time, Pallas kernels for 0%

commit v1 on v0

v1 whole, which is shorter than its diff:
```python
import functools

import jax
import jax.numpy as jnp
from jax import lax
from jax.experimental import pallas as pl
from jax.experimental.pallas import tpu as pltpu
from jax.sharding import Mesh
from jax.sharding import PartitionSpec as P

SLOTS = 8
D = 768
HALF = 384
QG = 256
N_CLS = 128
PER = 3
CLS = ("cls_0", "cls_1", "cls_2")
CLS_REP = ("cls_0", "cls_1", "cls_2", "rep")
SEND = PER * HALF + D
BACK = 2 * D + 128
F32 = jnp.float32
BF16 = jnp.bfloat16
VMEM = pltpu.VMEM
SMEM = pltpu.SMEM


def vmem_spec():
    return pl.BlockSpec(memory_space=VMEM)


def smem_spec():
    return pl.BlockSpec(memory_space=SMEM)


def iota(shape, dim):
    return lax.broadcasted_iota(jnp.int32, shape, dim)


def dot(a, b):
    return jnp.dot(a, b, preferred_element_type=F32)


def dot_last(a, b):
    return lax.dot_general(a, b, (((1,), (1,)), ((), ())), preferred_element_type=F32)


def dot_first(a, b):
    return lax.dot_general(a, b, (((0,), (0,)), ((), ())), preferred_element_type=F32)


def encode_kernel(idx_ref, feat_ref, weight_ref, gain_ref, tgt_ref, q_ref, out_ref):
    block = idx_ref[0]
    hidden = dot(feat_ref[...], weight_ref[...])
    mean = jnp.mean(hidden * hidden, axis=1, keepdims=True)
    encoded = (hidden * lax.rsqrt(mean + 1e-06) * gain_ref[...]).astype(BF16)
    rows = [tgt_ref[pl.ds(3 * block + a, 1), :].astype(F32) for a in range(3)]
    columns = [jnp.broadcast_to(row, (128, 128)).T for row in rows]
    ranks = []
    for row in rows:
        rank = jnp.zeros((1, 128), F32)
        for column in columns:
            rank += jnp.sum(jnp.where(column < row, 1.0, 0.0), axis=0, keepdims=True)
        ranks.append(rank)
    rank = jnp.concatenate(ranks, axis=1)
    line = iota((QG, HALF), 0)
    first = ((line >> 1) * PER).astype(F32)
    odd = (line & 1) == 1
    for k in range(PER):
        hit = rank == first + float(k)
        total = dot(jnp.where(hit & ~odd, 1.0, 0.0).astype(BF16), encoded[:, :HALF])
        total += dot(jnp.where(hit & odd, 1.0, 0.0).astype(BF16), encoded[:, HALF:])
        out_ref[:, k * HALF : (k + 1) * HALF] = total.astype(BF16)
    own = q_ref[...].astype(F32)
    wide_odd = (iota((QG, D), 0) & 1) == 1
    out_ref[:, PER * HALF :] = jnp.where(wide_odd, own[1:2], own[0:1]).astype(BF16)


def place_kernel(idx_ref, tgt_ref, out_ref):
    base = idx_ref[1] * (2 * HALF) + idx_ref[2] * HALF
    parts = [tgt_ref[pl.ds(3 * idx_ref[2] + a, N_CLS, stride=6), :] for a in range(3)]
    offsets = jnp.concatenate(parts, axis=1) - base
    inside = (offsets >= 0) & (offsets < HALF)
    far = 4096.0
    keys = jnp.where(inside, offsets.astype(F32), far)
    lane = iota((N_CLS, HALF), 1).astype(F32)
    source = iota((N_CLS, QG), 0)
    line = iota((N_CLS, QG), 1)
    spread = [
        jnp.where((line >> 1 == source) & ((line & 1) == h), 1.0, 0.0).astype(BF16)
        for h in range(2)
    ]
    for k in range(PER):
        least = jnp.min(keys, axis=1, keepdims=True)
        keys = jnp.where(keys == least, far, keys)
        chosen = jnp.where(lane == least, 1.0, 0.0).astype(BF16)
        for h in range(2):
            out_ref[2 * k + h] = dot_first(chosen, spread[h]).astype(BF16)


def refresh_kernel(place_ref, got_ref, free_ref, out_ref):
    for h in range(2):
        cols = slice(h * HALF, (h + 1) * HALF)
        placed = dot(place_ref[h], got_ref[:, :HALF])
        for k in range(1, PER):
            placed += dot(place_ref[2 * k + h], got_ref[:, k * HALF : (k + 1) * HALF])
        out_ref[:, cols] = (free_ref[:, cols].astype(F32) + placed).astype(BF16)


def count_hits(ids_ref, first, width):
    label = first + iota((QG, width), 1)
    hits = jnp.zeros((QG, width), F32)
    for k in range(4):
        hits += jnp.where(ids_ref[:, k : k + 1] == label, 1.0, 0.0)
    return hits.astype(BF16)


def positive_kernel(idx_ref, ids_ref, lab_ref, out_ref):
    step = pl.program_id(0)

    @pl.when(step == 0)
    def _():
        out_ref[...] = jnp.zeros_like(out_ref)

    slot = step + (step >= idx_ref[3]).astype(jnp.int32)
    first = idx_ref[1] * (SLOTS * D) + slot * D
    out_ref[...] += dot(count_hits(ids_ref, first, D), lab_ref[...])


def absorb(logits, vectors, m_prev, s_prev, acc_prev):
    m_new = m_prev
    for part in logits:
        m_new = jnp.maximum(m_new, jnp.max(part, axis=1, keepdims=True))
    scale = jnp.exp(m_prev - m_new)
    s_new = s_prev * scale
    acc_new = acc_prev * scale
    for part, rows in zip(logits, vectors):
        weight = jnp.exp(part - m_new)
        s_new += jnp.sum(weight, axis=1, keepdims=True)
        acc_new += dot(weight.astype(BF16), rows)
    return m_new, s_new, acc_new


def old_kernel(idx_ref, got_ref, lab_ref, m_ref, s_ref, acc_ref):
    step = pl.program_id(0)

    @pl.when(step == 0)
    def _():
        m_ref[...] = jnp.full_like(m_ref, -jnp.inf)
        s_ref[...] = jnp.zeros_like(s_ref)
        acc_ref[...] = jnp.zeros_like(acc_ref)

    logits = dot_last(got_ref[:, PER * HALF :], lab_ref[...])
    m_new, s_new, acc_new = absorb(
        [logits], [lab_ref[...]], m_ref[:, :1], s_ref[:, :1], acc_ref[...]
    )
    m_ref[...] = jnp.broadcast_to(m_new, m_ref.shape)
    s_ref[...] = jnp.broadcast_to(s_new, s_ref.shape)
    acc_ref[...] = acc_new


def three_parts(value):
    high = value.astype(BF16).astype(F32)
    rest = value - high
    middle = rest.astype(BF16).astype(F32)
    return [high, middle, rest - middle]


def fresh_kernel(idx_ref, ids_ref, got_ref, own_ref, other_ref, pos_ref, m_ref, s_ref, acc_ref, out_ref):
    queries = got_ref[:, PER * HALF :]
    vectors = [own_ref[...], other_ref[...]]
    logits = [dot_last(queries, rows) for rows in vectors]
    m_new, s_new, acc_new = absorb(logits, vectors, m_ref[:, :1], s_ref[:, :1], acc_ref[...])
    rep = idx_ref[2]
    first = idx_ref[1] * (SLOTS * D) + idx_ref[3] * D
    positive = pos_ref[...]
    for rows, half in zip(vectors, (rep, 1 - rep)):
        positive += dot(count_hits(ids_ref, first + half * HALF, HALF), rows)
    picked = jnp.sum(queries.astype(F32) * positive, axis=1, keepdims=True)
    lane = iota((QG, 128), 1)
    stats = jnp.zeros((QG, 128), F32)
    for at, part in enumerate(three_parts(m_new) + three_parts(s_new) + three_parts(picked)):
        stats = jnp.where(lane == at, part, stats)
    out_ref[:, :D] = acc_new.astype(BF16)
    out_ref[:, D : 2 * D] = positive.astype(BF16)
    out_ref[:, 2 * D :] = stats.astype(BF16)


def finish_kernel(inv_ref, back_ref, loss_ref, grad_ref):
    stats = back_ref[:, 2 * D :].astype(F32)

    def column(at):
        return stats[:, at : at + 1] + stats[:, at + 1 : at + 2] + stats[:, at + 2 : at + 3]

    peak, total, picked = column(0), column(3), column(6)
    odd = (iota((QG, 1), 0) & 1) == 1
    for h in range(2):
        mine = odd if h else ~odd
        top = jnp.max(jnp.where(mine, peak, -jnp.inf), axis=0, keepdims=True)
        weight = jnp.where(mine, jnp.exp(peak - top), 0.0)
        exp_total = jnp.sum(weight * total, axis=0, keepdims=True)
        inverse = inv_ref[h]
        chosen = jnp.sum(jnp.where(mine, picked, 0.0), axis=0, keepdims=True)
        loss = top + jnp.log(exp_total) - chosen * inverse
        loss_ref[h : h + 1, :] = jnp.broadcast_to(loss, (1, 128))
        scaled = back_ref[:, :D].astype(F32) * (weight / exp_total)
        scaled -= jnp.where(mine, back_ref[:, D : 2 * D].astype(F32), 0.0) * inverse
        grad_ref[h : h + 1, :] = jnp.sum(scaled, axis=0, keepdims=True)


def per_device(
    queries,
    positives,
    label_vectors,
    refresh_slot,
    features,
    encoder_weight,
    encoder_gain,
    free_vectors,
    targets,
):
    cls_index = lax.axis_index(CLS)
    rep_index = lax.axis_index("rep")
    idx = jnp.stack([cls_index * 2 + rep_index, cls_index, rep_index, refresh_slot]).astype(jnp.int32)
    target_rows = targets.reshape(768, 128)
    ids = lax.dynamic_index_in_dim(positives, rep_index, 0, keepdims=False)
    own_ids = lax.dynamic_slice_in_dim(ids, cls_index * 2, 2)
    inverse = 1.0 / jnp.sum((own_ids >= 0).astype(F32), axis=1)

    sending = pl.pallas_call(
        encode_kernel,
        out_shape=jax.ShapeDtypeStruct((QG, SEND), BF16),
        in_specs=[smem_spec()] + [vmem_spec()] * 5,
        out_specs=vmem_spec(),
        name="encode",
    )(idx, features, encoder_weight, encoder_gain.reshape(1, D), target_rows, queries.reshape(2, D))
    got = lax.all_to_all(sending.reshape(N_CLS, 2, SEND), CLS, 0, 0, tiled=True)
    got = got.reshape(QG, SEND)

    place = pl.pallas_call(
        place_kernel,
        out_shape=jax.ShapeDtypeStruct((2 * PER, HALF, QG), BF16),
        in_specs=[smem_spec(), vmem_spec()],
        out_specs=vmem_spec(),
        name="place",
    )(idx, target_rows)

    def slot_block(step, idx_ref):
        return (step + (step >= idx_ref[3]).astype(jnp.int32), 0)

    def whole(step, idx_ref):
        return (0, 0)

    slot_spec = pl.BlockSpec((D, D), slot_block)
    positive_old = pl.pallas_call(
        positive_kernel,
        out_shape=jax.ShapeDtypeStruct((QG, D), F32),
        grid_spec=pltpu.PrefetchScalarGridSpec(
            num_scalar_prefetch=1,
            grid=(SLOTS - 1,),
            in_specs=[pl.BlockSpec((QG, 4), whole), slot_spec],
            out_specs=pl.BlockSpec((QG, D), whole),
        ),
        name="positive",
    )(idx, ids, label_vectors)

    refreshed = pl.pallas_call(
        refresh_kernel,
        out_shape=jax.ShapeDtypeStruct((HALF, D), BF16),
        in_specs=[vmem_spec()] * 3,
        out_specs=vmem_spec(),
        name="refresh",
    )(place, got, free_vectors)
    partner = lax.ppermute(refreshed, "rep", [(0, 1), (1, 0)])

    state = pl.pallas_call(
        old_kernel,
        out_shape=[
            jax.ShapeDtypeStruct((QG, 128), F32),
            jax.ShapeDtypeStruct((QG, 128), F32),
            jax.ShapeDtypeStruct((QG, D), F32),
        ],
        grid_spec=pltpu.PrefetchScalarGridSpec(
            num_scalar_prefetch=1,
            grid=(SLOTS - 1,),
            in_specs=[pl.BlockSpec((QG, SEND), whole), slot_spec],
            out_specs=[
                pl.BlockSpec((QG, 128), whole),
                pl.BlockSpec((QG, 128), whole),
                pl.BlockSpec((QG, D), whole),
            ],
        ),
        name="old",
    )(idx, got, label_vectors)

    leaving = pl.pallas_call(
        fresh_kernel,
        out_shape=jax.ShapeDtypeStruct((QG, BACK), BF16),
        in_specs=[smem_spec()] + [vmem_spec()] * 8,
        out_specs=vmem_spec(),
        name="fresh",
    )(idx, ids, got, refreshed, partner, positive_old, *state)
    back = lax.all_to_all(leaving.reshape(N_CLS, 2, BACK), CLS, 0, 0, tiled=True)
    loss, grads = pl.pallas_call(
        finish_kernel,
        out_shape=[jax.ShapeDtypeStruct((2, 128), F32), jax.ShapeDtypeStruct((2, D), F32)],
        in_specs=[smem_spec(), vmem_spec()],
        out_specs=[vmem_spec()] * 2,
        name="finish",
    )(inverse, back.reshape(QG, BACK))
    return (
        loss[:, 0].reshape(1, 2),
        grads.astype(BF16).reshape(1, 2, D),
        refreshed,
    )


def solution(mesh):
    torus = Mesh(
        mesh.devices.reshape(4, 8, 4, mesh.shape["rep"]), ("cls_0", "cls_1", "cls_2", "rep")
    )
    placed = (
        P("rep", CLS, None),
        P(),
        P(CLS, None),
        P(),
        P(CLS_REP, None),
        P(),
        P(),
        P(CLS_REP, None),
        P(),
    )
    return jax.shard_map(
        per_device,
        mesh=torus,
        in_specs=placed,
        out_specs=(P("rep", CLS), P("rep", CLS, None), P(CLS_REP, None)),
        check_vma=False,
    )
```

time: 243 us -> 132 us (0.54)
  local copies, waits for them, and re-layouts: 64.1 us -> 12.9 us
  Pallas kernels: 0 us -> 40.5 us
  starting transfers between devices: 52.7 us -> 22.2 us
  blocking collectives: 22.3 us -> 0 us
  matrix products: 21.1 us -> 0 us
  other arithmetic: 17 us -> 2.5 us
  between operations: 15.1 us -> 1.33 us
  waiting for transfers between devices: 48.7 us -> 52.2 us
    pallas_call x0 -> x7, Pallas kernels: none -> 40.5 us  [the longest x1 12.9 us: per_device(): pl.pallas_call(old_kernel, out_shape=[jax.ShapeDtypeStruct((QG, 128), F32...]
    gather x5 -> x0, local copies, waits for them, and re-layouts: 36.5 us -> none  [the longest x3 32.2 us: per_device(): jnp.take_along_axis(logits, jnp.clip(label_offsets, 0, usable_count - 1),...]
    all_to_all x7 -> x2, starting transfers between devices: 52.6 us -> 22.2 us  [the longest x1 15 us: per_device(): got = lax.all_to_all(sending.reshape(N_CLS, 2, SEND), CLS, 0, 0, tiled=True)]
    all_to_all x2 -> x0, blocking collectives: 22.3 us -> none  [the longest x1 11.9 us: sum_at_owner(): lax.all_to_all(pieces, axis, split_axis=0, concat_axis=0, tiled=True)]
    dot_general x3 -> x0, matrix products: 21.1 us -> none  [the longest x1 11.4 us: per_device(): jnp.dot(coefficients, current, preferred_element_type=jnp.float32)]
    sort x2 -> x0, local copies, waits for them, and re-layouts: 9.75 us -> none  [per_device(): jnp.sort(jnp.where(kept_rows, row_offsets, half_rows), axis=1)]
    sort x2 -> x0, other arithmetic: 7.54 us -> none  [the longest x1 3.77 us: per_device(): jnp.argsort(own_targets)]
    unnamed x19 -> x4, local copies, waits for them, and re-layouts: 8.25 us -> 0.83 us
  transfers between devices with their start and end apart: 8 -> 3, of which waited for: 6 -> 2; matrix products, arithmetic and copies ran while one was open for 20% -> 1% of each run, Pallas kernels for 0% -> 19%
where the time goes in v1:
time: 132 us
  waiting for transfers between devices  52.2 us (40%)
  Pallas kernels  40.5 us (31%)
  starting transfers between devices  22.2 us (17%)
  local copies, waits for them, and re-layouts  12.9 us (10%)
  other arithmetic  2.5 us (2%)
  between operations  1.33 us (1%)
    all_to_all x1, waiting for transfers between devices, per_device(): lax.all_to_all(leaving.reshape(N_CLS, 2, BACK), CLS, 0, 0, tiled=True)  26.1 us
    all_to_all x1, waiting for transfers between devices, per_device(): got = lax.all_to_all(sending.reshape(N_CLS, 2, SEND), CLS, 0, 0, tiled=True)  26.1 us
    all_to_all x1, starting transfers between devices, per_device(): got = lax.all_to_all(sending.reshape(N_CLS, 2, SEND), CLS, 0, 0, tiled=True)  15 us
    pallas_call x1, Pallas kernels, per_device(): pl.pallas_call(old_kernel, out_shape=[jax.ShapeDtypeStruct((QG, 128), F32...  12.9 us
    pallas_call x1, Pallas kernels, per_device(): pl.pallas_call(positive_kernel, out_shape=jax.ShapeDtypeStruct((QG, D), F...  9.66 us
    all_to_all x1, starting transfers between devices, per_device(): lax.all_to_all(leaving.reshape(N_CLS, 2, BACK), CLS, 0, 0, tiled=True)  7.2 us
    pallas_call x1, Pallas kernels, per_device(): pl.pallas_call(fresh_kernel, out_shape=jax.ShapeDtypeStruct((QG, BACK), B...  5.01 us
    pallas_call x1, Pallas kernels, per_device(): pl.pallas_call(encode_kernel, out_shape=jax.ShapeDtypeStruct((QG, SEND),...  4.5 us
  transfers between devices with their start and end apart: 3, of which 2 were waited for; matrix products, arithmetic and copies ran while one was open for 1% of the time, Pallas kernels for 19%

profile of v1, /device:TPU:32, one launch (start us, length us, event | category | flops | bytes accessed | tf_op | source)
XLA Modules:
  0.0 131.6 jit_solution(969978605163974439)
XLA Ops:
  1.3 1.3 reshape.34.gain_ref
  2.6 0.6 pad_add_fusion.idx_ref
  3.2 4.5 %encode.1 = bf16[256,1920]{1,0:T(8,128)(2,1)} custom-call(s32[4]{0:T(128)} %pad_add_fusion.idx_ref, bf16[384,768]{1,0:T(8,128)(2,1)} %feat_ref.1, bf16[768,768]{1,0:T(8,128)(2,1)} %weight_ref.1, f32[1,768]{1,0:T(1,128)} %reshape.34.gain_ref, s32[768,128]{1,0:T(8,128)} %bitcast.11, bf16[2,768]{1,0:T(2,128)(2,1)} %bitcast.15), custom_call_target="tpu_custom_call" | custom-call | tf_op jit(solution)/shard_map/encode/pallas_call | solution.py:229
  7.7 3.2 %reshape.37 = bf16[128,2,1920]{2,1,0:T(2,128)(2,1)} reshape(bf16[256,1920]{1,0:T(8,128)(2,1)} %encode.1) | data formatting | bytes 1966080 | tf_op jit(solution)/shard_map/reshape | solution.py:236
  10.8 15.0 %all-to-all-start = ((bf16[128,2,1920]{2,1,0:T(2,128)(2,1)}), bf16[128,2,1920]{2,1,0:T(2,128)(2,1)S(1)}, u32[]{:S(2)}, u32[]{:S(2)}) async-start(bf16[128,2,1920]{2,1,0:T(2,128)(2,1)} %reshape.37), calls=%async_computation | async-start | bytes 1966080 | tf_op jit(solution)/shard_map/all_to_all | solution.py:236
  25.9 2.7 %place.1.place_ref = bf16[6,384,256]{2,1,0:T(8,128)(2,1)} custom-call(s32[4]{0:T(128)} %pad_add_fusion.idx_ref, s32[768,128]{1,0:T(8,128)} %bitcast.12), custom_call_target="tpu_custom_call" | custom-call | tf_op jit(solution)/shard_map/place/pallas_call | solution.py:239
  28.6 26.1 %all-to-all-done = bf16[128,2,1920]{2,1,0:T(2,128)(2,1)S(1)} async-done(((bf16[128,2,1920]{2,1,0:T(2,128)(2,1)}), bf16[128,2,1920]{2,1,0:T(2,128)(2,1)S(1)}, u32[]{:S(2)}, u32[]{:S(2)}) %all-to-all-start) | async-done | bytes 983072 | tf_op jit(solution)/shard_map/all_to_all | solution.py:236
  54.6 1.3 %reshape.38.got_ref = bf16[256,1920]{1,0:T(8,128)(2,1)} reshape(bf16[128,2,1920]{2,1,0:T(2,128)(2,1)S(1)} %all-to-all-done) | data formatting | bytes 1966080 | tf_op jit(solution)/shard_map/reshape | solution.py:237
  56.0 0.0 copy-start.1
  56.0 3.3 %refresh.1.own_ref = bf16[384,768]{1,0:T(8,128)(2,1)} custom-call(bf16[6,384,256]{2,1,0:T(8,128)(2,1)} %place.1.place_ref, bf16[256,1920]{1,0:T(8,128)(2,1)} %reshape.38.got_ref, bf16[384,768]{1,0:T(8,128)(2,1)} %free_ref.1), custom_call_target="tpu_custom_call" | custom-call | tf_op jit(solution)/shard_map/refresh/pallas_call | solution.py:266
  59.3 0.0 collective-permute-start
  59.3 0.0 copy-done.1
  59.3 0.8 copy.13
  60.1 9.7 %positive.1.pos_ref = f32[256,768]{1,0:T(8,128)} custom-call(s32[4]{0:T(128)} %pad_add_fusion.idx_ref, s32[256,4]{1,0:T(8,128)} %bitcast.13, bf16[6144,768]{1,0:T(8,128)(2,1)} %lab_ref.3), custom_call_target="tpu_custom_call" | custom-call | tf_op jit(solution)/shard_map/positive/pallas_call | solution.py:254
  69.8 12.9 %old.1 = (f32[256,128]{1,0:T(8,128)}, f32[256,128]{1,0:T(8,128)}, f32[256,768]{1,0:T(8,128)}) custom-call(s32[4]{0:T(128)} %pad_add_fusion.idx_ref, bf16[256,1920]{1,0:T(8,128)(2,1)} %reshape.38.got_ref, bf16[6144,768]{1,0:T(8,128)(2,1)} %lab_ref.3), custom_call_target="tpu_custom_call" | custom-call | tf_op jit(solution)/shard_map/old/pallas_call | solution.py:275
  82.7 0.0 collective-permute-done.other_ref
  82.7 0.0 copy-start
  82.7 0.8 copy-done
  83.5 5.0 %fresh.1 = bf16[256,1664]{1,0:T(8,128)(2,1)} custom-call(s32[4]{0:T(128)} %pad_add_fusion.idx_ref, s32[256,4]{1,0:T(8,128)} %bitcast.14, bf16[256,1920]{1,0:T(8,128)(2,1)} %reshape.38.got_ref, bf16[384,768]{1,0:T(8,128)(2,1)} %refresh.1.own_ref, bf16[384,768]{1,0:T(8,128)(2,1)} %copy-done, f32[256,768]{1,0:T(8,128)} %positive.1.pos_ref, ...), custom_call_target="tpu_custom_call" | custom-call | tf_op jit(solution)/shard_map/fresh/pallas_call | solution.py:295
  88.5 3.0 %reshape.39 = bf16[128,2,1664]{2,1,0:T(2,128)(2,1)} reshape(bf16[256,1664]{1,0:T(8,128)(2,1)} %fresh.1) | data formatting | bytes 1703936 | tf_op jit(solution)/shard_map/reshape | solution.py:302
  91.5 7.2 %all-to-all-start.1 = ((bf16[128,2,1664]{2,1,0:T(2,128)(2,1)}), bf16[128,2,1664]{2,1,0:T(2,128)(2,1)S(1)}, u32[]{:S(2)}, u32[]{:S(2)}) async-start(bf16[128,2,1664]{2,1,0:T(2,128)(2,1)} %reshape.39), calls=%async_computation.1 | async-start | bytes 1703936 | tf_op jit(solution)/shard_map/all_to_all | solution.py:302
  98.7 0.1 convert_reduce_fusion
  98.8 0.5 broadcast_divide_fusion.inv_ref
  99.3 26.1 %all-to-all-done.1 = bf16[128,2,1664]{2,1,0:T(2,128)(2,1)S(1)} async-done(((bf16[128,2,1664]{2,1,0:T(2,128)(2,1)}), bf16[128,2,1664]{2,1,0:T(2,128)(2,1)S(1)}, u32[]{:S(2)}, u32[]{:S(2)}) %all-to-all-start.1) | async-done | bytes 852000 | tf_op jit(solution)/shard_map/all_to_all | solution.py:302
  125.4 1.2 reshape.40.back_ref
  126.6 2.4 %finish.1 = (f32[2,128]{1,0:T(2,128)}, f32[2,768]{1,0:T(2,128)}) custom-call(f32[2]{0:T(128)} %broadcast_divide_fusion.inv_ref, bf16[256,1664]{1,0:T(8,128)(2,1)} %reshape.40.back_ref), custom_call_target="tpu_custom_call" | custom-call | tf_op jit(solution)/shard_map/finish/pallas_call | solution.py:303
  129.0 1.3 slice_reduce_fusion
  130.3 1.3 convert_bitcast_fusion
  (1 shorter events, 0.0 us)
Async XLA Ops:
  10.8 43.8 %all-to-all-start = ((bf16[128,2,1920]{2,1,0:T(2,128)(2,1)}), bf16[128,2,1920]{2,1,0:T(2,128)(2,1)S(1)}, u32[]{:S(2)}, u32[]{:S(2)}) async-start(bf16[128,2,1920]{2,1,0:T(2,128)(2,1)} %reshape.37), calls=%async_computation | async-start | bytes 1966080 | tf_op jit(solution)/shard_map/all_to_all | solution.py:236
  56.0 3.3 %copy-start.1 = (s32[2,256,4]{1,2,0:T(4,128)S(1)}, s32[2,256,4]{1,2,0:T(4,128)}, u32[]{:S(2)}) copy-start(s32[2,256,4]{1,2,0:T(4,128)} %param.10) | copy-start | bytes 24580
  59.3 23.4 %collective-permute-start = (bf16[384,768]{1,0:T(8,128)(2,1)}, bf16[384,768]{1,0:T(8,128)(2,1)S(1)}, u32[]{:S(2)}, u32[]{:S(2)}) collective-permute-start(bf16[384,768]{1,0:T(8,128)(2,1)} %refresh.1.own_ref), channel_id=1, source_target_pairs={{0,1},{1,0},{2,3},{3,2},{4,5},{5,4},{6,7},{7,6},{8,9},{9,8},{10,11... | collective-permute-start | bytes 1769480 | tf_op jit(solution)/shard_map/ppermute | solution.py:273
  82.7 0.8 copy-start
  91.5 33.9 %all-to-all-start.1 = ((bf16[128,2,1664]{2,1,0:T(2,128)(2,1)}), bf16[128,2,1664]{2,1,0:T(2,128)(2,1)S(1)}, u32[]{:S(2)}, u32[]{:S(2)}) async-start(bf16[128,2,1664]{2,1,0:T(2,128)(2,1)} %reshape.39), calls=%async_computation.1 | async-start | bytes 1703936 | tf_op jit(solution)/shard_map/all_to_all | solution.py:302

commit v2 on v1

v2 whole, which is shorter than its diff:
```python
import jax
import jax.numpy as jnp
from jax import lax
from jax.experimental import pallas as pl
from jax.experimental.pallas import tpu as pltpu
from jax.sharding import Mesh
from jax.sharding import PartitionSpec as P

SLOTS = 8
OLD = SLOTS - 1
D = 768
HALF = 384
QG = 256
N_CLS = 128
PER = 3
CLS = ("cls_0", "cls_1", "cls_2")
CLS_REP = ("cls_0", "cls_1", "cls_2", "rep")
ROWS = PER * HALF
SEND = ROWS + D
BACK = 2 * D + 128
F32 = jnp.float32
BF16 = jnp.bfloat16


def vmem_spec():
    return pl.BlockSpec(memory_space=pltpu.VMEM)


def smem_spec():
    return pl.BlockSpec(memory_space=pltpu.SMEM)


def iota(shape, dim):
    return lax.broadcasted_iota(jnp.int32, shape, dim)


def dot(a, b):
    return jnp.dot(a, b, preferred_element_type=F32)


def dot_last(a, b):
    return lax.dot_general(a, b, (((1,), (1,)), ((), ())), preferred_element_type=F32)


def dot_first(a, b):
    return lax.dot_general(a, b, (((0,), (0,)), ((), ())), preferred_element_type=F32)


def one_hot(mask):
    return jnp.where(mask, 1.0, 0.0).astype(BF16)


def spread_down(row):
    return jnp.broadcast_to(row, (128, 128)).T


def encode_kernel(feat_ref, weight_ref, gain_ref, tgt_ref, q_ref, out_ref):
    block = lax.axis_index(CLS_REP)
    hidden = dot(feat_ref[...], weight_ref[...])
    mean = jnp.mean(hidden * hidden, axis=1, keepdims=True)
    gain = jnp.concatenate([gain_ref[i : i + 1, :] for i in range(6)], axis=1)
    encoded = (hidden * lax.rsqrt(mean + 1e-06) * gain).astype(BF16)
    rows = [tgt_ref[pl.ds(3 * block + a, 1), :].astype(F32) for a in range(3)]
    columns = [spread_down(row) for row in rows]
    ranks = []
    for row in rows:
        rank = jnp.zeros((1, 128), F32)
        for column in columns:
            rank += jnp.sum(jnp.where(column < row, 1.0, 0.0), axis=0, keepdims=True)
        ranks.append(rank)
    rank = jnp.concatenate(ranks, axis=1)
    line = iota((QG, HALF), 0)
    first = ((line >> 1) * PER).astype(F32)
    odd = (line & 1) == 1
    for k in range(PER):
        hit = rank == first + float(k)
        total = dot(one_hot(hit & ~odd), encoded[:, :HALF])
        total += dot(one_hot(hit & odd), encoded[:, HALF:])
        out_ref[..., k * HALF : (k + 1) * HALF] = total.astype(BF16).reshape(N_CLS, 2, HALF)
    out_ref[..., ROWS:] = jnp.broadcast_to(q_ref[...], (N_CLS, 2, D))


def place_kernel(tgt_ref, ids_ref, key_ref, plane_ref, flag_ref):
    cls_index, rep_index = lax.axis_index(CLS), lax.axis_index("rep")
    base = cls_index * (2 * HALF) + rep_index * HALF
    parts = [tgt_ref[pl.ds(3 * rep_index + a, N_CLS, stride=6), :] for a in range(3)]
    offsets = jnp.concatenate(parts, axis=1) - base
    inside = (offsets >= 0) & (offsets < HALF)
    far = 4096.0
    keys = jnp.where(inside, offsets.astype(F32), far)
    source = iota((N_CLS, QG), 0)
    twice = (iota((N_CLS, QG), 1) >> 1) == source
    for k in range(PER):
        least = jnp.min(keys, axis=1, keepdims=True)
        keys = jnp.where(keys == least, far, keys)
        wide = jnp.broadcast_to(least, (N_CLS, QG))
        key_ref[k : k + 1, :] = jnp.sum(jnp.where(twice, wide, 0.0), axis=0, keepdims=True)
    first = cls_index * (SLOTS * D)
    lane = iota((QG, 128), 1)
    seen = jnp.zeros((QG, 128), F32)
    for k in range(4):
        own = (ids_ref[rep_index, k : k + 1, :] - first).astype(F32)
        plane = jnp.concatenate([spread_down(own[:, :128]), spread_down(own[:, 128:])], axis=0)
        plane_ref[k] = plane
        seen = jnp.where((plane.astype(jnp.int32) >> 7) == lane, 1.0, seen)
    flag_ref[...] = jnp.max(seen, axis=0, keepdims=True).astype(jnp.int32)


def hits_of(plane_ref, first):
    label = iota((QG, 128), 1).astype(F32) + first.astype(F32)
    hits = jnp.zeros((QG, 128), F32)
    for k in range(4):
        hits += jnp.where(plane_ref[k] == label, 1.0, 0.0)
    return hits.astype(BF16)


def old_slot(step, slot_ref):
    return step + (step >= slot_ref[0]).astype(jnp.int32)


def positive_kernel(slot_ref, flag_ref, plane_ref, lab_ref, out_ref):
    step = pl.program_id(0)

    @pl.when(step == 0)
    def _():
        out_ref[...] = jnp.zeros_like(out_ref)

    slot = old_slot(step, slot_ref)
    for part in range(6):
        tile = slot * 6 + part

        @pl.when(flag_ref[0, tile] > 0)
        def _():
            rows = lab_ref[part * 128 : (part + 1) * 128, :]
            out_ref[...] += dot(hits_of(plane_ref, tile * 128), rows)


def refresh_kernel(key_ref, got_ref, free_ref, pos_ref, out_ref):
    own = iota((HALF, QG), 0).astype(F32)
    odd = (iota((HALF, QG), 1) & 1) == 1
    matches = [key_ref[k : k + 1, :] == own for k in range(PER)]
    got = [got_ref[..., k * HALF : (k + 1) * HALF].reshape(QG, HALF) for k in range(PER)]
    for h in range(2):
        cols = slice(h * HALF, (h + 1) * HALF)
        mine = odd if h else ~odd
        placed = jnp.zeros((HALF, HALF), F32)
        for k in range(PER):
            placed += dot(one_hot(matches[k] & mine), got[k])
        out_ref[:, cols] = (free_ref[:, cols].astype(F32) + placed).astype(BF16)


def three_parts(value):
    high = value.astype(BF16).astype(F32)
    rest = value - high
    middle = rest.astype(BF16).astype(F32)
    return [high, middle, rest - middle]


def over_lanes(fn, value):
    total = value[:, :128]
    for at in range(128, value.shape[1], 128):
        total = fn(total, value[:, at : at + 128])
    return total


def score_kernel(
    slot_ref, flag_ref, got_ref, own_ref, other_ref, lab_ref, plane_ref, pos_ref, out_ref,
    q_buf, lab_buf, plane_buf, pos_buf, sems,
):
    rep = lax.axis_index("rep")
    slot = slot_ref[0]

    def rows_at(first, size):
        return lab_buf.at[pl.ds(first, size), :]

    query_copy = pltpu.make_async_copy(got_ref.at[:, :, pl.ds(ROWS, D)], q_buf, sems.at[SLOTS])
    query_copy.start()
    lab_copies = []
    for i in range(OLD):
        source = (i + (i >= slot).astype(jnp.int32)) * D
        lab_copies.append(
            pltpu.make_async_copy(lab_ref.at[pl.ds(source, D), :], rows_at(i * D, D), sems.at[i])
        )
        lab_copies[-1].start()
    own_copy = pltpu.make_async_copy(
        own_ref, rows_at(OLD * D + rep * HALF, HALF), sems.at[OLD]
    )
    other_copy = pltpu.make_async_copy(
        other_ref, rows_at(OLD * D + (1 - rep) * HALF, HALF), sems.at[SLOTS + 1]
    )
    plane_copy = pltpu.make_async_copy(plane_ref, plane_buf, sems.at[SLOTS + 2])
    pos_copy = pltpu.make_async_copy(pos_ref, pos_buf, sems.at[SLOTS + 3])
    for copy in (own_copy, other_copy, plane_copy, pos_copy):
        copy.start()
    query_copy.wait()
    queries = q_buf[...].reshape(QG, D)

    def logits_of(i):
        if i < OLD:
            lab_copies[i].wait()
        else:
            own_copy.wait()
            other_copy.wait()
        return dot_last(queries, lab_buf[i * D : (i + 1) * D, :])

    peak = jnp.full((QG, 1), -jnp.inf, F32)
    total = jnp.zeros((QG, 128), F32)
    grads = jnp.zeros((QG, D), F32)
    following = logits_of(0)
    for i in range(SLOTS):
        logits = following
        if i + 1 < SLOTS:
            following = logits_of(i + 1)
        higher = jnp.maximum(peak, jnp.max(over_lanes(jnp.maximum, logits), axis=1, keepdims=True))
        scale = jnp.exp(peak - higher)
        weight = jnp.exp(logits - higher)
        total = total * scale + over_lanes(jnp.add, weight)
        grads = grads * scale + dot(weight.astype(BF16), lab_buf[i * D : (i + 1) * D, :])
        peak = higher
    out_ref[..., :D] = grads.astype(BF16).reshape(N_CLS, 2, D)
    plane_copy.wait()
    pos_copy.wait()
    for part in range(6):
        tile = slot * 6 + part

        @pl.when(flag_ref[0, tile] > 0)
        def _():
            rows = lab_buf[OLD * D + part * 128 : OLD * D + (part + 1) * 128, :]
            pos_buf[...] += dot(hits_of(plane_buf, tile * 128), rows)

    positive = pos_buf[...]
    out_ref[..., D : 2 * D] = positive.astype(BF16).reshape(N_CLS, 2, D)
    picked = jnp.sum(queries.astype(F32) * positive, axis=1, keepdims=True)
    exp_total = jnp.sum(total, axis=1, keepdims=True)
    lane = iota((QG, 128), 1)
    stats = jnp.zeros((QG, 128), F32)
    for at, part in enumerate(three_parts(peak) + three_parts(exp_total) + three_parts(picked)):
        stats = jnp.where(lane == at, part, stats)
    out_ref[..., 2 * D :] = stats.astype(BF16).reshape(N_CLS, 2, 128)


def finish_kernel(ids_ref, back_ref, loss_ref, grad_ref):
    back = back_ref[...].reshape(QG, BACK)
    stats = back[:, 2 * D :].astype(F32)

    def column(at):
        return stats[:, at : at + 1] + stats[:, at + 1 : at + 2] + stats[:, at + 2 : at + 3]

    peak, total, picked = column(0), column(3), column(6)
    odd = (iota((QG, 1), 0) & 1) == 1
    valid = jnp.where(ids_ref[lax.axis_index("rep")] >= 0, 1.0, 0.0)
    column_of = iota((4, QG), 1) - 2 * lax.axis_index(CLS)
    losses, grads = [], []
    for h in range(2):
        mine = odd if h else ~odd
        top = jnp.max(jnp.where(mine, peak, -jnp.inf), axis=0, keepdims=True)
        weight = jnp.where(mine, jnp.exp(peak - top), 0.0)
        exp_total = jnp.sum(weight * total, axis=0, keepdims=True)
        count = jnp.sum(jnp.where(column_of == h, valid, 0.0), axis=1, keepdims=True)
        inverse = 1.0 / jnp.sum(count, axis=0, keepdims=True)
        chosen = jnp.sum(jnp.where(mine, picked, 0.0), axis=0, keepdims=True)
        losses.append(top + jnp.log(exp_total) - chosen * inverse)
        scaled = back[:, :D].astype(F32) * (weight / exp_total)
        scaled -= jnp.where(mine, back[:, D : 2 * D].astype(F32), 0.0) * inverse
        grads.append(jnp.sum(scaled, axis=0, keepdims=True))
    loss_ref[...] = jnp.concatenate(losses, axis=1)
    grad_ref[...] = jnp.concatenate(grads, axis=0).astype(BF16).reshape(1, 2, D)


def per_device(
    queries,
    positives,
    label_vectors,
    refresh_slot,
    features,
    encoder_weight,
    encoder_gain,
    free_vectors,
    targets,
):
    target_rows = targets.reshape(768, 128)
    slot = refresh_slot.reshape(1)
    ids = positives.transpose(0, 2, 1)

    sending = pl.pallas_call(
        encode_kernel,
        out_shape=jax.ShapeDtypeStruct((N_CLS, 2, SEND), BF16),
        in_specs=[vmem_spec()] * 5,
        out_specs=vmem_spec(),
        name="encode",
    )(features, encoder_weight, encoder_gain.reshape(6, 128), target_rows, queries)
    keys, planes, flags = pl.pallas_call(
        place_kernel,
        out_shape=[
            jax.ShapeDtypeStruct((8, QG), F32),
            jax.ShapeDtypeStruct((4, QG, 128), F32),
            jax.ShapeDtypeStruct((1, 128), jnp.int32),
        ],
        in_specs=[vmem_spec()] * 2,
        out_specs=[vmem_spec()] * 3,
        name="place",
    )(target_rows, ids)
    got = lax.all_to_all(sending, CLS, 0, 0, tiled=True)

    def all_of(shape):
        return pl.BlockSpec(shape, lambda *args: (0,) * len(shape))

    positive_old = pl.pallas_call(
        positive_kernel,
        out_shape=jax.ShapeDtypeStruct((QG, D), F32),
        grid_spec=pltpu.PrefetchScalarGridSpec(
            num_scalar_prefetch=2,
            grid=(OLD,),
            in_specs=[
                all_of((4, QG, 128)),
                pl.BlockSpec((D, D), lambda step, slot_ref, flag_ref: (old_slot(step, slot_ref), 0)),
            ],
            out_specs=all_of((QG, D)),
        ),
        name="positive",
    )(slot, flags, planes, label_vectors)

    refreshed = pl.pallas_call(
        refresh_kernel,
        out_shape=jax.ShapeDtypeStruct((HALF, D), BF16),
        grid=(1,),
        in_specs=[
            all_of((8, QG)),
            pl.BlockSpec((N_CLS, 2, ROWS), lambda step: (0, 0, 0)),
            all_of((HALF, D)),
            pl.BlockSpec(memory_space=pl.ANY),
        ],
        out_specs=all_of((HALF, D)),
        name="refresh",
    )(keys, got, free_vectors, positive_old)
    partner = lax.ppermute(refreshed, "rep", [(0, 1), (1, 0)])

    any_spec = pl.BlockSpec(memory_space=pl.ANY)
    leaving = pl.pallas_call(
        score_kernel,
        out_shape=jax.ShapeDtypeStruct((N_CLS, 2, BACK), BF16),
        in_specs=[smem_spec(), smem_spec()] + [any_spec] * 6,
        out_specs=vmem_spec(),
        scratch_shapes=[
            pltpu.VMEM((N_CLS, 2, D), BF16),
            pltpu.VMEM((SLOTS * D, D), BF16),
            pltpu.VMEM((4, QG, 128), F32),
            pltpu.VMEM((QG, D), F32),
            pltpu.SemaphoreType.DMA((SLOTS + 4,)),
        ],
        name="score",
    )(slot, flags, got, refreshed, partner, label_vectors, planes, positive_old)
    back = lax.all_to_all(leaving, CLS, 0, 0, tiled=True)
    loss, grads = pl.pallas_call(
        finish_kernel,
        out_shape=[jax.ShapeDtypeStruct((1, 2), F32), jax.ShapeDtypeStruct((1, 2, D), BF16)],
        in_specs=[vmem_spec()] * 2,
        out_specs=[vmem_spec()] * 2,
        name="finish",
    )(ids, back)
    return loss, grads, refreshed


def solution(mesh):
    torus = Mesh(
        mesh.devices.reshape(4, 8, 4, mesh.shape["rep"]), ("cls_0", "cls_1", "cls_2", "rep")
    )
    placed = (
        P("rep", CLS, None),
        P(),
        P(CLS, None),
        P(),
        P(CLS_REP, None),
        P(),
        P(),
        P(CLS_REP, None),
        P(),
    )
    return jax.shard_map(
        per_device,
        mesh=torus,
        in_specs=placed,
        out_specs=(P("rep", CLS), P("rep", CLS, None), P(CLS_REP, None)),
        check_vma=False,
    )
```

time: 132 us -> 104 us (0.79)
  blocking collectives: 0 us -> 33.5 us
  waiting for transfers between devices: 52.2 us -> 21 us
  local copies, waits for them, and re-layouts: 12.9 us -> 1.77 us
  Pallas kernels: 40.5 us -> 30.8 us
  starting transfers between devices: 22.2 us -> 15 us
  other arithmetic: 2.5 us -> 0 us
    all_to_all x0 -> x1, blocking collectives: none -> 33.5 us  [per_device(): back = lax.all_to_all(leaving, CLS, 0, 0, tiled=True)]
    all_to_all x2 -> x1, waiting for transfers between devices: 52.2 us -> 18.7 us  [per_device(): got = lax.all_to_all(sending, CLS, 0, 0, tiled=True)]
    reshape x5 -> x0, local copies, waits for them, and re-layouts: 9.97 us -> none  [the longest x1 3.18 us: per_device(): got = lax.all_to_all(sending.reshape(N_CLS, 2, SEND), CLS, 0, 0, tiled=True)]
    all_to_all x2 -> x1, starting transfers between devices: 22.2 us -> 15 us  [per_device(): got = lax.all_to_all(sending, CLS, 0, 0, tiled=True)]
    pallas_call x5 -> x4, Pallas kernels: 27.5 us -> 20.8 us  [the longest x1 10.9 us: per_device(): pl.pallas_call(score_kernel, out_shape=jax.ShapeDtypeStruct((N_CLS, 2, BA...]
    pallas_call x1, Pallas kernels: 9.66 us -> 7.13 us  [per_device(): pl.pallas_call(positive_kernel, out_shape=jax.ShapeDtypeStruct((QG, D), F...]
    ppermute x1, waiting for transfers between devices: 0.01 us -> 2.21 us  [per_device(): partner = lax.ppermute(refreshed, 'rep', [(0, 1), (1, 0)])]
  transfers between devices with their start and end apart: 3 -> 2, of which waited for: 2 -> 2; matrix products, arithmetic and copies ran while one was open for 1% -> 0% of each run, Pallas kernels for 19% -> 9%
where the time goes in v2:
time: 104 us; the launch traced here: 103 us
  blocking collectives  33.5 us (32%)
  Pallas kernels  30.8 us (30%)
  waiting for transfers between devices  21 us (20%)
  starting transfers between devices  15 us (14%)
  local copies, waits for them, and re-layouts  1.77 us (2%)
  between operations  1.3 us (1%)
    all_to_all x1, blocking collectives, per_device(): back = lax.all_to_all(leaving, CLS, 0, 0, tiled=True)  33.5 us
    all_to_all x1, waiting for transfers between devices, per_device(): got = lax.all_to_all(sending, CLS, 0, 0, tiled=True)  18.7 us
    all_to_all x1, starting transfers between devices, per_device(): got = lax.all_to_all(sending, CLS, 0, 0, tiled=True)  15 us
    pallas_call x1, Pallas kernels, per_device(): pl.pallas_call(score_kernel, out_shape=jax.ShapeDtypeStruct((N_CLS, 2, BA...  10.9 us
    pallas_call x1, Pallas kernels, per_device(): pl.pallas_call(positive_kernel, out_shape=jax.ShapeDtypeStruct((QG, D), F...  7.13 us
    pallas_call x1, Pallas kernels, per_device(): pl.pallas_call(encode_kernel, out_shape=jax.ShapeDtypeStruct((N_CLS, 2, S...  4.45 us
    pallas_call x1, Pallas kernels, per_device(): pl.pallas_call(finish_kernel, out_shape=[jax.ShapeDtypeStruct((1, 2), F32...  3.2 us
    pallas_call x1, Pallas kernels, per_device(): pl.pallas_call(refresh_kernel, out_shape=jax.ShapeDtypeStruct((HALF, D),...  2.88 us
  transfers between devices with their start and end apart: 2, of which 2 were waited for; matrix products, arithmetic and copies ran while one was open for 0% of the time, Pallas kernels for 9%

profile of v2, /device:TPU:32, one launch (start us, length us, event | category | flops | bytes accessed | tf_op | source)
XLA Modules:
  0.0 103.3 jit_solution(17777900544375182799)
XLA Ops:
  0.6 4.4 %encode.1 = bf16[128,2,1920]{2,1,0:T(2,128)(2,1)} custom-call(bf16[384,768]{1,0:T(8,128)(2,1)} %feat_ref.1, bf16[768,768]{1,0:T(8,128)(2,1)} %weight_ref.1, f32[6,128]{1,0:T(8,128)} %bitcast.10, s32[768,128]{1,0:T(8,128)} %bitcast.6, bf16[1,2,768]{2,1,0:T(2,128)(2,1)} %q_ref.1), custom_call_target="tpu_custom_call" | custom-call | tf_op jit(solution)/shard_map/encode/pallas_call | solution.py:285
  5.1 15.0 %all-to-all-start = ((bf16[128,2,1920]{2,1,0:T(2,128)(2,1)}), bf16[128,2,1920]{2,1,0:T(2,128)(2,1)S(1)}, u32[]{:S(2)}, u32[]{:S(2)}) async-start(bf16[128,2,1920]{2,1,0:T(2,128)(2,1)} %encode.1), calls=%async_computation | async-start | bytes 1966080 | tf_op jit(solution)/shard_map/all_to_all | solution.py:303
  20.7 2.3 %place.1 = (f32[8,256]{1,0:T(8,128)}, f32[4,256,128]{2,1,0:T(8,128)}, s32[1,128]{1,0:T(1,128)}) custom-call(s32[768,128]{1,0:T(8,128)} %bitcast.7, s32[2,4,256]{2,1,0:T(4,128)} %bitcast.8), custom_call_target="tpu_custom_call" | custom-call | tf_op jit(solution)/shard_map/place/pallas_call | solution.py:292
  23.0 7.1 %positive.1.pos_ref = f32[256,768]{1,0:T(8,128)} custom-call(s32[1]{0:T(128)} %bitcast.4.slot_ref, s32[1,128]{1,0:T(1,128)} %get-tuple-element.8.flag_ref, f32[4,256,128]{2,1,0:T(8,128)} %get-tuple-element.10.plane_ref, bf16[6144,768]{1,0:T(8,128)(2,1)} %lab_ref.3), custom_call_target="tpu_custom_call" | custom-call | tf_op jit(solution)/shard_map/positive/pallas_call | solution.py:308
  30.1 18.7 %all-to-all-done.got_ref = bf16[128,2,1920]{2,1,0:T(2,128)(2,1)S(1)} async-done(((bf16[128,2,1920]{2,1,0:T(2,128)(2,1)}), bf16[128,2,1920]{2,1,0:T(2,128)(2,1)S(1)}, u32[]{:S(2)}, u32[]{:S(2)}) %all-to-all-start) | async-done | bytes 983072 | tf_op jit(solution)/shard_map/all_to_all | solution.py:303
  48.9 0.0 copy-start
  48.9 1.0 copy-done
  49.8 2.9 %refresh.1.own_ref = bf16[384,768]{1,0:T(8,128)(2,1)} custom-call(f32[8,256]{1,0:T(8,128)} %get-tuple-element.9.key_ref, bf16[128,2,1920]{2,1,0:T(2,128)(2,1)} %copy-done, bf16[384,768]{1,0:T(8,128)(2,1)} %free_ref.1, f32[256,768]{1,0:T(8,128)} %positive.1.pos_ref), custom_call_target="tpu_custom_call" | custom-call | tf_op jit(solution)/shard_map/refresh/pallas_call | solution.py:323
  52.7 0.0 collective-permute-start
  52.7 2.2 %collective-permute-done.other_ref = bf16[384,768]{1,0:T(8,128)(2,1)S(1)} collective-permute-done((bf16[384,768]{1,0:T(8,128)(2,1)}, bf16[384,768]{1,0:T(8,128)(2,1)S(1)}, u32[]{:S(2)}, u32[]{:S(2)}) %collective-permute-start) | collective-permute-done | bytes 589856 | tf_op jit(solution)/shard_map/ppermute | solution.py:336
  54.9 0.0 copy-start.1
  54.9 0.8 copy-done.1
  55.7 10.9 %score.1 = bf16[128,2,1664]{2,1,0:T(2,128)(2,1)} custom-call(s32[1]{0:T(128)} %bitcast.5.slot_ref, s32[1,128]{1,0:T(1,128)} %get-tuple-element.8.flag_ref, bf16[128,2,1920]{2,1,0:T(2,128)(2,1)} %copy-done, bf16[384,768]{1,0:T(8,128)(2,1)} %refresh.1.own_ref, bf16[384,768]{1,0:T(8,128)(2,1)} %copy-done.1, bf16[6144,768]{1,0:T(8,128)(2,1)} %lab_ref.3, ...), custom_call_target="tpu_custom_call" | custom-call | tf_op jit(solution)/shard_map/score/pallas_call | solution.py:339
  66.6 33.5 %all_to_all.10.back_ref = bf16[128,2,1664]{2,1,0:T(2,128)(2,1)} all-to-all(bf16[128,2,1664]{2,1,0:T(2,128)(2,1)} %score.1), channel_id=1, replica_groups=mesh['cls_0'=4,'cls_1'=8,'cls_2'=4,'rep'=2] {'cls_0','cls_1','cls_2'}, dimensions={0} | all-to-all | bytes 1703936 | tf_op jit(solution)/shard_map/all_to_all | solution.py:353
  100.1 3.2 %finish.1 = (f32[1,2]{1,0:T(1,128)}, bf16[1,2,768]{2,1,0:T(2,128)(2,1)}) custom-call(s32[2,4,256]{2,1,0:T(4,128)} %bitcast.9, bf16[128,2,1664]{2,1,0:T(2,128)(2,1)} %all_to_all.10.back_ref), custom_call_target="tpu_custom_call" | custom-call | tf_op jit(solution)/shard_map/finish/pallas_call | solution.py:354
Async XLA Ops:
  5.1 43.8 %all-to-all-start = ((bf16[128,2,1920]{2,1,0:T(2,128)(2,1)}), bf16[128,2,1920]{2,1,0:T(2,128)(2,1)S(1)}, u32[]{:S(2)}, u32[]{:S(2)}) async-start(bf16[128,2,1920]{2,1,0:T(2,128)(2,1)} %encode.1), calls=%async_computation | async-start | bytes 1966080 | tf_op jit(solution)/shard_map/all_to_all | solution.py:303
  48.9 1.0 copy-start
  52.7 2.2 %collective-permute-start = (bf16[384,768]{1,0:T(8,128)(2,1)}, bf16[384,768]{1,0:T(8,128)(2,1)S(1)}, u32[]{:S(2)}, u32[]{:S(2)}) collective-permute-start(bf16[384,768]{1,0:T(8,128)(2,1)} %refresh.1.own_ref), channel_id=1, source_target_pairs={{0,1},{1,0},{2,3},{3,2},{4,5},{5,4},{6,7},{7,6},{8,9},{9,8},{10,11... | collective-permute-start | bytes 1769480 | tf_op jit(solution)/shard_map/ppermute | solution.py:336
  54.9 0.8 copy-start.1

commit v3 on v2

--- a/solution.py
+++ b/solution.py
@@ -16,7 +16,6 @@
 CLS = ("cls_0", "cls_1", "cls_2")
 CLS_REP = ("cls_0", "cls_1", "cls_2", "rep")
 ROWS = PER * HALF
-SEND = ROWS + D
 BACK = 2 * D + 128
 F32 = jnp.float32
 BF16 = jnp.bfloat16
@@ -54,7 +53,7 @@
     return jnp.broadcast_to(row, (128, 128)).T
 
 
-def encode_kernel(feat_ref, weight_ref, gain_ref, tgt_ref, q_ref, out_ref):
+def encode_kernel(feat_ref, weight_ref, gain_ref, tgt_ref, out_ref):
     block = lax.axis_index(CLS_REP)
     hidden = dot(feat_ref[...], weight_ref[...])
     mean = jnp.mean(hidden * hidden, axis=1, keepdims=True)
@@ -77,7 +76,6 @@
         total = dot(one_hot(hit & ~odd), encoded[:, :HALF])
         total += dot(one_hot(hit & odd), encoded[:, HALF:])
         out_ref[..., k * HALF : (k + 1) * HALF] = total.astype(BF16).reshape(N_CLS, 2, HALF)
-    out_ref[..., ROWS:] = jnp.broadcast_to(q_ref[...], (N_CLS, 2, D))
 
 
 def place_kernel(tgt_ref, ids_ref, key_ref, plane_ref, flag_ref):
@@ -114,28 +112,36 @@
     return hits.astype(BF16)
 
 
-def old_slot(step, slot_ref):
-    return step + (step >= slot_ref[0]).astype(jnp.int32)
-
-
-def positive_kernel(slot_ref, flag_ref, plane_ref, lab_ref, out_ref):
-    step = pl.program_id(0)
-
-    @pl.when(step == 0)
-    def _():
-        out_ref[...] = jnp.zeros_like(out_ref)
-
-    slot = old_slot(step, slot_ref)
-    for part in range(6):
-        tile = slot * 6 + part
+def positive_kernel(slot_ref, flag_ref, plane_ref, lab_ref, out_ref, lab_buf, sems):
+    out_ref[...] = jnp.zeros_like(out_ref)
+
+    def copy_of(i, part):
+        tile = (i + (i >= slot_ref[0]).astype(jnp.int32)) * 6 + part
+        at = i * 6 + part
+        return tile, pltpu.make_async_copy(
+            lab_ref.at[pl.ds(tile * 128, 128), :], lab_buf.at[at], sems.at[at]
+        )
+
+    for i in range(OLD):
+        for part in range(6):
+            tile, copy = copy_of(i, part)
+            pl.when(flag_ref[0, tile] > 0)(copy.start)
+
+    def body(at, carry):
+        i = at // 6
+        tile, copy = copy_of(i, at - i * 6)
 
         @pl.when(flag_ref[0, tile] > 0)
         def _():
-            rows = lab_ref[part * 128 : (part + 1) * 128, :]
-            out_ref[...] += dot(hits_of(plane_ref, tile * 128), rows)
-
-
-def refresh_kernel(key_ref, got_ref, free_ref, pos_ref, out_ref):
+            copy.wait()
+            out_ref[...] += dot(hits_of(plane_ref, tile * 128), lab_buf[at])
+
+        return carry
+
+    lax.fori_loop(0, OLD * 6, body, 0)
+
+
+def refresh_kernel(key_ref, got_ref, free_ref, pos_ref, peak_ref, out_ref):
     own = iota((HALF, QG), 0).astype(F32)
     odd = (iota((HALF, QG), 1) & 1) == 1
     matches = [key_ref[k : k + 1, :] == own for k in range(PER)]
@@ -149,6 +155,58 @@
         out_ref[:, cols] = (free_ref[:, cols].astype(F32) + placed).astype(BF16)
 
 
+def over_lanes(fn, value):
+    total = value[:, :128]
+    for at in range(128, value.shape[1], 128):
+        total = fn(total, value[:, at : at + 128])
+    return total
+
+
+def absorb(state, logits, rows):
+    peak, total, grads = state
+    higher = jnp.maximum(peak, jnp.max(over_lanes(jnp.maximum, logits), axis=1, keepdims=True))
+    scale = jnp.exp(peak - higher)
+    weight = jnp.exp(logits - higher)
+    total = total * scale + over_lanes(jnp.add, weight)
+    grads = grads * scale + dot(weight.astype(BF16), rows)
+    return higher, total, grads
+
+
+def old_kernel(slot_ref, *refs):
+    pieces, (lab_ref, q_ref, peak_ref, total_ref, grad_ref, lab_buf, sems) = refs[:4], refs[4:]
+    copies = []
+    for i in range(OLD):
+        source = (i + (i >= slot_ref[0]).astype(jnp.int32)) * D
+        copies.append(
+            pltpu.make_async_copy(lab_ref.at[pl.ds(source, D), :], lab_buf.at[i], sems.at[i])
+        )
+        copies[-1].start()
+    line, lane = iota((QG, 64), 0), iota((QG, 64), 1)
+    behind_y = (lax.axis_index("cls_0") - (line >> 6)) & 3
+    behind_x = (lax.axis_index("cls_2") - ((line >> 1) & 3)) & 3
+    spot = behind_x * 16 + ((line >> 3) & 7) * 2 + (line & 1)
+    ordered = jnp.zeros((QG, D), F32)
+    for back, piece_ref in enumerate(pieces):
+        ordered += dot(one_hot((spot == lane) & (behind_y == back)), piece_ref[...])
+    queries = ordered.astype(BF16)
+    q_ref[...] = queries
+
+    def logits_of(i):
+        copies[i].wait()
+        return dot_last(queries, lab_buf[i])
+
+    state = (jnp.full((QG, 1), -jnp.inf, F32), jnp.zeros((QG, 128), F32), jnp.zeros((QG, D), F32))
+    following = logits_of(0)
+    for i in range(OLD):
+        logits = following
+        if i + 1 < OLD:
+            following = logits_of(i + 1)
+        state = absorb(state, logits, lab_buf[i])
+    peak_ref[...] = jnp.broadcast_to(state[0], (QG, 128))
+    total_ref[...] = state[1]
+    grad_ref[...] = state[2]
+
+
 def three_parts(value):
     high = value.astype(BF16).astype(F32)
     rest = value - high
@@ -156,77 +214,40 @@
     return [high, middle, rest - middle]
 
 
-def over_lanes(fn, value):
-    total = value[:, :128]
-    for at in range(128, value.shape[1], 128):
-        total = fn(total, value[:, at : at + 128])
-    return total
-
-
-def score_kernel(
-    slot_ref, flag_ref, got_ref, own_ref, other_ref, lab_ref, plane_ref, pos_ref, out_ref,
-    q_buf, lab_buf, plane_buf, pos_buf, sems,
+def fresh_kernel(
+    slot_ref, flag_ref, own_ref, other_ref, q_ref, peak_ref, total_ref, grad_ref, plane_ref,
+    pos_ref, out_ref, own_buf, other_buf, q_buf, peak_buf, total_buf, grad_buf, plane_buf,
+    pos_buf, sems,
 ):
     rep = lax.axis_index("rep")
     slot = slot_ref[0]
-
-    def rows_at(first, size):
-        return lab_buf.at[pl.ds(first, size), :]
-
-    query_copy = pltpu.make_async_copy(got_ref.at[:, :, pl.ds(ROWS, D)], q_buf, sems.at[SLOTS])
-    query_copy.start()
-    lab_copies = []
-    for i in range(OLD):
-        source = (i + (i >= slot).astype(jnp.int32)) * D
-        lab_copies.append(
-            pltpu.make_async_copy(lab_ref.at[pl.ds(source, D), :], rows_at(i * D, D), sems.at[i])
-        )
-        lab_copies[-1].start()
-    own_copy = pltpu.make_async_copy(
-        own_ref, rows_at(OLD * D + rep * HALF, HALF), sems.at[OLD]
-    )
-    other_copy = pltpu.make_async_copy(
-        other_ref, rows_at(OLD * D + (1 - rep) * HALF, HALF), sems.at[SLOTS + 1]
-    )
-    plane_copy = pltpu.make_async_copy(plane_ref, plane_buf, sems.at[SLOTS + 2])
-    pos_copy = pltpu.make_async_copy(pos_ref, pos_buf, sems.at[SLOTS + 3])
-    for copy in (own_copy, other_copy, plane_copy, pos_copy):
+    pairs = [
+        (q_ref, q_buf), (own_ref, own_buf), (other_ref, other_buf), (peak_ref, peak_buf),
+        (total_ref, total_buf), (grad_ref, grad_buf), (plane_ref, plane_buf), (pos_ref, pos_buf),
+    ]
+    copies = [pltpu.make_async_copy(a, b, sems.at[i]) for i, (a, b) in enumerate(pairs)]
+    for copy in copies:
         copy.start()
-    query_copy.wait()
-    queries = q_buf[...].reshape(QG, D)
-
-    def logits_of(i):
-        if i < OLD:
-            lab_copies[i].wait()
-        else:
-            own_copy.wait()
-            other_copy.wait()
-        return dot_last(queries, lab_buf[i * D : (i + 1) * D, :])
-
-    peak = jnp.full((QG, 1), -jnp.inf, F32)
-    total = jnp.zeros((QG, 128), F32)
-    grads = jnp.zeros((QG, D), F32)
-    following = logits_of(0)
-    for i in range(SLOTS):
-        logits = following
-        if i + 1 < SLOTS:
-            following = logits_of(i + 1)
-        higher = jnp.maximum(peak, jnp.max(over_lanes(jnp.maximum, logits), axis=1, keepdims=True))
-        scale = jnp.exp(peak - higher)
-        weight = jnp.exp(logits - higher)
-        total = total * scale + over_lanes(jnp.add, weight)
-        grads = grads * scale + dot(weight.astype(BF16), lab_buf[i * D : (i + 1) * D, :])
-        peak = higher
+    copies[0].wait()
+    copies[1].wait()
+    queries = q_buf[...]
+    own_logits = dot_last(queries, own_buf[...])
+    copies[2].wait()
+    other_logits = dot_last(queries, other_buf[...])
+    for copy in copies[3:]:
+        copy.wait()
+    rows = jnp.concatenate([own_buf[...], other_buf[...]], axis=0)
+    state = (peak_buf[:, :1], total_buf[...], grad_buf[...])
+    peak, total, grads = absorb(state, jnp.concatenate([own_logits, other_logits], axis=1), rows)
     out_ref[..., :D] = grads.astype(BF16).reshape(N_CLS, 2, D)
-    plane_copy.wait()
-    pos_copy.wait()
-    for part in range(6):
-        tile = slot * 6 + part
-
-        @pl.when(flag_ref[0, tile] > 0)
-        def _():
-            rows = lab_buf[OLD * D + part * 128 : OLD * D + (part + 1) * 128, :]
-            pos_buf[...] += dot(hits_of(plane_buf, tile * 128), rows)
+    for buf, half in ((own_buf, rep), (other_buf, 1 - rep)):
+        for part in range(3):
+            tile = slot * 6 + half * 3 + part
+
+            @pl.when(flag_ref[0, tile] > 0)
+            def _():
+                chosen = buf[part * 128 : (part + 1) * 128, :]
+                pos_buf[...] += dot(hits_of(plane_buf, tile * 128), chosen)
 
     positive = pos_buf[...]
     out_ref[..., D : 2 * D] = positive.astype(BF16).reshape(N_CLS, 2, D)
@@ -267,6 +288,11 @@
     grad_ref[...] = jnp.concatenate(grads, axis=0).astype(BF16).reshape(1, 2, D)
 
 
+def from_behind(value, axis, shift):
+    length = lax.axis_size(axis)
+    return lax.ppermute(value, axis, [(i, (i + shift) % length) for i in range(length)])
+
+
 def per_device(
     queries,
     positives,
@@ -282,13 +308,16 @@
     slot = refresh_slot.reshape(1)
     ids = positives.transpose(0, 2, 1)
 
+    column = lax.all_to_all(
+        jnp.broadcast_to(queries.reshape(1, 2, D), (8, 2, D)), "cls_1", 0, 0, tiled=True
+    )
     sending = pl.pallas_call(
         encode_kernel,
-        out_shape=jax.ShapeDtypeStruct((N_CLS, 2, SEND), BF16),
-        in_specs=[vmem_spec()] * 5,
+        out_shape=jax.ShapeDtypeStruct((N_CLS, 2, ROWS), BF16),
+        in_specs=[vmem_spec()] * 4,
         out_specs=vmem_spec(),
         name="encode",
-    )(features, encoder_weight, encoder_gain.reshape(6, 128), target_rows, queries)
+    )(features, encoder_weight, encoder_gain.reshape(6, 128), target_rows)
     keys, planes, flags = pl.pallas_call(
         place_kernel,
         out_shape=[
@@ -300,56 +329,68 @@
         out_specs=[vmem_spec()] * 3,
         name="place",
     )(target_rows, ids)
+    sending, column = lax.optimization_barrier((sending, column))
     got = lax.all_to_all(sending, CLS, 0, 0, tiled=True)
 
-    def all_of(shape):
-        return pl.BlockSpec(shape, lambda *args: (0,) * len(shape))
-
+    column = column.reshape(16, D)
+    row = [column] + [from_behind(column, "cls_2", shift) for shift in (1, 2, 3)]
+    layer = jnp.concatenate(row, axis=0)
+    pieces = [layer] + [from_behind(layer, "cls_0", shift) for shift in (1, 2, 3)]
+
+    any_spec = pl.BlockSpec(memory_space=pl.ANY)
     positive_old = pl.pallas_call(
         positive_kernel,
         out_shape=jax.ShapeDtypeStruct((QG, D), F32),
-        grid_spec=pltpu.PrefetchScalarGridSpec(
-            num_scalar_prefetch=2,
-            grid=(OLD,),
-            in_specs=[
-                all_of((4, QG, 128)),
-                pl.BlockSpec((D, D), lambda step, slot_ref, flag_ref: (old_slot(step, slot_ref), 0)),
-            ],
-            out_specs=all_of((QG, D)),
-        ),
+        in_specs=[smem_spec()] * 2 + [vmem_spec(), any_spec],
+        out_specs=vmem_spec(),
+        scratch_shapes=[
+            pltpu.VMEM((OLD * 6, 128, D), BF16),
+            pltpu.SemaphoreType.DMA((OLD * 6,)),
+        ],
         name="positive",
     )(slot, flags, planes, label_vectors)
+
+    all_queries, peak, total, grads = pl.pallas_call(
+        old_kernel,
+        out_shape=[
+            jax.ShapeDtypeStruct((QG, D), BF16),
+            jax.ShapeDtypeStruct((QG, 128), F32),
+            jax.ShapeDtypeStruct((QG, 128), F32),
+            jax.ShapeDtypeStruct((QG, D), F32),
+        ],
+        in_specs=[smem_spec()] + [vmem_spec()] * 4 + [any_spec],
+        out_specs=[vmem_spec()] * 4,
+        scratch_shapes=[pltpu.VMEM((OLD, D, D), BF16), pltpu.SemaphoreType.DMA((OLD,))],
+        name="old",
+    )(slot, *pieces, label_vectors)
 
     refreshed = pl.pallas_call(
         refresh_kernel,
         out_shape=jax.ShapeDtypeStruct((HALF, D), BF16),
-        grid=(1,),
-        in_specs=[
-            all_of((8, QG)),
-            pl.BlockSpec((N_CLS, 2, ROWS), lambda step: (0, 0, 0)),
-            all_of((HALF, D)),
-            pl.BlockSpec(memory_space=pl.ANY),
-        ],
-        out_specs=all_of((HALF, D)),
+        in_specs=[vmem_spec()] * 3 + [any_spec] * 2,
+        out_specs=vmem_spec(),
         name="refresh",
-    )(keys, got, free_vectors, positive_old)
+    )(keys, got, free_vectors, positive_old, peak)
     partner = lax.ppermute(refreshed, "rep", [(0, 1), (1, 0)])
 
-    any_spec = pl.BlockSpec(memory_space=pl.ANY)
     leaving = pl.pallas_call(
-        score_kernel,
+        fresh_kernel,
         out_shape=jax.ShapeDtypeStruct((N_CLS, 2, BACK), BF16),
-        in_specs=[smem_spec(), smem_spec()] + [any_spec] * 6,
+        in_specs=[smem_spec()] * 2 + [any_spec] * 8,
         out_specs=vmem_spec(),
         scratch_shapes=[
-            pltpu.VMEM((N_CLS, 2, D), BF16),
-            pltpu.VMEM((SLOTS * D, D), BF16),
+            pltpu.VMEM((HALF, D), BF16),
+            pltpu.VMEM((HALF, D), BF16),
+            pltpu.VMEM((QG, D), BF16),
+            pltpu.VMEM((QG, 128), F32),
+            pltpu.VMEM((QG, 128), F32),
+            pltpu.VMEM((QG, D), F32),
             pltpu.VMEM((4, QG, 128), F32),
             pltpu.VMEM((QG, D), F32),
-            pltpu.SemaphoreType.DMA((SLOTS + 4,)),
+            pltpu.SemaphoreType.DMA((8,)),
         ],
-        name="score",
-    )(slot, flags, got, refreshed, partner, label_vectors, planes, positive_old)
+        name="fresh",
+    )(slot, flags, refreshed, partner, all_queries, peak, total, grads, planes, positive_old)
     back = lax.all_to_all(leaving, CLS, 0, 0, tiled=True)
     loss, grads = pl.pallas_call(
         finish_kernel,

time: 104 us -> 114 us (1.096)
  starting transfers between devices: 15 us -> 29.4 us
  waiting for transfers between devices: 21 us -> 8.97 us
  blocking collectives: 33.5 us -> 36.9 us
  Pallas kernels: 30.8 us -> 33.1 us
  local copies, waits for them, and re-layouts: 1.77 us -> 3.65 us
    all_to_all x1, waiting for transfers between devices: 18.7 us -> 0.01 us  [per_device(): got = lax.all_to_all(sending, CLS, 0, 0, tiled=True)]
    ppermute x0 -> x6, starting transfers between devices: none -> 9.27 us  [from_behind(): lax.ppermute(value, axis, [(i, (i + shift) % length) for i in range(lengt...]
    all_to_all x0 -> x1, starting transfers between devices: none -> 8.57 us  [per_device(): lax.all_to_all(jnp.broadcast_to(queries.reshape(1, 2, D), (8, 2, D)), 'cl...]
    ppermute x0 -> x6, waiting for transfers between devices: none -> 4.62 us  [from_behind(): lax.ppermute(value, axis, [(i, (i + shift) % length) for i in range(lengt...]
    pallas_call x2 -> x3, Pallas kernels: 15.3 us -> 19.1 us  [the longest x1 9.39 us: per_device(): pl.pallas_call(old_kernel, out_shape=[jax.ShapeDtypeStruct((QG, D), BF16)...]
    all_to_all x1, starting transfers between devices: 15 us -> 11.5 us  [per_device(): got = lax.all_to_all(sending, CLS, 0, 0, tiled=True)]
    all_to_all x1, blocking collectives: 33.5 us -> 36.9 us  [per_device(): back = lax.all_to_all(leaving, CLS, 0, 0, tiled=True)]
    all_to_all x0 -> x1, waiting for transfers between devices: none -> 2.13 us  [per_device(): lax.all_to_all(jnp.broadcast_to(queries.reshape(1, 2, D), (8, 2, D)), 'cl...]
  transfers between devices with their start and end apart: 2 -> 9, of which waited for: 2 -> 3; matrix products, arithmetic and copies ran while one was open for 0% -> 0% of each run, Pallas kernels for 9% -> 19%
where the time goes in v3:
time: 114 us; the launch traced here: 113 us
  blocking collectives  36.9 us (32%)
  Pallas kernels  33.1 us (29%)
  starting transfers between devices  29.4 us (26%)
  waiting for transfers between devices  8.97 us (8%)
  local copies, waits for them, and re-layouts  3.65 us (3%)
  between operations  1.43 us (1%)
    all_to_all x1, blocking collectives, per_device(): back = lax.all_to_all(leaving, CLS, 0, 0, tiled=True)  36.9 us
    all_to_all x1, starting transfers between devices, per_device(): got = lax.all_to_all(sending, CLS, 0, 0, tiled=True)  11.5 us
    pallas_call x1, Pallas kernels, per_device(): pl.pallas_call(old_kernel, out_shape=[jax.ShapeDtypeStruct((QG, D), BF16)...  9.39 us
    ppermute x6, starting transfers between devices, from_behind(): lax.ppermute(value, axis, [(i, (i + shift) % length) for i in range(lengt...  9.27 us
    all_to_all x1, starting transfers between devices, per_device(): lax.all_to_all(jnp.broadcast_to(queries.reshape(1, 2, D), (8, 2, D)), 'cl...  8.57 us
    pallas_call x1, Pallas kernels, per_device(): pl.pallas_call(positive_kernel, out_shape=jax.ShapeDtypeStruct((QG, D), F...  5.63 us
    pallas_call x1, Pallas kernels, per_device(): pl.pallas_call(fresh_kernel, out_shape=jax.ShapeDtypeStruct((N_CLS, 2, BA...  5.45 us
    ppermute x6, waiting for transfers between devices, from_behind(): lax.ppermute(value, axis, [(i, (i + shift) % length) for i in range(lengt...  4.62 us
  transfers between devices with their start and end apart: 9, of which 3 were waited for; matrix products, arithmetic and copies ran while one was open for 0% of the time, Pallas kernels for 19%

profile of v3, /device:TPU:32, one launch (start us, length us, event | category | flops | bytes accessed | tf_op | source)
XLA Modules:
  0.0 113.4 jit_solution(71380550339347847)
XLA Ops:
  0.6 1.3 %broadcast_in_dim.8 = bf16[8,2,768]{2,1,0:T(2,128)(2,1)} broadcast(bf16[2,768]{1,0:T(2,128)(2,1)} %bitcast.13), dimensions={1,2} | broadcast | bytes 27648 | tf_op jit(solution)/shard_map/broadcast_in_dim | solution.py:312
  1.9 8.6 %all-to-all-start = ((bf16[8,2,768]{2,1,0:T(2,128)(2,1)}), bf16[8,2,768]{2,1,0:T(2,128)(2,1)S(1)}, u32[]{:S(2)}, u32[]{:S(2)}) async-start(bf16[8,2,768]{2,1,0:T(2,128)(2,1)} %broadcast_in_dim.8), calls=%async_computation | async-start | bytes 49152 | tf_op jit(solution)/shard_map/all_to_all | solution.py:311
  10.5 4.3 %encode.1 = bf16[128,2,1152]{2,1,0:T(2,128)(2,1)} custom-call(bf16[384,768]{1,0:T(8,128)(2,1)} %feat_ref.1, bf16[768,768]{1,0:T(8,128)(2,1)} %weight_ref.1, f32[6,128]{1,0:T(8,128)} %bitcast.12, s32[768,128]{1,0:T(8,128)} %bitcast.8), custom_call_target="tpu_custom_call" | custom-call | tf_op jit(solution)/shard_map/encode/pallas_call | solution.py:314
  14.8 2.1 %all-to-all-done = bf16[8,2,768]{2,1,0:T(2,128)(2,1)S(1)} async-done(((bf16[8,2,768]{2,1,0:T(2,128)(2,1)}), bf16[8,2,768]{2,1,0:T(2,128)(2,1)S(1)}, u32[]{:S(2)}, u32[]{:S(2)}) %all-to-all-start) | async-done | bytes 24608 | tf_op jit(solution)/shard_map/all_to_all | solution.py:311
  16.9 11.5 %all-to-all-start.1 = ((bf16[128,2,1152]{2,1,0:T(2,128)(2,1)}), bf16[128,2,1152]{2,1,0:T(2,128)(2,1)S(1)}, u32[]{:S(2)}, u32[]{:S(2)}) async-start(bf16[128,2,1152]{2,1,0:T(2,128)(2,1)} %encode.1), calls=%async_computation.1 | async-start | bytes 1179648 | tf_op jit(solution)/shard_map/all_to_all | solution.py:333
  28.5 2.8 %collective-permute-start.2 = (bf16[16,768]{1,0:T(8,128)(2,1)S(1)}, bf16[16,768]{1,0:T(8,128)(2,1)S(1)}, u32[]{:S(2)}, u32[]{:S(2)}) collective-permute-start(bf16[16,768]{1,0:T(8,128)(2,1)S(1)} %reshape.21), channel_id=1, source_target_pairs={{0,6},{2,0},{4,2},{6,4},{1,7},{3,1},{5,3},{7,5},{8,14},{10,8},{12,... | collective-permute-start | bytes 73736 | tf_op jit(solution)/shard_map/ppermute | solution.py:293
  31.2 0.9 collective-permute-start.1
  32.1 0.9 collective-permute-start
  33.0 4.6 %collective-permute-done = bf16[16,768]{1,0:T(8,128)(2,1)S(1)} collective-permute-done((bf16[16,768]{1,0:T(8,128)(2,1)S(1)}, bf16[16,768]{1,0:T(8,128)(2,1)S(1)}, u32[]{:S(2)}, u32[]{:S(2)}) %collective-permute-start) | collective-permute-done | bytes 24608 | tf_op jit(solution)/shard_map/ppermute | solution.py:293
  37.6 0.0 collective-permute-done.1
  37.6 0.0 collective-permute-done.2
  37.6 0.0 copy-start.2
  37.6 3.3 %collective-permute-start.5 = (bf16[64,768]{1,0:T(8,128)(2,1)S(1)}, bf16[64,768]{1,0:T(8,128)(2,1)S(1)}, u32[]{:S(2)}, u32[]{:S(2)}) collective-permute-start(bf16[64,768]{1,0:T(8,128)(2,1)S(1)} %constant_dynamic-update-slice_fusion.refs_0_), channel_id=1, source_target_pairs={{0,192},{64,0},{128,64},{192,128},{1,193},{65,1},{129,65},{193,129... | collective-permute-start | bytes 294920 | tf_op jit(solution)/shard_map/ppermute | solution.py:293
  40.9 0.4 collective-permute-start.4
  41.4 1.1 collective-permute-start.3
  43.1 2.3 %place.1 = (f32[8,256]{1,0:T(8,128)}, f32[4,256,128]{2,1,0:T(8,128)}, s32[1,128]{1,0:T(1,128)}) custom-call(s32[768,128]{1,0:T(8,128)} %bitcast.9, s32[2,4,256]{2,1,0:T(4,128)} %bitcast.10), custom_call_target="tpu_custom_call" | custom-call | tf_op jit(solution)/shard_map/place/pallas_call | solution.py:321
  45.4 5.6 %positive.1.pos_ref = f32[256,768]{1,0:T(8,128)} custom-call(s32[1]{0:T(128)} %bitcast.5.slot_ref, s32[1,128]{1,0:T(1,128)} %get-tuple-element.14.flag_ref, f32[4,256,128]{2,1,0:T(8,128)} %get-tuple-element.17.plane_ref, bf16[6144,768]{1,0:T(8,128)(2,1)} %refs_4_.1), custom_call_target="tpu_custom_call" | custom-call | tf_op jit(solution)/shard_map/positive/pallas_call | solution.py:341
  51.0 0.0 collective-permute-done.5.refs_3_
  51.0 0.0 copy-start.3
  51.0 0.0 collective-permute-done.4.refs_2_
  51.0 0.0 copy-start.4
  51.0 0.0 collective-permute-done.3.refs_1_
  51.1 0.0 copy-start.5
  51.1 0.0 copy-done.2
  51.1 0.6 copy-done.3
  51.6 0.1 copy-done.4
  51.7 0.0 copy-done.5
  51.7 9.4 %old.1 = (bf16[256,768]{1,0:T(8,128)(2,1)}, f32[256,128]{1,0:T(8,128)}, f32[256,128]{1,0:T(8,128)}, f32[256,768]{1,0:T(8,128)}) custom-call(s32[1]{0:T(128)} %bitcast.6.slot_ref, bf16[64,768]{1,0:T(8,128)(2,1)} %copy-done.2, bf16[64,768]{1,0:T(8,128)(2,1)} %copy-done.5, bf16[64,768]{1,0:T(8,128)(2,1)} %copy-done.4, bf16[64,768]{1,0:T(8,128)(2,1)} %copy-done.3, ...), custom_call_target="tpu_custom_call" | custom-call | tf_op jit(solution)/shard_map/old/pallas_call | solution.py:353
  61.1 0.0 all-to-all-done.1.got_ref
  61.1 0.0 copy-start
  61.1 0.8 copy-done
  62.0 2.9 %refresh.1.own_ref = bf16[384,768]{1,0:T(8,128)(2,1)} custom-call(f32[8,256]{1,0:T(8,128)} %get-tuple-element.15.key_ref, bf16[128,2,1152]{2,1,0:T(2,128)(2,1)} %copy-done, bf16[384,768]{1,0:T(8,128)(2,1)} %free_ref.1, f32[256,768]{1,0:T(8,128)} %positive.1.pos_ref, f32[256,128]{1,0:T(8,128)} %get-tuple-element.19.peak_ref), custom_call_target="tpu_custom_call" | custom-call | tf_op jit(solution)/shard_map/refresh/pallas_call | solution.py:367
  64.8 0.0 collective-permute-start.6
  64.8 2.2 %collective-permute-done.6.other_ref = bf16[384,768]{1,0:T(8,128)(2,1)S(1)} collective-permute-done((bf16[384,768]{1,0:T(8,128)(2,1)}, bf16[384,768]{1,0:T(8,128)(2,1)S(1)}, u32[]{:S(2)}, u32[]{:S(2)}) %collective-permute-start.6) | collective-permute-done | bytes 589856 | tf_op jit(solution)/shard_map/ppermute | solution.py:374
  67.1 0.0 copy-start.1
  67.1 0.8 copy-done.1
  67.9 5.4 %fresh.1 = bf16[128,2,1664]{2,1,0:T(2,128)(2,1)} custom-call(s32[1]{0:T(128)} %bitcast.7.slot_ref, s32[1,128]{1,0:T(1,128)} %get-tuple-element.14.flag_ref, bf16[384,768]{1,0:T(8,128)(2,1)} %refresh.1.own_ref, bf16[384,768]{1,0:T(8,128)(2,1)} %copy-done.1, bf16[256,768]{1,0:T(8,128)(2,1)} %get-tuple-element.20.q_ref, f32[256,128]{1,0:T(8,128)} %get-tuple-element.19.peak_ref, ...), custom_call_target="tpu_custom_call" | custom-call | tf_op jit(solution)/shard_map/fresh/pallas_call | solution.py:376
  73.3 36.9 %all_to_all.15.back_ref = bf16[128,2,1664]{2,1,0:T(2,128)(2,1)} all-to-all(bf16[128,2,1664]{2,1,0:T(2,128)(2,1)} %fresh.1), channel_id=1, replica_groups=mesh['cls_0'=4,'cls_1'=8,'cls_2'=4,'rep'=2] {'cls_0','cls_1','cls_2'}, dimensions={0} | all-to-all | bytes 1703936 | tf_op jit(solution)/shard_map/all_to_all | solution.py:394
  110.2 3.2 %finish.1 = (f32[1,2]{1,0:T(1,128)}, bf16[1,2,768]{2,1,0:T(2,128)(2,1)}) custom-call(s32[2,4,256]{2,1,0:T(4,128)} %bitcast.11, bf16[128,2,1664]{2,1,0:T(2,128)(2,1)} %all_to_all.15.back_ref), custom_call_target="tpu_custom_call" | custom-call | tf_op jit(solution)/shard_map/finish/pallas_call | solution.py:395
  (5 shorter events, 0.0 us)
Async XLA Ops:
  1.9 15.0 %all-to-all-start = ((bf16[8,2,768]{2,1,0:T(2,128)(2,1)}), bf16[8,2,768]{2,1,0:T(2,128)(2,1)S(1)}, u32[]{:S(2)}, u32[]{:S(2)}) async-start(bf16[8,2,768]{2,1,0:T(2,128)(2,1)} %broadcast_in_dim.8), calls=%async_computation | async-start | bytes 49152 | tf_op jit(solution)/shard_map/all_to_all | solution.py:311
  16.9 44.2 %all-to-all-start.1 = ((bf16[128,2,1152]{2,1,0:T(2,128)(2,1)}), bf16[128,2,1152]{2,1,0:T(2,128)(2,1)S(1)}, u32[]{:S(2)}, u32[]{:S(2)}) async-start(bf16[128,2,1152]{2,1,0:T(2,128)(2,1)} %encode.1), calls=%async_computation.1 | async-start | bytes 1179648 | tf_op jit(solution)/shard_map/all_to_all | solution.py:333
  28.5 9.1 %collective-permute-start.2 = (bf16[16,768]{1,0:T(8,128)(2,1)S(1)}, bf16[16,768]{1,0:T(8,128)(2,1)S(1)}, u32[]{:S(2)}, u32[]{:S(2)}) collective-permute-start(bf16[16,768]{1,0:T(8,128)(2,1)S(1)} %reshape.21), channel_id=1, source_target_pairs={{0,6},{2,0},{4,2},{6,4},{1,7},{3,1},{5,3},{7,5},{8,14},{10,8},{12,... | collective-permute-start | bytes 73736 | tf_op jit(solution)/shard_map/ppermute | solution.py:293
  31.2 6.3 %collective-permute-start.1 = (bf16[16,768]{1,0:T(8,128)(2,1)S(1)}, bf16[16,768]{1,0:T(8,128)(2,1)S(1)}, u32[]{:S(2)}, u32[]{:S(2)}) collective-permute-start(bf16[16,768]{1,0:T(8,128)(2,1)S(1)} %reshape.21), channel_id=1, source_target_pairs={{0,4},{2,6},{4,0},{6,2},{1,5},{3,7},{5,1},{7,3},{8,12},{10,14},{12... | collective-permute-start | bytes 73736 | tf_op jit(solution)/shard_map/ppermute | solution.py:293
  32.1 5.5 %collective-permute-start = (bf16[16,768]{1,0:T(8,128)(2,1)S(1)}, bf16[16,768]{1,0:T(8,128)(2,1)S(1)}, u32[]{:S(2)}, u32[]{:S(2)}) collective-permute-start(bf16[16,768]{1,0:T(8,128)(2,1)S(1)} %reshape.21), channel_id=1, source_target_pairs={{0,2},{2,4},{4,6},{6,0},{1,3},{3,5},{5,7},{7,1},{8,10},{10,12},{12... | collective-permute-start | bytes 73736 | tf_op jit(solution)/shard_map/ppermute | solution.py:293
  37.6 13.4 %copy-start.2 = (bf16[64,768]{1,0:T(8,128)(2,1)}, bf16[64,768]{1,0:T(8,128)(2,1)S(1)}, u32[]{:S(2)}) copy-start(bf16[64,768]{1,0:T(8,128)(2,1)S(1)} %constant_dynamic-update-slice_fusion.refs_0_) | copy-start | bytes 294916
  37.6 13.4 %collective-permute-start.5 = (bf16[64,768]{1,0:T(8,128)(2,1)S(1)}, bf16[64,768]{1,0:T(8,128)(2,1)S(1)}, u32[]{:S(2)}, u32[]{:S(2)}) collective-permute-start(bf16[64,768]{1,0:T(8,128)(2,1)S(1)} %constant_dynamic-update-slice_fusion.refs_0_), channel_id=1, source_target_pairs={{0,192},{64,0},{128,64},{192,128},{1,193},{65,1},{129,65},{193,129... | collective-permute-start | bytes 294920 | tf_op jit(solution)/shard_map/ppermute | solution.py:293
  40.9 10.1 %collective-permute-start.4 = (bf16[64,768]{1,0:T(8,128)(2,1)S(1)}, bf16[64,768]{1,0:T(8,128)(2,1)S(1)}, u32[]{:S(2)}, u32[]{:S(2)}) collective-permute-start(bf16[64,768]{1,0:T(8,128)(2,1)S(1)} %constant_dynamic-update-slice_fusion.refs_0_), channel_id=1, source_target_pairs={{0,128},{64,192},{128,0},{192,64},{1,129},{65,193},{129,1},{193,65... | collective-permute-start | bytes 294920 | tf_op jit(solution)/shard_map/ppermute | solution.py:293
  41.4 9.7 %collective-permute-start.3 = (bf16[64,768]{1,0:T(8,128)(2,1)S(1)}, bf16[64,768]{1,0:T(8,128)(2,1)S(1)}, u32[]{:S(2)}, u32[]{:S(2)}) collective-permute-start(bf16[64,768]{1,0:T(8,128)(2,1)S(1)} %constant_dynamic-update-slice_fusion.refs_0_), channel_id=1, source_target_pairs={{0,64},{64,128},{128,192},{192,0},{1,65},{65,129},{129,193},{193,1... | collective-permute-start | bytes 294920 | tf_op jit(solution)/shard_map/ppermute | solution.py:293
  51.0 0.6 copy-start.3
  51.0 0.7 copy-start.4
  51.1 0.7 copy-start.5
  61.1 0.8 copy-start
  64.8 2.2 %collective-permute-start.6 = (bf16[384,768]{1,0:T(8,128)(2,1)}, bf16[384,768]{1,0:T(8,128)(2,1)S(1)}, u32[]{:S(2)}, u32[]{:S(2)}) collective-permute-start(bf16[384,768]{1,0:T(8,128)(2,1)} %refresh.1.own_ref), channel_id=1, source_target_pairs={{0,1},{1,0},{2,3},{3,2},{4,5},{5,4},{6,7},{7,6},{8,9},{9,8},{10,11... | collective-permute-start | bytes 1769480 | tf_op jit(solution)/shard_map/ppermute | solution.py:374
  67.1 0.8 copy-start.1

commit v4 on v2

--- a/solution.py
+++ b/solution.py
@@ -20,6 +20,7 @@
 BACK = 2 * D + 128
 F32 = jnp.float32
 BF16 = jnp.bfloat16
+PARAMS = pltpu.CompilerParams(vmem_limit_bytes=24 * 1024 * 1024)
 
 
 def vmem_spec():
@@ -114,25 +115,33 @@
     return hits.astype(BF16)
 
 
-def old_slot(step, slot_ref):
-    return step + (step >= slot_ref[0]).astype(jnp.int32)
-
-
-def positive_kernel(slot_ref, flag_ref, plane_ref, lab_ref, out_ref):
-    step = pl.program_id(0)
-
-    @pl.when(step == 0)
-    def _():
-        out_ref[...] = jnp.zeros_like(out_ref)
-
-    slot = old_slot(step, slot_ref)
-    for part in range(6):
-        tile = slot * 6 + part
+def positive_kernel(slot_ref, flag_ref, plane_ref, lab_ref, out_ref, lab_buf, sems):
+    out_ref[...] = jnp.zeros_like(out_ref)
+
+    def copy_of(i, part):
+        tile = (i + (i >= slot_ref[0]).astype(jnp.int32)) * 6 + part
+        at = i * 6 + part
+        return tile, pltpu.make_async_copy(
+            lab_ref.at[pl.ds(tile * 128, 128), :], lab_buf.at[at], sems.at[at]
+        )
+
+    for i in range(OLD):
+        for part in range(6):
+            tile, copy = copy_of(i, part)
+            pl.when(flag_ref[0, tile] > 0)(copy.start)
+
+    def body(at, carry):
+        i = at // 6
+        tile, copy = copy_of(i, at - i * 6)
 
         @pl.when(flag_ref[0, tile] > 0)
         def _():
-            rows = lab_ref[part * 128 : (part + 1) * 128, :]
-            out_ref[...] += dot(hits_of(plane_ref, tile * 128), rows)
+            copy.wait()
+            out_ref[...] += dot(hits_of(plane_ref, tile * 128), lab_buf[at])
+
+        return carry
+
+    lax.fori_loop(0, OLD * 6, body, 0)
 
 
 def refresh_kernel(key_ref, got_ref, free_ref, pos_ref, out_ref):
@@ -165,68 +174,53 @@
 
 def score_kernel(
     slot_ref, flag_ref, got_ref, own_ref, other_ref, lab_ref, plane_ref, pos_ref, out_ref,
-    q_buf, lab_buf, plane_buf, pos_buf, sems,
+    own_buf, lab_buf, pos_buf, sems,
 ):
     rep = lax.axis_index("rep")
     slot = slot_ref[0]
-
-    def rows_at(first, size):
-        return lab_buf.at[pl.ds(first, size), :]
-
-    query_copy = pltpu.make_async_copy(got_ref.at[:, :, pl.ds(ROWS, D)], q_buf, sems.at[SLOTS])
-    query_copy.start()
-    lab_copies = []
+    own_copy = pltpu.make_async_copy(own_ref, own_buf, sems.at[OLD])
+    own_copy.start()
+    copies = []
     for i in range(OLD):
         source = (i + (i >= slot).astype(jnp.int32)) * D
-        lab_copies.append(
-            pltpu.make_async_copy(lab_ref.at[pl.ds(source, D), :], rows_at(i * D, D), sems.at[i])
+        copies.append(
+            pltpu.make_async_copy(lab_ref.at[pl.ds(source, D), :], lab_buf.at[i], sems.at[i])
         )
-        lab_copies[-1].start()
-    own_copy = pltpu.make_async_copy(
-        own_ref, rows_at(OLD * D + rep * HALF, HALF), sems.at[OLD]
-    )
-    other_copy = pltpu.make_async_copy(
-        other_ref, rows_at(OLD * D + (1 - rep) * HALF, HALF), sems.at[SLOTS + 1]
-    )
-    plane_copy = pltpu.make_async_copy(plane_ref, plane_buf, sems.at[SLOTS + 2])
-    pos_copy = pltpu.make_async_copy(pos_ref, pos_buf, sems.at[SLOTS + 3])
-    for copy in (own_copy, other_copy, plane_copy, pos_copy):
-        copy.start()
-    query_copy.wait()
-    queries = q_buf[...].reshape(QG, D)
+        copies[-1].start()
+    queries = got_ref[..., ROWS:].reshape(QG, D)
+    blocks = [other_ref, own_buf] + [lab_buf.at[i] for i in range(OLD)]
 
     def logits_of(i):
-        if i < OLD:
-            lab_copies[i].wait()
-        else:
+        if i == 1:
             own_copy.wait()
-            other_copy.wait()
-        return dot_last(queries, lab_buf[i * D : (i + 1) * D, :])
+        elif i > 1:
+            copies[i - 2].wait()
+        return dot_last(queries, blocks[i][...])
 
     peak = jnp.full((QG, 1), -jnp.inf, F32)
     total = jnp.zeros((QG, 128), F32)
     grads = jnp.zeros((QG, D), F32)
     following = logits_of(0)
-    for i in range(SLOTS):
+    for i, block in enumerate(blocks):
         logits = following
-        if i + 1 < SLOTS:
+        if i + 1 < len(blocks):
             following = logits_of(i + 1)
         higher = jnp.maximum(peak, jnp.max(over_lanes(jnp.maximum, logits), axis=1, keepdims=True))
         scale = jnp.exp(peak - higher)
         weight = jnp.exp(logits - higher)
         total = total * scale + over_lanes(jnp.add, weight)
-        grads = grads * scale + dot(weight.astype(BF16), lab_buf[i * D : (i + 1) * D, :])
+        grads = grads * scale + dot(weight.astype(BF16), block[...])
         peak = higher
     out_ref[..., :D] = grads.astype(BF16).reshape(N_CLS, 2, D)
-    plane_copy.wait()
-    pos_copy.wait()
-    for part in range(6):
-        tile = slot * 6 + part
-
-        @pl.when(flag_ref[0, tile] > 0)
-        def _():
-            rows = lab_buf[OLD * D + part * 128 : OLD * D + (part + 1) * 128, :]
-            pos_buf[...] += dot(hits_of(plane_buf, tile * 128), rows)
+    pos_buf[...] = pos_ref[...]
+    for block, half in ((own_buf, rep), (other_ref, 1 - rep)):
+        for part in range(3):
+            tile = slot * 6 + half * 3 + part
+
+            @pl.when(flag_ref[0, tile] > 0)
+            def _():
+                rows = block[part * 128 : (part + 1) * 128, :]
+                pos_buf[...] += dot(hits_of(plane_ref, tile * 128), rows)
 
     positive = pos_buf[...]
     out_ref[..., D : 2 * D] = positive.astype(BF16).reshape(N_CLS, 2, D)
@@ -267,6 +261,10 @@
     grad_ref[...] = jnp.concatenate(grads, axis=0).astype(BF16).reshape(1, 2, D)
 
 
+def in_hbm(value):
+    return pltpu.with_memory_space_constraint(value, pltpu.HBM)
+
+
 def per_device(
     queries,
     positives,
@@ -279,6 +277,7 @@
     targets,
 ):
     target_rows = targets.reshape(768, 128)
+    label_vectors = in_hbm(label_vectors)
     slot = refresh_slot.reshape(1)
     ids = positives.transpose(0, 2, 1)
 
@@ -287,6 +286,7 @@
         out_shape=jax.ShapeDtypeStruct((N_CLS, 2, SEND), BF16),
         in_specs=[vmem_spec()] * 5,
         out_specs=vmem_spec(),
+        compiler_params=PARAMS,
         name="encode",
     )(features, encoder_weight, encoder_gain.reshape(6, 128), target_rows, queries)
     keys, planes, flags = pl.pallas_call(
@@ -298,64 +298,57 @@
         ],
         in_specs=[vmem_spec()] * 2,
         out_specs=[vmem_spec()] * 3,
+        compiler_params=PARAMS,
         name="place",
     )(target_rows, ids)
     got = lax.all_to_all(sending, CLS, 0, 0, tiled=True)
 
-    def all_of(shape):
-        return pl.BlockSpec(shape, lambda *args: (0,) * len(shape))
-
+    any_spec = pl.BlockSpec(memory_space=pl.ANY)
     positive_old = pl.pallas_call(
         positive_kernel,
         out_shape=jax.ShapeDtypeStruct((QG, D), F32),
-        grid_spec=pltpu.PrefetchScalarGridSpec(
-            num_scalar_prefetch=2,
-            grid=(OLD,),
-            in_specs=[
-                all_of((4, QG, 128)),
-                pl.BlockSpec((D, D), lambda step, slot_ref, flag_ref: (old_slot(step, slot_ref), 0)),
-            ],
-            out_specs=all_of((QG, D)),
-        ),
+        in_specs=[smem_spec()] * 2 + [vmem_spec(), any_spec],
+        out_specs=vmem_spec(),
+        scratch_shapes=[
+            pltpu.VMEM((OLD * 6, 128, D), BF16),
+            pltpu.SemaphoreType.DMA((OLD * 6,)),
+        ],
+        compiler_params=PARAMS,
         name="positive",
     )(slot, flags, planes, label_vectors)
 
     refreshed = pl.pallas_call(
         refresh_kernel,
         out_shape=jax.ShapeDtypeStruct((HALF, D), BF16),
-        grid=(1,),
-        in_specs=[
-            all_of((8, QG)),
-            pl.BlockSpec((N_CLS, 2, ROWS), lambda step: (0, 0, 0)),
-            all_of((HALF, D)),
-            pl.BlockSpec(memory_space=pl.ANY),
-        ],
-        out_specs=all_of((HALF, D)),
+        in_specs=[vmem_spec()] * 3 + [any_spec],
+        out_specs=vmem_spec(),
+        compiler_params=PARAMS,
         name="refresh",
     )(keys, got, free_vectors, positive_old)
     partner = lax.ppermute(refreshed, "rep", [(0, 1), (1, 0)])
 
-    any_spec = pl.BlockSpec(memory_space=pl.ANY)
     leaving = pl.pallas_call(
         score_kernel,
         out_shape=jax.ShapeDtypeStruct((N_CLS, 2, BACK), BF16),
-        in_specs=[smem_spec(), smem_spec()] + [any_spec] * 6,
+        in_specs=[smem_spec()] * 2
+        + [vmem_spec(), any_spec, vmem_spec(), any_spec, vmem_spec(), vmem_spec()],
         out_specs=vmem_spec(),
         scratch_shapes=[
-            pltpu.VMEM((N_CLS, 2, D), BF16),
-            pltpu.VMEM((SLOTS * D, D), BF16),
-            pltpu.VMEM((4, QG, 128), F32),
+            pltpu.VMEM((HALF, D), BF16),
+            pltpu.VMEM((OLD, D, D), BF16),
             pltpu.VMEM((QG, D), F32),
-            pltpu.SemaphoreType.DMA((SLOTS + 4,)),
+            pltpu.SemaphoreType.DMA((SLOTS,)),
         ],
+        compiler_params=PARAMS,
         name="score",
-    )(slot, flags, got, refreshed, partner, label_vectors, planes, positive_old)
+    )(slot, flags, got, in_hbm(refreshed), partner, label_vectors, planes, positive_old)
     back = lax.all_to_all(leaving, CLS, 0, 0, tiled=True)
     loss, grads = pl.pallas_call(
         finish_kernel,
         out_shape=[jax.ShapeDtypeStruct((1, 2), F32), jax.ShapeDtypeStruct((1, 2, D), BF16)],
         in_specs=[vmem_spec()] * 2,
         out_specs=[vmem_spec()] * 2,
+        compiler_params=PARAMS,
         name="finish",
     )(ids, back)
     return loss, grads, refreshed

time: 104 us -> 101 us (0.971)
  Pallas kernels: 30.8 us -> 20.8 us
  local copies, waits for them, and re-layouts: 1.77 us -> 6.39 us
  waiting for transfers between devices: 21 us -> 23.7 us
    unnamed x4 -> x18, local copies, waits for them, and re-layouts: 1.77 us -> 6.39 us
    all_to_all x1, waiting for transfers between devices: 18.7 us -> 21.5 us  [per_device(): got = lax.all_to_all(sending, CLS, 0, 0, tiled=True)]
    pallas_call x1, Pallas kernels: 7.13 us -> 4.47 us  [per_device(): pl.pallas_call(positive_kernel, out_shape=jax.ShapeDtypeStruct((QG, D), F...]
    pallas_call x1, Pallas kernels: 2.26 us -> 0.46 us  [per_device(): pl.pallas_call(place_kernel, out_shape=[jax.ShapeDtypeStruct((8, QG), F32...]
    pallas_call x1, Pallas kernels: 4.45 us -> 2.89 us  [per_device(): pl.pallas_call(encode_kernel, out_shape=jax.ShapeDtypeStruct((N_CLS, 2, S...]
    pallas_call x1, Pallas kernels: 10.9 us -> 9.37 us  [per_device(): pl.pallas_call(score_kernel, out_shape=jax.ShapeDtypeStruct((N_CLS, 2, BA...]
    pallas_call x1, Pallas kernels: 2.88 us -> 1.62 us  [per_device(): pl.pallas_call(refresh_kernel, out_shape=jax.ShapeDtypeStruct((HALF, D),...]
    pallas_call x1, Pallas kernels: 3.2 us -> 2.03 us  [per_device(): pl.pallas_call(finish_kernel, out_shape=[jax.ShapeDtypeStruct((1, 2), F32...]
  transfers between devices with their start and end apart: 2 -> 2, of which waited for: 2 -> 2; matrix products, arithmetic and copies ran while one was open for 0% -> 0% of each run, Pallas kernels for 9% -> 5%
where the time goes in v4:
time: 101 us
  blocking collectives  33.7 us (33%)
  waiting for transfers between devices  23.7 us (23%)
  Pallas kernels  20.8 us (21%)
  starting transfers between devices  15 us (15%)
  local copies, waits for them, and re-layouts  6.39 us (6%)
  between operations  1.34 us (1%)
    all_to_all x1, blocking collectives, per_device(): back = lax.all_to_all(leaving, CLS, 0, 0, tiled=True)  33.7 us
    all_to_all x1, waiting for transfers between devices, per_device(): got = lax.all_to_all(sending, CLS, 0, 0, tiled=True)  21.5 us
    all_to_all x1, starting transfers between devices, per_device(): got = lax.all_to_all(sending, CLS, 0, 0, tiled=True)  15 us
    pallas_call x1, Pallas kernels, per_device(): pl.pallas_call(score_kernel, out_shape=jax.ShapeDtypeStruct((N_CLS, 2, BA...  9.37 us
    unnamed x18, local copies, waits for them, and re-layouts  6.39 us
    pallas_call x1, Pallas kernels, per_device(): pl.pallas_call(positive_kernel, out_shape=jax.ShapeDtypeStruct((QG, D), F...  4.47 us
    pallas_call x1, Pallas kernels, per_device(): pl.pallas_call(encode_kernel, out_shape=jax.ShapeDtypeStruct((N_CLS, 2, S...  2.89 us
    ppermute x1, waiting for transfers between devices, per_device(): partner = lax.ppermute(refreshed, 'rep', [(0, 1), (1, 0)])  2.21 us
  transfers between devices with their start and end apart: 2, of which 2 were waited for; matrix products, arithmetic and copies ran while one was open for 0% of the time, Pallas kernels for 5%

profile of v4, /device:TPU:32, one launch (start us, length us, event | category | flops | bytes accessed | tf_op | source)
XLA Modules:
  0.0 101.0 jit_solution(13508274239008220582)
XLA Ops:
  0.6 0.0 copy-start
  0.6 1.0 copy-done
  1.6 0.0 copy-start.2
  1.6 1.3 %copy-done.2 = bf16[768,768]{1,0:T(8,128)(2,1)S(1)} copy-done((bf16[768,768]{1,0:T(8,128)(2,1)S(1)}, bf16[768,768]{1,0:T(8,128)(2,1)}, u32[]{:S(2)}) %copy-start.2) | copy-done | bytes 1179672
  2.9 0.0 copy-start.3
  2.9 1.1 %copy-done.3 = bf16[384,768]{1,0:T(8,128)(2,1)S(1)} copy-done((bf16[384,768]{1,0:T(8,128)(2,1)S(1)}, bf16[384,768]{1,0:T(8,128)(2,1)}, u32[]{:S(2)}) %copy-start.3) | copy-done | bytes 589848
  4.0 0.0 copy-start.7
  4.0 0.7 copy-done.7
  4.7 0.0 copy-start.8
  4.7 0.7 copy-done.8
  5.3 0.0 copy-start.4
  5.3 2.9 %encode.1 = bf16[128,2,1920]{2,1,0:T(2,128)(2,1)} custom-call(bf16[384,768]{1,0:T(8,128)(2,1)S(1)} %copy-done.3, bf16[768,768]{1,0:T(8,128)(2,1)S(1)} %copy-done.2, f32[6,128]{1,0:T(8,128)S(1)} %bitcast.10, s32[768,128]{1,0:T(8,128)S(1)} %bitcast.6, bf16[1,2,768]{2,1,0:T(2,128)(2,1)S(1)} %copy-done.8), custom_call_target="tpu_custom_call" | custom-call | tf_op jit(solution)/shard_map/encode/pallas_call | solution.py:284
  8.2 15.0 %all-to-all-start = ((bf16[128,2,1920]{2,1,0:T(2,128)(2,1)}), bf16[128,2,1920]{2,1,0:T(2,128)(2,1)S(1)}, u32[]{:S(2)}, u32[]{:S(2)}) async-start(bf16[128,2,1920]{2,1,0:T(2,128)(2,1)} %encode.1), calls=%async_computation | async-start | bytes 1966080 | tf_op jit(solution)/shard_map/all_to_all | solution.py:304
  23.9 0.0 copy-start.1
  23.9 1.0 copy-done.1
  24.9 0.0 copy-start.5
  24.9 0.7 copy-done.5
  25.6 0.5 place.1
  26.1 4.5 %positive.1.pos_ref = f32[256,768]{1,0:T(8,128)S(1)} custom-call(s32[1]{0:T(128)} %bitcast.4.slot_ref, s32[1,128]{1,0:T(1,128)S(1)} %get-tuple-element.8.flag_ref, f32[4,256,128]{2,1,0:T(8,128)S(1)} %get-tuple-element.10.plane_ref, bf16[6144,768]{1,0:T(8,128)(2,1)} %lab_ref.3), custom_call_target="tpu_custom_call" | custom-call | tf_op jit(solution)/shard_map/positive/pallas_call | solution.py:307
  30.5 0.0 copy-start.6
  30.5 21.5 %all-to-all-done.got_ref = bf16[128,2,1920]{2,1,0:T(2,128)(2,1)S(1)} async-done(((bf16[128,2,1920]{2,1,0:T(2,128)(2,1)}), bf16[128,2,1920]{2,1,0:T(2,128)(2,1)S(1)}, u32[]{:S(2)}, u32[]{:S(2)}) %all-to-all-start) | async-done | bytes 983072 | tf_op jit(solution)/shard_map/all_to_all | solution.py:304
  52.0 0.0 copy-done.4
  52.0 1.6 %refresh.1.own_ref = bf16[384,768]{1,0:T(8,128)(2,1)} custom-call(f32[8,256]{1,0:T(8,128)S(1)} %get-tuple-element.9.key_ref, bf16[128,2,1920]{2,1,0:T(2,128)(2,1)S(1)} %all-to-all-done.got_ref, bf16[384,768]{1,0:T(8,128)(2,1)S(1)} %copy-done.4, f32[256,768]{1,0:T(8,128)S(1)} %positive.1.pos_ref), custom_call_target="tpu_custom_call" | custom-call | tf_op jit(solution)/shard_map/refresh/pallas_call | solution.py:320
  53.7 0.0 collective-permute-start
  53.7 2.2 %collective-permute-done.other_ref = bf16[384,768]{1,0:T(8,128)(2,1)S(1)} collective-permute-done((bf16[384,768]{1,0:T(8,128)(2,1)}, bf16[384,768]{1,0:T(8,128)(2,1)S(1)}, u32[]{:S(2)}, u32[]{:S(2)}) %collective-permute-start) | collective-permute-done | bytes 589856 | tf_op jit(solution)/shard_map/ppermute | solution.py:328
  55.9 9.4 %score.1 = bf16[128,2,1664]{2,1,0:T(2,128)(2,1)S(1)} custom-call(s32[1]{0:T(128)} %bitcast.5.slot_ref, s32[1,128]{1,0:T(1,128)S(1)} %get-tuple-element.8.flag_ref, bf16[128,2,1920]{2,1,0:T(2,128)(2,1)S(1)} %all-to-all-done.got_ref, bf16[384,768]{1,0:T(8,128)(2,1)} %refresh.1.own_ref, bf16[384,768]{1,0:T(8,128)(2,1)S(1)} %collective-permute-done.other_ref, ...), custom_call_target="tpu_custom_call" | custom-call | tf_op jit(solution)/shard_map/score/pallas_call | solution.py:330
  65.2 33.7 %all_to_all.10.back_ref = bf16[128,2,1664]{2,1,0:T(2,128)(2,1)S(1)} all-to-all(bf16[128,2,1664]{2,1,0:T(2,128)(2,1)S(1)} %score.1), channel_id=1, replica_groups=mesh['cls_0'=4,'cls_1'=8,'cls_2'=4,'rep'=2] {'cls_0','cls_1','cls_2'}, dimensions={0} | all-to-all | bytes 1703936 | tf_op jit(solution)/shard_map/all_to_all | solution.py:345
  98.9 0.0 copy-done.6
  98.9 2.0 %finish.1 = (f32[1,2]{1,0:T(1,128)}, bf16[1,2,768]{2,1,0:T(2,128)(2,1)}) custom-call(s32[2,4,256]{2,1,0:T(4,128)S(1)} %bitcast.9, bf16[128,2,1664]{2,1,0:T(2,128)(2,1)S(1)} %all_to_all.10.back_ref), custom_call_target="tpu_custom_call" | custom-call | tf_op jit(solution)/shard_map/finish/pallas_call | solution.py:346
Async XLA Ops:
  0.6 1.0 copy-start
  1.6 1.3 %copy-start.2 = (bf16[768,768]{1,0:T(8,128)(2,1)S(1)}, bf16[768,768]{1,0:T(8,128)(2,1)}, u32[]{:S(2)}) copy-start(bf16[768,768]{1,0:T(8,128)(2,1)} %weight_ref.1) | copy-start | bytes 3538948
  2.9 1.1 %copy-start.3 = (bf16[384,768]{1,0:T(8,128)(2,1)S(1)}, bf16[384,768]{1,0:T(8,128)(2,1)}, u32[]{:S(2)}) copy-start(bf16[384,768]{1,0:T(8,128)(2,1)} %feat_ref.1) | copy-start | bytes 1769476
  4.0 0.7 copy-start.7
  4.7 0.7 copy-start.8
  5.3 46.7 %copy-start.4 = (bf16[384,768]{1,0:T(8,128)(2,1)S(1)}, bf16[384,768]{1,0:T(8,128)(2,1)}, u32[]{:S(2)}) copy-start(bf16[384,768]{1,0:T(8,128)(2,1)} %free_ref.1) | copy-start | bytes 1769476
  8.2 43.8 %all-to-all-start = ((bf16[128,2,1920]{2,1,0:T(2,128)(2,1)}), bf16[128,2,1920]{2,1,0:T(2,128)(2,1)S(1)}, u32[]{:S(2)}, u32[]{:S(2)}) async-start(bf16[128,2,1920]{2,1,0:T(2,128)(2,1)} %encode.1), calls=%async_computation | async-start | bytes 1966080 | tf_op jit(solution)/shard_map/all_to_all | solution.py:304
  23.9 1.0 copy-start.1
  24.9 0.7 copy-start.5
  30.5 68.4 %copy-start.6 = (s32[2,256,4]{1,2,0:T(4,128)S(1)}, s32[2,256,4]{1,2,0:T(4,128)}, u32[]{:S(2)}) copy-start(s32[2,256,4]{1,2,0:T(4,128)} %param.10) | copy-start | bytes 24580
  53.7 2.2 %collective-permute-start = (bf16[384,768]{1,0:T(8,128)(2,1)}, bf16[384,768]{1,0:T(8,128)(2,1)S(1)}, u32[]{:S(2)}, u32[]{:S(2)}) collective-permute-start(bf16[384,768]{1,0:T(8,128)(2,1)} %refresh.1.own_ref), channel_id=1, source_target_pairs={{0,1},{1,0},{2,3},{3,2},{4,5},{5,4},{6,7},{7,6},{8,9},{9,8},{10,11... | collective-permute-start | bytes 1769480 | tf_op jit(solution)/shard_map/ppermute | solution.py:328

commit v5 on v4

--- a/solution.py
+++ b/solution.py
@@ -55,13 +55,21 @@
     return jnp.broadcast_to(row, (128, 128)).T
 
 
-def encode_kernel(feat_ref, weight_ref, gain_ref, tgt_ref, q_ref, out_ref):
-    block = lax.axis_index(CLS_REP)
-    hidden = dot(feat_ref[...], weight_ref[...])
-    mean = jnp.mean(hidden * hidden, axis=1, keepdims=True)
-    gain = jnp.concatenate([gain_ref[i : i + 1, :] for i in range(6)], axis=1)
-    encoded = (hidden * lax.rsqrt(mean + 1e-06) * gain).astype(BF16)
-    rows = [tgt_ref[pl.ds(3 * block + a, 1), :].astype(F32) for a in range(3)]
+def encode_kernel(
+    feat_ref, weight_ref, gain_ref, tgt_ref, q_ref, out_ref,
+    feat_buf, weight_buf, gain_buf, tgt_buf, q_buf, sems,
+):
+    row = 3 * lax.axis_index(CLS_REP)
+    begin = pl.multiple_of(jnp.minimum(row // 8 * 8, 768 - 16), 8)
+    pairs = [
+        (tgt_ref.at[pl.ds(begin, 16), :], tgt_buf), (q_ref, q_buf), (weight_ref, weight_buf),
+        (feat_ref, feat_buf), (gain_ref, gain_buf),
+    ]
+    copies = [pltpu.make_async_copy(a, b, sems.at[i]) for i, (a, b) in enumerate(pairs)]
+    for copy in copies:
+        copy.start()
+    copies[0].wait()
+    rows = [tgt_buf[pl.ds(row - begin + a, 1), :].astype(F32) for a in range(3)]
     columns = [spread_down(row) for row in rows]
     ranks = []
     for row in rows:
@@ -73,12 +81,21 @@
     line = iota((QG, HALF), 0)
     first = ((line >> 1) * PER).astype(F32)
     odd = (line & 1) == 1
+    chosen = []
     for k in range(PER):
         hit = rank == first + float(k)
-        total = dot(one_hot(hit & ~odd), encoded[:, :HALF])
-        total += dot(one_hot(hit & odd), encoded[:, HALF:])
+        chosen.append((one_hot(hit & ~odd), one_hot(hit & odd)))
+    copies[1].wait()
+    out_ref[..., ROWS:] = jnp.broadcast_to(q_buf[...], (N_CLS, 2, D))
+    for copy in copies[2:]:
+        copy.wait()
+    hidden = dot(feat_buf[...], weight_buf[...])
+    mean = jnp.mean(hidden * hidden, axis=1, keepdims=True)
+    gain = jnp.concatenate([gain_buf[i : i + 1, :] for i in range(6)], axis=1)
+    encoded = (hidden * lax.rsqrt(mean + 1e-06) * gain).astype(BF16)
+    for k, (even_rows, odd_rows) in enumerate(chosen):
+        total = dot(even_rows, encoded[:, :HALF]) + dot(odd_rows, encoded[:, HALF:])
         out_ref[..., k * HALF : (k + 1) * HALF] = total.astype(BF16).reshape(N_CLS, 2, HALF)
-    out_ref[..., ROWS:] = jnp.broadcast_to(q_ref[...], (N_CLS, 2, D))
 
 
 def place_kernel(tgt_ref, ids_ref, key_ref, plane_ref, flag_ref):
@@ -172,34 +189,14 @@
     return total
 
 
-def score_kernel(
-    slot_ref, flag_ref, got_ref, own_ref, other_ref, lab_ref, plane_ref, pos_ref, out_ref,
-    own_buf, lab_buf, pos_buf, sems,
-):
-    rep = lax.axis_index("rep")
-    slot = slot_ref[0]
-    own_copy = pltpu.make_async_copy(own_ref, own_buf, sems.at[OLD])
-    own_copy.start()
-    copies = []
-    for i in range(OLD):
-        source = (i + (i >= slot).astype(jnp.int32)) * D
-        copies.append(
-            pltpu.make_async_copy(lab_ref.at[pl.ds(source, D), :], lab_buf.at[i], sems.at[i])
-        )
-        copies[-1].start()
-    queries = got_ref[..., ROWS:].reshape(QG, D)
-    blocks = [other_ref, own_buf] + [lab_buf.at[i] for i in range(OLD)]
+def absorb_all(state, queries, blocks, waits):
+    peak, total, grads = state
 
     def logits_of(i):
-        if i == 1:
-            own_copy.wait()
-        elif i > 1:
-            copies[i - 2].wait()
+        for copy in waits[i]:
+            copy.wait()
         return dot_last(queries, blocks[i][...])
 
-    peak = jnp.full((QG, 1), -jnp.inf, F32)
-    total = jnp.zeros((QG, 128), F32)
-    grads = jnp.zeros((QG, D), F32)
     following = logits_of(0)
     for i, block in enumerate(blocks):
         logits = following
@@ -211,8 +208,48 @@
         total = total * scale + over_lanes(jnp.add, weight)
         grads = grads * scale + dot(weight.astype(BF16), block[...])
         peak = higher
+    return peak, total, grads
+
+
+def old_kernel(
+    slot_ref, got_ref, own_ref, lab_ref, peak_ref, total_ref, grad_ref, own_buf, lab_buf, sems
+):
+    slot = slot_ref[0]
+    own_copy = pltpu.make_async_copy(own_ref, own_buf, sems.at[OLD])
+    own_copy.start()
+    copies = []
+    for i in range(OLD):
+        source = (i + (i >= slot).astype(jnp.int32)) * D
+        copies.append(
+            pltpu.make_async_copy(lab_ref.at[pl.ds(source, D), :], lab_buf.at[i], sems.at[i])
+        )
+        copies[-1].start()
+    start = (jnp.full((QG, 1), -jnp.inf, F32), jnp.zeros((QG, 128), F32), jnp.zeros((QG, D), F32))
+    peak, total, grads = absorb_all(
+        start,
+        got_ref[..., ROWS:].reshape(QG, D),
+        [own_buf] + [lab_buf.at[i] for i in range(OLD)],
+        [[own_copy]] + [[copy] for copy in copies],
+    )
+    peak_ref[...] = jnp.broadcast_to(peak, (QG, 128))
+    total_ref[...] = total
+    grad_ref[...] = grads
+
+
+def score_kernel(
+    slot_ref, flag_ref, got_ref, own_ref, other_ref, peak_ref, total_ref, grad_ref, plane_ref,
+    pos_ref, out_ref, own_buf, pos_buf, sem,
+):
+    rep = lax.axis_index("rep")
+    slot = slot_ref[0]
+    own_copy = pltpu.make_async_copy(own_ref, own_buf, sem)
+    own_copy.start()
+    queries = got_ref[..., ROWS:].reshape(QG, D)
+    state = (peak_ref[:, :1], total_ref[...], grad_ref[...])
+    peak, total, grads = absorb_all(state, queries, [other_ref], [[]])
     out_ref[..., :D] = grads.astype(BF16).reshape(N_CLS, 2, D)
     pos_buf[...] = pos_ref[...]
+    own_copy.wait()
     for block, half in ((own_buf, rep), (other_ref, 1 - rep)):
         for part in range(3):
             tile = slot * 6 + half * 3 + part
@@ -281,14 +318,29 @@
     slot = refresh_slot.reshape(1)
     ids = positives.transpose(0, 2, 1)
 
+    any_spec = pl.BlockSpec(memory_space=pl.ANY)
     sending = pl.pallas_call(
         encode_kernel,
         out_shape=jax.ShapeDtypeStruct((N_CLS, 2, SEND), BF16),
-        in_specs=[vmem_spec()] * 5,
+        in_specs=[any_spec] * 5,
         out_specs=vmem_spec(),
+        scratch_shapes=[
+            pltpu.VMEM((HALF, D), BF16),
+            pltpu.VMEM((D, D), BF16),
+            pltpu.VMEM((6, 128), F32),
+            pltpu.VMEM((16, 128), jnp.int32),
+            pltpu.VMEM((1, 2, D), BF16),
+            pltpu.SemaphoreType.DMA((5,)),
+        ],
         compiler_params=PARAMS,
         name="encode",
-    )(features, encoder_weight, encoder_gain.reshape(6, 128), target_rows, queries)
+    )(
+        in_hbm(features),
+        in_hbm(encoder_weight),
+        in_hbm(encoder_gain.reshape(6, 128)),
+        in_hbm(target_rows),
+        in_hbm(queries),
+    )
     keys, planes, flags = pl.pallas_call(
         place_kernel,
         out_shape=[
@@ -303,7 +355,6 @@
     )(target_rows, ids)
     got = lax.all_to_all(sending, CLS, 0, 0, tiled=True)
 
-    any_spec = pl.BlockSpec(memory_space=pl.ANY)
     positive_old = pl.pallas_call(
         positive_kernel,
         out_shape=jax.ShapeDtypeStruct((QG, D), F32),
@@ -327,21 +378,38 @@
     )(keys, got, free_vectors, positive_old)
     partner = lax.ppermute(refreshed, "rep", [(0, 1), (1, 0)])
 
+    own = in_hbm(refreshed)
+    state = pl.pallas_call(
+        old_kernel,
+        out_shape=[
+            jax.ShapeDtypeStruct((QG, 128), F32),
+            jax.ShapeDtypeStruct((QG, 128), F32),
+            jax.ShapeDtypeStruct((QG, D), F32),
+        ],
+        in_specs=[smem_spec(), vmem_spec(), any_spec, any_spec],
+        out_specs=[vmem_spec()] * 3,
+        scratch_shapes=[
+            pltpu.VMEM((HALF, D), BF16),
+            pltpu.VMEM((OLD, D, D), BF16),
+            pltpu.SemaphoreType.DMA((SLOTS,)),
+        ],
+        compiler_params=PARAMS,
+        name="old",
+    )(slot, got, own, label_vectors)
+    partner, *state = lax.optimization_barrier((partner, *state))
     leaving = pl.pallas_call(
         score_kernel,
         out_shape=jax.ShapeDtypeStruct((N_CLS, 2, BACK), BF16),
-        in_specs=[smem_spec()] * 2
-        + [vmem_spec(), any_spec, vmem_spec(), any_spec, vmem_spec(), vmem_spec()],
+        in_specs=[smem_spec()] * 2 + [vmem_spec(), any_spec] + [vmem_spec()] * 6,
         out_specs=vmem_spec(),
         scratch_shapes=[
             pltpu.VMEM((HALF, D), BF16),
-            pltpu.VMEM((OLD, D, D), BF16),
             pltpu.VMEM((QG, D), F32),
-            pltpu.SemaphoreType.DMA((SLOTS,)),
+            pltpu.SemaphoreType.DMA,
         ],
         compiler_params=PARAMS,
         name="score",
-    )(slot, flags, got, in_hbm(refreshed), partner, label_vectors, planes, positive_old)
+    )(slot, flags, got, own, partner, *state, planes, positive_old)
     back = lax.all_to_all(leaving, CLS, 0, 0, tiled=True)
     loss, grads = pl.pallas_call(
         finish_kernel,

time: 101 us -> 96.7 us (0.957)
  local copies, waits for them, and re-layouts: 6.39 us -> 1.7 us
  Pallas kernels: 20.8 us -> 22.4 us
  waiting for transfers between devices: 23.7 us -> 22.5 us
    pallas_call x0 -> x1, Pallas kernels: none -> 7.86 us  [per_device(): pl.pallas_call(old_kernel, out_shape=[jax.ShapeDtypeStruct((QG, 128), F32...]
    pallas_call x1, Pallas kernels: 9.37 us -> 2.47 us  [per_device(): pl.pallas_call(score_kernel, out_shape=jax.ShapeDtypeStruct((N_CLS, 2, BA...]
    unnamed x18 -> x8, local copies, waits for them, and re-layouts: 6.39 us -> 1.7 us
    ppermute x1, waiting for transfers between devices: 2.21 us -> 0.01 us  [per_device(): partner = lax.ppermute(refreshed, 'rep', [(0, 1), (1, 0)])]
    pallas_call x1, Pallas kernels: 2.89 us -> 4.43 us  [per_device(): pl.pallas_call(encode_kernel, out_shape=jax.ShapeDtypeStruct((N_CLS, 2, S...]
  transfers between devices with their start and end apart: 2 -> 2, of which waited for: 2 -> 1; matrix products, arithmetic and copies ran while one was open for 0% -> 0% of each run, Pallas kernels for 5% -> 12%
where the time goes in v5:
time: 96.7 us; the launch traced here: 96.1 us
  blocking collectives  33.2 us (34%)
  waiting for transfers between devices  22.5 us (23%)
  Pallas kernels  22.4 us (23%)
  starting transfers between devices  15 us (16%)
  local copies, waits for them, and re-layouts  1.7 us (2%)
  between operations  1.35 us (1%)
    all_to_all x1, blocking collectives, per_device(): back = lax.all_to_all(leaving, CLS, 0, 0, tiled=True)  33.2 us
    all_to_all x1, waiting for transfers between devices, per_device(): got = lax.all_to_all(sending, CLS, 0, 0, tiled=True)  22.5 us
    all_to_all x1, starting transfers between devices, per_device(): got = lax.all_to_all(sending, CLS, 0, 0, tiled=True)  15 us
    pallas_call x1, Pallas kernels, per_device(): pl.pallas_call(old_kernel, out_shape=[jax.ShapeDtypeStruct((QG, 128), F32...  7.86 us
    pallas_call x1, Pallas kernels, per_device(): pl.pallas_call(encode_kernel, out_shape=jax.ShapeDtypeStruct((N_CLS, 2, S...  4.43 us
    pallas_call x1, Pallas kernels, per_device(): pl.pallas_call(positive_kernel, out_shape=jax.ShapeDtypeStruct((QG, D), F...  3.52 us
    pallas_call x1, Pallas kernels, per_device(): pl.pallas_call(score_kernel, out_shape=jax.ShapeDtypeStruct((N_CLS, 2, BA...  2.47 us
    pallas_call x1, Pallas kernels, per_device(): pl.pallas_call(finish_kernel, out_shape=[jax.ShapeDtypeStruct((1, 2), F32...  2.03 us
  transfers between devices with their start and end apart: 2, of which 1 were waited for; matrix products, arithmetic and copies ran while one was open for 0% of the time, Pallas kernels for 12%

profile of v5, /device:TPU:32, one launch (start us, length us, event | category | flops | bytes accessed | tf_op | source)
XLA Modules:
  0.0 96.1 jit_solution(6665009764782534842)
XLA Ops:
  0.6 0.0 copy-start.1
  0.6 4.4 %encode.1 = bf16[128,2,1920]{2,1,0:T(2,128)(2,1)} custom-call(bf16[384,768]{1,0:T(8,128)(2,1)} %feat_ref.1, bf16[768,768]{1,0:T(8,128)(2,1)} %weight_ref.1, f32[6,128]{1,0:T(8,128)} %bitcast.11, s32[768,128]{1,0:T(8,128)} %bitcast.7, bf16[1,2,768]{2,1,0:T(2,128)(2,1)} %q_ref.1), custom_call_target="tpu_custom_call" | custom-call | tf_op jit(solution)/shard_map/encode/pallas_call | solution.py:322
  5.1 15.0 %all-to-all-start = ((bf16[128,2,1920]{2,1,0:T(2,128)(2,1)}), bf16[128,2,1920]{2,1,0:T(2,128)(2,1)S(1)}, u32[]{:S(2)}, u32[]{:S(2)}) async-start(bf16[128,2,1920]{2,1,0:T(2,128)(2,1)} %encode.1), calls=%async_computation | async-start | bytes 1966080 | tf_op jit(solution)/shard_map/all_to_all | solution.py:356
  20.8 0.0 copy-start
  20.8 1.0 %copy-done = s32[98304]{0:T(1024)S(1)} copy-done((s32[98304]{0:T(1024)S(1)}, s32[98304]{0:T(1024)}, u32[]{:S(2)}) %copy-start) | copy-done | bytes 393240
  21.7 0.0 copy-start.2
  21.8 0.7 copy-done.2
  22.4 0.5 place.1
  22.9 3.5 %positive.1.pos_ref = f32[256,768]{1,0:T(8,128)S(1)} custom-call(s32[1]{0:T(128)} %bitcast.4.slot_ref, s32[1,128]{1,0:T(1,128)S(1)} %get-tuple-element.15.flag_ref, f32[4,256,128]{2,1,0:T(8,128)S(1)} %get-tuple-element.17.plane_ref, bf16[6144,768]{1,0:T(8,128)(2,1)} %lab_ref.3), custom_call_target="tpu_custom_call" | custom-call | tf_op jit(solution)/shard_map/positive/pallas_call | solution.py:358
  26.4 22.5 %all-to-all-done.got_ref = bf16[128,2,1920]{2,1,0:T(2,128)(2,1)S(1)} async-done(((bf16[128,2,1920]{2,1,0:T(2,128)(2,1)}), bf16[128,2,1920]{2,1,0:T(2,128)(2,1)S(1)}, u32[]{:S(2)}, u32[]{:S(2)}) %all-to-all-start) | async-done | bytes 983072 | tf_op jit(solution)/shard_map/all_to_all | solution.py:356
  48.9 0.0 copy-done.1
  48.9 1.6 %refresh.1.own_ref = bf16[384,768]{1,0:T(8,128)(2,1)} custom-call(f32[8,256]{1,0:T(8,128)S(1)} %get-tuple-element.16.key_ref, bf16[128,2,1920]{2,1,0:T(2,128)(2,1)S(1)} %all-to-all-done.got_ref, bf16[384,768]{1,0:T(8,128)(2,1)S(1)} %copy-done.1, f32[256,768]{1,0:T(8,128)S(1)} %positive.1.pos_ref), custom_call_target="tpu_custom_call" | custom-call | tf_op jit(solution)/shard_map/refresh/pallas_call | solution.py:371
  50.5 0.0 copy-start.3
  50.5 0.0 collective-permute-start
  50.5 7.9 %old.1 = (f32[256,128]{1,0:T(8,128)S(1)}, f32[256,128]{1,0:T(8,128)S(1)}, f32[256,768]{1,0:T(8,128)S(1)}) custom-call(s32[1]{0:T(128)} %bitcast.5.slot_ref, bf16[128,2,1920]{2,1,0:T(2,128)(2,1)S(1)} %all-to-all-done.got_ref, bf16[384,768]{1,0:T(8,128)(2,1)} %refresh.1.own_ref, bf16[6144,768]{1,0:T(8,128)(2,1)} %lab_ref.3), custom_call_target="tpu_custom_call" | custom-call | tf_op jit(solution)/shard_map/old/pallas_call | solution.py:382
  58.4 0.0 collective-permute-done.other_ref
  58.4 2.5 %score.1 = bf16[128,2,1664]{2,1,0:T(2,128)(2,1)S(1)} custom-call(s32[1]{0:T(128)} %bitcast.6.slot_ref, s32[1,128]{1,0:T(1,128)S(1)} %get-tuple-element.15.flag_ref, bf16[128,2,1920]{2,1,0:T(2,128)(2,1)S(1)} %all-to-all-done.got_ref, bf16[384,768]{1,0:T(8,128)(2,1)} %refresh.1.own_ref, bf16[384,768]{1,0:T(8,128)(2,1)S(1)} %collective-permute-done.other_ref, ...), custom_call_target="tpu_custom_call" | custom-call | tf_op jit(solution)/shard_map/score/pallas_call | solution.py:400
  60.9 33.2 %all_to_all.10.back_ref = bf16[128,2,1664]{2,1,0:T(2,128)(2,1)S(1)} all-to-all(bf16[128,2,1664]{2,1,0:T(2,128)(2,1)S(1)} %score.1), channel_id=1, replica_groups=mesh['cls_0'=4,'cls_1'=8,'cls_2'=4,'rep'=2] {'cls_0','cls_1','cls_2'}, dimensions={0} | all-to-all | bytes 1703936 | tf_op jit(solution)/shard_map/all_to_all | solution.py:413
  94.1 0.0 copy-done.3
  94.1 2.0 %finish.1 = (f32[1,2]{1,0:T(1,128)}, bf16[1,2,768]{2,1,0:T(2,128)(2,1)}) custom-call(s32[2,4,256]{2,1,0:T(4,128)S(1)} %bitcast.10, bf16[128,2,1664]{2,1,0:T(2,128)(2,1)S(1)} %all_to_all.10.back_ref), custom_call_target="tpu_custom_call" | custom-call | tf_op jit(solution)/shard_map/finish/pallas_call | solution.py:414
Async XLA Ops:
  0.6 48.3 %copy-start.1 = (bf16[384,768]{1,0:T(8,128)(2,1)S(1)}, bf16[384,768]{1,0:T(8,128)(2,1)}, u32[]{:S(2)}) copy-start(bf16[384,768]{1,0:T(8,128)(2,1)} %free_ref.1) | copy-start | bytes 1769476
  5.1 43.8 %all-to-all-start = ((bf16[128,2,1920]{2,1,0:T(2,128)(2,1)}), bf16[128,2,1920]{2,1,0:T(2,128)(2,1)S(1)}, u32[]{:S(2)}, u32[]{:S(2)}) async-start(bf16[128,2,1920]{2,1,0:T(2,128)(2,1)} %encode.1), calls=%async_computation | async-start | bytes 1966080 | tf_op jit(solution)/shard_map/all_to_all | solution.py:356
  20.8 1.0 %copy-start = (s32[98304]{0:T(1024)S(1)}, s32[98304]{0:T(1024)}, u32[]{:S(2)}) copy-start(s32[98304]{0:T(1024)} %param.17) | copy-start | bytes 1179652
  21.7 0.7 copy-start.2
  50.5 43.6 %copy-start.3 = (s32[2,256,4]{1,2,0:T(4,128)S(1)}, s32[2,256,4]{1,2,0:T(4,128)}, u32[]{:S(2)}) copy-start(s32[2,256,4]{1,2,0:T(4,128)} %param.10) | copy-start | bytes 24580
  50.5 7.9 %collective-permute-start = (bf16[384,768]{1,0:T(8,128)(2,1)}, bf16[384,768]{1,0:T(8,128)(2,1)S(1)}, u32[]{:S(2)}, u32[]{:S(2)}) collective-permute-start(bf16[384,768]{1,0:T(8,128)(2,1)} %refresh.1.own_ref), channel_id=1, source_target_pairs={{0,1},{1,0},{2,3},{3,2},{4,5},{5,4},{6,7},{7,6},{8,9},{9,8},{10,11... | collective-permute-start | bytes 1769480 | tf_op jit(solution)/shard_map/ppermute | solution.py:379

commit v6 on v5

--- a/solution.py
+++ b/solution.py
@@ -17,7 +17,8 @@
 CLS_REP = ("cls_0", "cls_1", "cls_2", "rep")
 ROWS = PER * HALF
 SEND = ROWS + D
-BACK = 2 * D + 128
+QUARTER = 192
+BACK = D + 256
 F32 = jnp.float32
 BF16 = jnp.bfloat16
 PARAMS = pltpu.CompilerParams(vmem_limit_bytes=24 * 1024 * 1024)
@@ -55,12 +56,16 @@
     return jnp.broadcast_to(row, (128, 128)).T
 
 
+def own_target_rows():
+    row = 3 * lax.axis_index(CLS_REP)
+    return row, pl.multiple_of(jnp.minimum(row // 8 * 8, 768 - 16), 8)
+
+
 def encode_kernel(
-    feat_ref, weight_ref, gain_ref, tgt_ref, q_ref, out_ref,
+    feat_ref, weight_ref, gain_ref, tgt_ref, q_ref, out_ref, row_ref,
     feat_buf, weight_buf, gain_buf, tgt_buf, q_buf, sems,
 ):
-    row = 3 * lax.axis_index(CLS_REP)
-    begin = pl.multiple_of(jnp.minimum(row // 8 * 8, 768 - 16), 8)
+    row, begin = own_target_rows()
     pairs = [
         (tgt_ref.at[pl.ds(begin, 16), :], tgt_buf), (q_ref, q_buf), (weight_ref, weight_buf),
         (feat_ref, feat_buf), (gain_ref, gain_buf),
@@ -93,12 +98,13 @@
     mean = jnp.mean(hidden * hidden, axis=1, keepdims=True)
     gain = jnp.concatenate([gain_buf[i : i + 1, :] for i in range(6)], axis=1)
     encoded = (hidden * lax.rsqrt(mean + 1e-06) * gain).astype(BF16)
+    row_ref[...] = encoded
     for k, (even_rows, odd_rows) in enumerate(chosen):
         total = dot(even_rows, encoded[:, :HALF]) + dot(odd_rows, encoded[:, HALF:])
         out_ref[..., k * HALF : (k + 1) * HALF] = total.astype(BF16).reshape(N_CLS, 2, HALF)
 
 
-def place_kernel(tgt_ref, ids_ref, key_ref, plane_ref, flag_ref):
+def place_kernel(tgt_ref, ids_ref, key_ref, plane_ref, flag_ref, across_ref):
     cls_index, rep_index = lax.axis_index(CLS), lax.axis_index("rep")
     base = cls_index * (2 * HALF) + rep_index * HALF
     parts = [tgt_ref[pl.ds(3 * rep_index + a, N_CLS, stride=6), :] for a in range(3)]
@@ -116,20 +122,28 @@
     first = cls_index * (SLOTS * D)
     lane = iota((QG, 128), 1)
     seen = jnp.zeros((QG, 128), F32)
+
+    def plane_of(half, k):
+        own = (ids_ref[half, k : k + 1, :] - first).astype(F32)
+        return jnp.concatenate([spread_down(own[:, :128]), spread_down(own[:, 128:])], axis=0)
+
     for k in range(4):
-        own = (ids_ref[rep_index, k : k + 1, :] - first).astype(F32)
-        plane = jnp.concatenate([spread_down(own[:, :128]), spread_down(own[:, 128:])], axis=0)
+        across_ref[k] = plane_of(1 - rep_index, k)
+        plane = plane_of(rep_index, k)
         plane_ref[k] = plane
         seen = jnp.where((plane.astype(jnp.int32) >> 7) == lane, 1.0, seen)
     flag_ref[...] = jnp.max(seen, axis=0, keepdims=True).astype(jnp.int32)
 
 
-def hits_of(plane_ref, first):
-    label = iota((QG, 128), 1).astype(F32) + first.astype(F32)
+def hits_at(plane_ref, label):
     hits = jnp.zeros((QG, 128), F32)
     for k in range(4):
         hits += jnp.where(plane_ref[k] == label, 1.0, 0.0)
     return hits.astype(BF16)
+
+
+def hits_of(plane_ref, first):
+    return hits_at(plane_ref, iota((QG, 128), 1).astype(F32) + first.astype(F32))
 
 
 def positive_kernel(slot_ref, flag_ref, plane_ref, lab_ref, out_ref, lab_buf, sems):
@@ -161,7 +175,42 @@
     lax.fori_loop(0, OLD * 6, body, 0)
 
 
-def refresh_kernel(key_ref, got_ref, free_ref, pos_ref, out_ref):
+def share_kernel(
+    slot_ref, tgt_ref, free_ref, row_ref, plane_ref, across_ref, here_ref, there_ref, tgt_buf, sem
+):
+    row, begin = own_target_rows()
+    copy = pltpu.make_async_copy(tgt_ref.at[pl.ds(begin, 16), :], tgt_buf, sem)
+    copy.start()
+    slot_first = slot_ref[0] * D
+    free_first = slot_first + lax.axis_index("rep") * HALF
+    copy.wait()
+    labels = []
+    for part in range(3):
+        target = tgt_buf[pl.ds(row - begin + part, 1), :]
+        owner = ((target >> 8) * 21846) >> 16
+        behind = owner - lax.axis_index(CLS)
+        local = behind * (SLOTS * D) + slot_first + (target - owner * D)
+        labels.append(local.astype(F32))
+    for planes, out_ref in ((plane_ref, here_ref), (across_ref, there_ref)):
+        total = jnp.zeros((QG, D), F32)
+        for part in range(3):
+            rows = slice(part * 128, (part + 1) * 128)
+            total += dot(hits_of(planes, free_first + part * 128), free_ref[rows, :])
+            total += dot(hits_at(planes, labels[part]), row_ref[rows, :])
+        out_ref[...] = total.astype(out_ref.dtype)
+
+
+def quarter_kernel(old_ref, here_ref, came_ref, *out_refs):
+    total = (old_ref[...] + here_ref[...] + came_ref[...].astype(F32)).astype(BF16)
+    line, lane = iota((D, 256), 0), iota((D, 256), 1)
+    for shift, out_ref in enumerate(out_refs):
+        first = ((lax.axis_index("cls_2") + shift) & 3) * QUARTER
+        pick = one_hot((line == first + lane) & (lane < QUARTER))
+        out_ref[...] = dot(total, pick).astype(BF16)
+
+
+def refresh_kernel(key_ref, got_ref, free_ref, *refs):
+    out_ref = refs[-1]
     own = iota((HALF, QG), 0).astype(F32)
     odd = (iota((HALF, QG), 1) & 1) == 1
     matches = [key_ref[k : k + 1, :] == own for k in range(PER)]
@@ -238,8 +287,9 @@
 
 def score_kernel(
     slot_ref, flag_ref, got_ref, own_ref, other_ref, peak_ref, total_ref, grad_ref, plane_ref,
-    pos_ref, out_ref, own_buf, pos_buf, sem,
+    pos_ref, *refs
 ):
+    quarter_refs, (out_ref, own_buf, pos_buf, sem) = refs[:4], refs[4:]
     rep = lax.axis_index("rep")
     slot = slot_ref[0]
     own_copy = pltpu.make_async_copy(own_ref, own_buf, sem)
@@ -260,25 +310,27 @@
                 pos_buf[...] += dot(hits_of(plane_ref, tile * 128), rows)
 
     positive = pos_buf[...]
-    out_ref[..., D : 2 * D] = positive.astype(BF16).reshape(N_CLS, 2, D)
     picked = jnp.sum(queries.astype(F32) * positive, axis=1, keepdims=True)
     exp_total = jnp.sum(total, axis=1, keepdims=True)
-    lane = iota((QG, 128), 1)
-    stats = jnp.zeros((QG, 128), F32)
+    lane = iota((QG, 256), 1)
+    tail = sum(ref[...].astype(F32) for ref in quarter_refs)
     for at, part in enumerate(three_parts(peak) + three_parts(exp_total) + three_parts(picked)):
-        stats = jnp.where(lane == at, part, stats)
-    out_ref[..., 2 * D :] = stats.astype(BF16).reshape(N_CLS, 2, 128)
+        tail = jnp.where(lane == QUARTER + at, part, tail)
+    out_ref[..., D:] = tail.astype(BF16).reshape(N_CLS, 2, 256)
 
 
 def finish_kernel(ids_ref, back_ref, loss_ref, grad_ref):
     back = back_ref[...].reshape(QG, BACK)
-    stats = back[:, 2 * D :].astype(F32)
+    tail = back[:, D:].astype(F32)
+    stats = tail[:, 128:]
 
     def column(at):
+        at += QUARTER - 128
         return stats[:, at : at + 1] + stats[:, at + 1 : at + 2] + stats[:, at + 2 : at + 3]
 
     peak, total, picked = column(0), column(3), column(6)
     odd = (iota((QG, 1), 0) & 1) == 1
+    ring = (iota((QG, 1), 0) >> 1) & 3
     valid = jnp.where(ids_ref[lax.axis_index("rep")] >= 0, 1.0, 0.0)
     column_of = iota((4, QG), 1) - 2 * lax.axis_index(CLS)
     losses, grads = [], []
@@ -292,8 +344,12 @@
         chosen = jnp.sum(jnp.where(mine, picked, 0.0), axis=0, keepdims=True)
         losses.append(top + jnp.log(exp_total) - chosen * inverse)
         scaled = back[:, :D].astype(F32) * (weight / exp_total)
-        scaled -= jnp.where(mine, back[:, D : 2 * D].astype(F32), 0.0) * inverse
-        grads.append(jnp.sum(scaled, axis=0, keepdims=True))
+        parts = []
+        for x in range(4):
+            from_x = jnp.where(mine & (ring == x), tail[:, :QUARTER], 0.0)
+            parts.append(jnp.sum(from_x, axis=0, keepdims=True))
+        positive = jnp.concatenate(parts, axis=1)
+        grads.append(jnp.sum(scaled, axis=0, keepdims=True) - positive * inverse)
     loss_ref[...] = jnp.concatenate(losses, axis=1)
     grad_ref[...] = jnp.concatenate(grads, axis=0).astype(BF16).reshape(1, 2, D)
 
@@ -319,11 +375,14 @@
     ids = positives.transpose(0, 2, 1)
 
     any_spec = pl.BlockSpec(memory_space=pl.ANY)
-    sending = pl.pallas_call(
+    sending, encoded = pl.pallas_call(
         encode_kernel,
-        out_shape=jax.ShapeDtypeStruct((N_CLS, 2, SEND), BF16),
+        out_shape=[
+            jax.ShapeDtypeStruct((N_CLS, 2, SEND), BF16),
+            jax.ShapeDtypeStruct((HALF, D), BF16),
+        ],
         in_specs=[any_spec] * 5,
-        out_specs=vmem_spec(),
+        out_specs=[vmem_spec()] * 2,
         scratch_shapes=[
             pltpu.VMEM((HALF, D), BF16),
             pltpu.VMEM((D, D), BF16),
@@ -341,15 +400,16 @@
         in_hbm(target_rows),
         in_hbm(queries),
     )
-    keys, planes, flags = pl.pallas_call(
+    keys, planes, flags, across = pl.pallas_call(
         place_kernel,
         out_shape=[
             jax.ShapeDtypeStruct((8, QG), F32),
             jax.ShapeDtypeStruct((4, QG, 128), F32),
             jax.ShapeDtypeStruct((1, 128), jnp.int32),
+            jax.ShapeDtypeStruct((4, QG, 128), F32),
         ],
         in_specs=[vmem_spec()] * 2,
-        out_specs=[vmem_spec()] * 3,
+        out_specs=[vmem_spec()] * 4,
         compiler_params=PARAMS,
         name="place",
     )(target_rows, ids)
@@ -368,14 +428,37 @@
         name="positive",
     )(slot, flags, planes, label_vectors)
 
+    here, there = pl.pallas_call(
+        share_kernel,
+        out_shape=[jax.ShapeDtypeStruct((QG, D), F32), jax.ShapeDtypeStruct((QG, D), BF16)],
+        in_specs=[smem_spec(), any_spec] + [vmem_spec()] * 4,
+        out_specs=[vmem_spec()] * 2,
+        scratch_shapes=[pltpu.VMEM((16, 128), jnp.int32), pltpu.SemaphoreType.DMA],
+        compiler_params=PARAMS,
+        name="share",
+    )(slot, in_hbm(target_rows), free_vectors, encoded, planes, across)
+    came = lax.ppermute(there, "rep", [(0, 1), (1, 0)])
+    quarters = pl.pallas_call(
+        quarter_kernel,
+        out_shape=[jax.ShapeDtypeStruct((QG, 256), BF16)] * 4,
+        in_specs=[vmem_spec()] * 3,
+        out_specs=[vmem_spec()] * 4,
+        compiler_params=PARAMS,
+        name="quarter",
+    )(positive_old, here, came)
+    along_x = [quarters[0]] + [
+        lax.ppermute(quarters[shift], "cls_2", [(x, (x + shift) % 4) for x in range(4)])
+        for shift in (1, 2, 3)
+    ]
+
     refreshed = pl.pallas_call(
         refresh_kernel,
         out_shape=jax.ShapeDtypeStruct((HALF, D), BF16),
-        in_specs=[vmem_spec()] * 3 + [any_spec],
+        in_specs=[vmem_spec()] * 3 + [any_spec] * 4,
         out_specs=vmem_spec(),
         compiler_params=PARAMS,
         name="refresh",
-    )(keys, got, free_vectors, positive_old)
+    )(keys, got, free_vectors, *along_x)
     partner = lax.ppermute(refreshed, "rep", [(0, 1), (1, 0)])
 
     own = in_hbm(refreshed)
@@ -400,7 +483,7 @@
     leaving = pl.pallas_call(
         score_kernel,
         out_shape=jax.ShapeDtypeStruct((N_CLS, 2, BACK), BF16),
-        in_specs=[smem_spec()] * 2 + [vmem_spec(), any_spec] + [vmem_spec()] * 6,
+        in_specs=[smem_spec()] * 2 + [vmem_spec(), any_spec] + [vmem_spec()] * 10,
         out_specs=vmem_spec(),
         scratch_shapes=[
             pltpu.VMEM((HALF, D), BF16),
@@ -409,7 +492,7 @@
         ],
         compiler_params=PARAMS,
         name="score",
-    )(slot, flags, got, own, partner, *state, planes, positive_old)
+    )(slot, flags, got, own, partner, *state, planes, positive_old, *along_x)
     back = lax.all_to_all(leaving, CLS, 0, 0, tiled=True)
     loss, grads = pl.pallas_call(
         finish_kernel,

time: 96.7 us -> 92.6 us (0.958)
  waiting for transfers between devices: 22.5 us -> 13.4 us
  starting transfers between devices: 15 us -> 19.9 us
  blocking collectives: 33.2 us -> 28.6 us
  Pallas kernels: 22.4 us -> 25.5 us
  local copies, waits for them, and re-layouts: 1.7 us -> 2.76 us
    all_to_all x1, waiting for transfers between devices: 22.5 us -> 3.42 us  [per_device(): got = lax.all_to_all(sending, CLS, 0, 0, tiled=True)]
    ppermute x0 -> x4, waiting for transfers between devices: none -> 9.94 us  [the longest x3 9.94 us: per_device(): lax.ppermute(quarters[shift], 'cls_2', [(x, (x + shift) % 4) for x in ran...]
    ppermute x0 -> x4, starting transfers between devices: none -> 4.83 us  [the longest x3 4.74 us: per_device(): lax.ppermute(quarters[shift], 'cls_2', [(x, (x + shift) % 4) for x in ran...]
    all_to_all x1, blocking collectives: 33.2 us -> 28.6 us  [per_device(): back = lax.all_to_all(leaving, CLS, 0, 0, tiled=True)]
    pallas_call x1 -> x3, Pallas kernels: 4.43 us -> 7.23 us  [the longest x1 4.44 us: per_device(): pl.pallas_call(encode_kernel, out_shape=[jax.ShapeDtypeStruct((N_CLS, 2,...]
    unnamed x8 -> x10, local copies, waits for them, and re-layouts: 1.7 us -> 2.76 us
  transfers between devices with their start and end apart: 2 -> 6, of which waited for: 1 -> 3; matrix products, arithmetic and copies ran while one was open for 0% -> 0% of each run, Pallas kernels for 12% -> 16%
where the time goes in v6:
time: 92.6 us; the launch traced here: 91.4 us
  blocking collectives  28.6 us (31%)
  Pallas kernels  25.5 us (28%)
  starting transfers between devices  19.9 us (21%)
  waiting for transfers between devices  13.4 us (14%)
  local copies, waits for them, and re-layouts  2.76 us (3%)
  between operations  1.39 us (2%)
    all_to_all x1, blocking collectives, per_device(): back = lax.all_to_all(leaving, CLS, 0, 0, tiled=True)  28.6 us
    all_to_all x1, starting transfers between devices, per_device(): got = lax.all_to_all(sending, CLS, 0, 0, tiled=True)  15 us
    ppermute x3, waiting for transfers between devices, per_device(): lax.ppermute(quarters[shift], 'cls_2', [(x, (x + shift) % 4) for x in ran...  9.94 us
    pallas_call x1, Pallas kernels, per_device(): pl.pallas_call(old_kernel, out_shape=[jax.ShapeDtypeStruct((QG, 128), F32...  7.86 us
    ppermute x3, starting transfers between devices, per_device(): lax.ppermute(quarters[shift], 'cls_2', [(x, (x + shift) % 4) for x in ran...  4.74 us
    pallas_call x1, Pallas kernels, per_device(): pl.pallas_call(encode_kernel, out_shape=[jax.ShapeDtypeStruct((N_CLS, 2,...  4.44 us
    pallas_call x1, Pallas kernels, per_device(): pl.pallas_call(positive_kernel, out_shape=jax.ShapeDtypeStruct((QG, D), F...  3.77 us
    all_to_all x1, waiting for transfers between devices, per_device(): got = lax.all_to_all(sending, CLS, 0, 0, tiled=True)  3.42 us
  transfers between devices with their start and end apart: 6, of which 3 were waited for; matrix products, arithmetic and copies ran while one was open for 0% of the time, Pallas kernels for 16%

profile of v6, /device:TPU:32, one launch (start us, length us, event | category | flops | bytes accessed | tf_op | source)
XLA Modules:
  0.0 91.4 jit_solution(3310260748117879233)
XLA Ops:
  0.6 0.0 copy-start.2
  0.6 4.4 %encode.1 = (bf16[128,2,1920]{2,1,0:T(2,128)(2,1)}, bf16[384,768]{1,0:T(8,128)(2,1)S(1)}) custom-call(bf16[384,768]{1,0:T(8,128)(2,1)} %feat_ref.1, bf16[768,768]{1,0:T(8,128)(2,1)} %weight_ref.1, f32[6,128]{1,0:T(8,128)} %bitcast.13, s32[768,128]{1,0:T(8,128)} %bitcast.8, bf16[1,2,768]{2,1,0:T(2,128)(2,1)} %q_ref.1), custom_call_target="tpu_custom_call" | custom-call | tf_op jit(solution)/shard_map/encode/pallas_call | solution.py:378
  5.1 15.0 %all-to-all-start = ((bf16[128,2,1920]{2,1,0:T(2,128)(2,1)}), bf16[128,2,1920]{2,1,0:T(2,128)(2,1)S(1)}, u32[]{:S(2)}, u32[]{:S(2)}) async-start(bf16[128,2,1920]{2,1,0:T(2,128)(2,1)} %get-tuple-element.25), calls=%async_computation | async-start | bytes 1966080 | tf_op jit(solution)/shard_map/all_to_all | solution.py:416
  20.8 0.0 copy-start
  20.8 1.0 %copy-done = s32[98304]{0:T(1024)S(1)} copy-done((s32[98304]{0:T(1024)S(1)}, s32[98304]{0:T(1024)}, u32[]{:S(2)}) %copy-start) | copy-done | bytes 393240
  21.8 0.0 copy-start.3
  21.8 0.7 copy-done.3
  22.5 0.6 place.1
  23.0 0.0 copy-start.1
  23.1 1.1 %copy-done.1 = bf16[384,768]{1,0:T(8,128)(2,1)S(1)} copy-done((bf16[384,768]{1,0:T(8,128)(2,1)S(1)}, bf16[384,768]{1,0:T(8,128)(2,1)}, u32[]{:S(2)}) %copy-start.1) | copy-done | bytes 589848
  24.1 2.2 %share.1 = (f32[256,768]{1,0:T(8,128)S(1)}, bf16[256,768]{1,0:T(8,128)(2,1)S(1)}) custom-call(s32[1]{0:T(128)} %bitcast.5.slot_ref, s32[768,128]{1,0:T(8,128)} %bitcast.9, bf16[384,768]{1,0:T(8,128)(2,1)S(1)} %copy-done.1, bf16[384,768]{1,0:T(8,128)(2,1)S(1)} %get-tuple-element.28.row_ref, f32[4,256,128]{2,1,0:T(8,128)S(1)} %get-tuple-element.27.plane_ref, ...), custom_call_target="tpu_custom_call" | custom-call | tf_op jit(solution)/shard_map/share/pallas_call | solution.py:431
  26.3 0.1 collective-permute-start
  26.4 3.8 %positive.1.old_ref.pos_ref = f32[256,768]{1,0:T(8,128)S(1)} custom-call(s32[1]{0:T(128)} %bitcast.4.slot_ref, s32[1,128]{1,0:T(1,128)S(1)} %get-tuple-element.24.flag_ref, f32[4,256,128]{2,1,0:T(8,128)S(1)} %get-tuple-element.27.plane_ref, bf16[6144,768]{1,0:T(8,128)(2,1)} %lab_ref.3), custom_call_target="tpu_custom_call" | custom-call | tf_op jit(solution)/shard_map/positive/pallas_call | solution.py:418
  30.2 0.0 collective-permute-done.came_ref
  30.2 0.6 quarter.1
  30.8 2.0 %collective-permute-start.1 = (bf16[256,256]{1,0:T(8,128)(2,1)S(1)}, bf16[256,256]{1,0:T(8,128)(2,1)S(1)}, u32[]{:S(2)}, u32[]{:S(2)}) collective-permute-start(bf16[256,256]{1,0:T(8,128)(2,1)S(1)} %get-tuple-element.33), channel_id=1, source_target_pairs={{0,2},{2,4},{4,6},{6,0},{1,3},{3,5},{5,7},{7,1},{8,10},{10,12},{12... | collective-permute-start | bytes 393224 | tf_op jit(solution)/shard_map/ppermute | solution.py:450
  32.8 2.1 %collective-permute-start.2 = (bf16[256,256]{1,0:T(8,128)(2,1)S(1)}, bf16[256,256]{1,0:T(8,128)(2,1)S(1)}, u32[]{:S(2)}, u32[]{:S(2)}) collective-permute-start(bf16[256,256]{1,0:T(8,128)(2,1)S(1)} %get-tuple-element.34), channel_id=1, source_target_pairs={{0,4},{2,6},{4,0},{6,2},{1,5},{3,7},{5,1},{7,3},{8,12},{10,14},{12... | collective-permute-start | bytes 393224 | tf_op jit(solution)/shard_map/ppermute | solution.py:450
  34.9 0.7 collective-permute-start.3
  35.5 4.7 %collective-permute-done.1.refs_1_ = bf16[256,256]{1,0:T(8,128)(2,1)S(1)} collective-permute-done((bf16[256,256]{1,0:T(8,128)(2,1)S(1)}, bf16[256,256]{1,0:T(8,128)(2,1)S(1)}, u32[]{:S(2)}, u32[]{:S(2)}) %collective-permute-start.1) | collective-permute-done | bytes 131104 | tf_op jit(solution)/shard_map/ppermute | solution.py:450
  40.2 5.3 %collective-permute-done.2.refs_2_ = bf16[256,256]{1,0:T(8,128)(2,1)S(1)} collective-permute-done((bf16[256,256]{1,0:T(8,128)(2,1)S(1)}, bf16[256,256]{1,0:T(8,128)(2,1)S(1)}, u32[]{:S(2)}, u32[]{:S(2)}) %collective-permute-start.2) | collective-permute-done | bytes 131104 | tf_op jit(solution)/shard_map/ppermute | solution.py:450
  45.5 0.0 collective-permute-done.3.refs_3_
  45.5 3.4 %all-to-all-done.got_ref = bf16[128,2,1920]{2,1,0:T(2,128)(2,1)S(1)} async-done(((bf16[128,2,1920]{2,1,0:T(2,128)(2,1)}), bf16[128,2,1920]{2,1,0:T(2,128)(2,1)S(1)}, u32[]{:S(2)}, u32[]{:S(2)}) %all-to-all-start) | async-done | bytes 983072 | tf_op jit(solution)/shard_map/all_to_all | solution.py:416
  48.9 0.0 copy-done.2
  48.9 1.6 %refresh.1.own_ref = bf16[384,768]{1,0:T(8,128)(2,1)} custom-call(f32[8,256]{1,0:T(8,128)S(1)} %get-tuple-element.26.key_ref, bf16[128,2,1920]{2,1,0:T(2,128)(2,1)S(1)} %all-to-all-done.got_ref, bf16[384,768]{1,0:T(8,128)(2,1)S(1)} %copy-done.2, bf16[256,256]{1,0:T(8,128)(2,1)S(1)} %get-tuple-element.32.refs_0_, ...), custom_call_target="tpu_custom_call" | custom-call | tf_op jit(solution)/shard_map/refresh/pallas_call | solution.py:454
  50.5 0.0 copy-start.4
  50.5 0.0 collective-permute-start.4
  50.6 7.9 %old.1 = (f32[256,128]{1,0:T(8,128)S(1)}, f32[256,128]{1,0:T(8,128)S(1)}, f32[256,768]{1,0:T(8,128)S(1)}) custom-call(s32[1]{0:T(128)} %bitcast.6.slot_ref, bf16[128,2,1920]{2,1,0:T(2,128)(2,1)S(1)} %all-to-all-done.got_ref, bf16[384,768]{1,0:T(8,128)(2,1)} %refresh.1.own_ref, bf16[6144,768]{1,0:T(8,128)(2,1)} %lab_ref.3), custom_call_target="tpu_custom_call" | custom-call | tf_op jit(solution)/shard_map/old/pallas_call | solution.py:465
  58.4 0.0 collective-permute-done.4.other_ref
  58.4 2.1 %score.1 = bf16[128,2,1024]{2,1,0:T(2,128)(2,1)S(1)} custom-call(s32[1]{0:T(128)} %bitcast.7.slot_ref, s32[1,128]{1,0:T(1,128)S(1)} %get-tuple-element.24.flag_ref, bf16[128,2,1920]{2,1,0:T(2,128)(2,1)S(1)} %all-to-all-done.got_ref, bf16[384,768]{1,0:T(8,128)(2,1)} %refresh.1.own_ref, bf16[384,768]{1,0:T(8,128)(2,1)S(1)} %collective-permute-done.4.other_ref, ...), custom_call_target="tpu_custom_call" | custom-call | tf_op jit(solution)/shard_map/score/pallas_call | solution.py:483
  60.5 28.6 %all_to_all.10.back_ref = bf16[128,2,1024]{2,1,0:T(2,128)(2,1)S(1)} all-to-all(bf16[128,2,1024]{2,1,0:T(2,128)(2,1)S(1)} %score.1), channel_id=1, replica_groups=mesh['cls_0'=4,'cls_1'=8,'cls_2'=4,'rep'=2] {'cls_0','cls_1','cls_2'}, dimensions={0} | all-to-all | bytes 1048576 | tf_op jit(solution)/shard_map/all_to_all | solution.py:496
  89.1 0.0 copy-done.4
  89.1 2.3 %finish.1 = (f32[1,2]{1,0:T(1,128)}, bf16[1,2,768]{2,1,0:T(2,128)(2,1)}) custom-call(s32[2,4,256]{2,1,0:T(4,128)S(1)} %bitcast.12, bf16[128,2,1024]{2,1,0:T(2,128)(2,1)S(1)} %all_to_all.10.back_ref), custom_call_target="tpu_custom_call" | custom-call | tf_op jit(solution)/shard_map/finish/pallas_call | solution.py:497
Async XLA Ops:
  0.6 48.3 %copy-start.2 = (bf16[384,768]{1,0:T(8,128)(2,1)S(1)}, bf16[384,768]{1,0:T(8,128)(2,1)}, u32[]{:S(2)}) copy-start(bf16[384,768]{1,0:T(8,128)(2,1)} %free_ref.3) | copy-start | bytes 1769476
  5.1 43.8 %all-to-all-start = ((bf16[128,2,1920]{2,1,0:T(2,128)(2,1)}), bf16[128,2,1920]{2,1,0:T(2,128)(2,1)S(1)}, u32[]{:S(2)}, u32[]{:S(2)}) async-start(bf16[128,2,1920]{2,1,0:T(2,128)(2,1)} %get-tuple-element.25), calls=%async_computation | async-start | bytes 1966080 | tf_op jit(solution)/shard_map/all_to_all | solution.py:416
  20.8 1.0 %copy-start = (s32[98304]{0:T(1024)S(1)}, s32[98304]{0:T(1024)}, u32[]{:S(2)}) copy-start(s32[98304]{0:T(1024)} %param.17) | copy-start | bytes 1179652
  21.8 0.7 copy-start.3
  23.0 1.1 %copy-start.1 = (bf16[384,768]{1,0:T(8,128)(2,1)S(1)}, bf16[384,768]{1,0:T(8,128)(2,1)}, u32[]{:S(2)}) copy-start(bf16[384,768]{1,0:T(8,128)(2,1)} %free_ref.3) | copy-start | bytes 1769476
  26.3 3.9 %collective-permute-start = (bf16[256,768]{1,0:T(8,128)(2,1)S(1)}, bf16[256,768]{1,0:T(8,128)(2,1)S(1)}, u32[]{:S(2)}, u32[]{:S(2)}) collective-permute-start(bf16[256,768]{1,0:T(8,128)(2,1)S(1)} %get-tuple-element.31), channel_id=1, source_target_pairs={{0,1},{1,0},{2,3},{3,2},{4,5},{5,4},{6,7},{7,6},{8,9},{9,8},{10,11... | collective-permute-start | bytes 1179656 | tf_op jit(solution)/shard_map/ppermute | solution.py:440
  30.8 9.4 %collective-permute-start.1 = (bf16[256,256]{1,0:T(8,128)(2,1)S(1)}, bf16[256,256]{1,0:T(8,128)(2,1)S(1)}, u32[]{:S(2)}, u32[]{:S(2)}) collective-permute-start(bf16[256,256]{1,0:T(8,128)(2,1)S(1)} %get-tuple-element.33), channel_id=1, source_target_pairs={{0,2},{2,4},{4,6},{6,0},{1,3},{3,5},{5,7},{7,1},{8,10},{10,12},{12... | collective-permute-start | bytes 393224 | tf_op jit(solution)/shard_map/ppermute | solution.py:450
  32.8 12.7 %collective-permute-start.2 = (bf16[256,256]{1,0:T(8,128)(2,1)S(1)}, bf16[256,256]{1,0:T(8,128)(2,1)S(1)}, u32[]{:S(2)}, u32[]{:S(2)}) collective-permute-start(bf16[256,256]{1,0:T(8,128)(2,1)S(1)} %get-tuple-element.34), channel_id=1, source_target_pairs={{0,4},{2,6},{4,0},{6,2},{1,5},{3,7},{5,1},{7,3},{8,12},{10,14},{12... | collective-permute-start | bytes 393224 | tf_op jit(solution)/shard_map/ppermute | solution.py:450
  34.9 10.6 %collective-permute-start.3 = (bf16[256,256]{1,0:T(8,128)(2,1)S(1)}, bf16[256,256]{1,0:T(8,128)(2,1)S(1)}, u32[]{:S(2)}, u32[]{:S(2)}) collective-permute-start(bf16[256,256]{1,0:T(8,128)(2,1)S(1)} %get-tuple-element.35), channel_id=1, source_target_pairs={{0,6},{2,0},{4,2},{6,4},{1,7},{3,1},{5,3},{7,5},{8,14},{10,8},{12,... | collective-permute-start | bytes 393224 | tf_op jit(solution)/shard_map/ppermute | solution.py:450
  50.5 38.6 %copy-start.4 = (s32[2,256,4]{1,2,0:T(4,128)S(1)}, s32[2,256,4]{1,2,0:T(4,128)}, u32[]{:S(2)}) copy-start(s32[2,256,4]{1,2,0:T(4,128)} %param.10) | copy-start | bytes 24580
  50.5 7.9 %collective-permute-start.4 = (bf16[384,768]{1,0:T(8,128)(2,1)}, bf16[384,768]{1,0:T(8,128)(2,1)S(1)}, u32[]{:S(2)}, u32[]{:S(2)}) collective-permute-start(bf16[384,768]{1,0:T(8,128)(2,1)} %refresh.1.own_ref), channel_id=1, source_target_pairs={{0,1},{1,0},{2,3},{3,2},{4,5},{5,4},{6,7},{7,6},{8,9},{9,8},{10,11... | collective-permute-start | bytes 1769480 | tf_op jit(solution)/shard_map/ppermute | solution.py:462

commit v7 on v6

--- a/solution.py
+++ b/solution.py
@@ -5,6 +5,7 @@
 from jax.experimental.pallas import tpu as pltpu
 from jax.sharding import Mesh
 from jax.sharding import PartitionSpec as P
+
 
 SLOTS = 8
 OLD = SLOTS - 1
@@ -104,10 +105,45 @@
         out_ref[..., k * HALF : (k + 1) * HALF] = total.astype(BF16).reshape(N_CLS, 2, HALF)
 
 
-def place_kernel(tgt_ref, ids_ref, key_ref, plane_ref, flag_ref, across_ref):
+def hits_at(plane_ref, label):
+    hits = jnp.zeros((QG, 128), F32)
+    for k in range(4):
+        hits += jnp.where(plane_ref[k] == label, 1.0, 0.0)
+    return hits.astype(BF16)
+
+
+def hits_of(plane_ref, first):
+    return hits_at(plane_ref, iota((QG, 128), 1).astype(F32) + first.astype(F32))
+
+
+def place_kernel(
+    slot_ref, tgt_ref, ids_ref, free_ref, row_ref, key_ref, plane_ref, flag_ref, here_ref,
+    there_ref, tgt_buf, ids_buf, free_buf, across_ref, sems,
+):
+    pairs = [(ids_ref, ids_buf), (tgt_ref, tgt_buf), (free_ref, free_buf)]
+    copies = [pltpu.make_async_copy(a, b, sems.at[i]) for i, (a, b) in enumerate(pairs)]
+    for copy in copies:
+        copy.start()
     cls_index, rep_index = lax.axis_index(CLS), lax.axis_index("rep")
+    first = cls_index * (SLOTS * D)
+    lane = iota((QG, 128), 1)
+    seen = jnp.zeros((QG, 128), F32)
+    copies[0].wait()
+
+    def plane_of(half, k):
+        own = (ids_buf[half, k : k + 1, :] - first).astype(F32)
+        return jnp.concatenate([spread_down(own[:, :128]), spread_down(own[:, 128:])], axis=0)
+
+    for k in range(4):
+        across_ref[k] = plane_of(1 - rep_index, k)
+        plane = plane_of(rep_index, k)
+        plane_ref[k] = plane
+        seen = jnp.where((plane.astype(jnp.int32) >> 7) == lane, 1.0, seen)
+    flag_ref[...] = jnp.max(seen, axis=0, keepdims=True).astype(jnp.int32)
+
+    copies[1].wait()
     base = cls_index * (2 * HALF) + rep_index * HALF
-    parts = [tgt_ref[pl.ds(3 * rep_index + a, N_CLS, stride=6), :] for a in range(3)]
+    parts = [tgt_buf[pl.ds(3 * rep_index + a, N_CLS, stride=6), :] for a in range(3)]
     offsets = jnp.concatenate(parts, axis=1) - base
     inside = (offsets >= 0) & (offsets < HALF)
     far = 4096.0
@@ -119,31 +155,23 @@
         keys = jnp.where(keys == least, far, keys)
         wide = jnp.broadcast_to(least, (N_CLS, QG))
         key_ref[k : k + 1, :] = jnp.sum(jnp.where(twice, wide, 0.0), axis=0, keepdims=True)
-    first = cls_index * (SLOTS * D)
-    lane = iota((QG, 128), 1)
-    seen = jnp.zeros((QG, 128), F32)
-
-    def plane_of(half, k):
-        own = (ids_ref[half, k : k + 1, :] - first).astype(F32)
-        return jnp.concatenate([spread_down(own[:, :128]), spread_down(own[:, 128:])], axis=0)
-
-    for k in range(4):
-        across_ref[k] = plane_of(1 - rep_index, k)
-        plane = plane_of(rep_index, k)
-        plane_ref[k] = plane
-        seen = jnp.where((plane.astype(jnp.int32) >> 7) == lane, 1.0, seen)
-    flag_ref[...] = jnp.max(seen, axis=0, keepdims=True).astype(jnp.int32)
-
-
-def hits_at(plane_ref, label):
-    hits = jnp.zeros((QG, 128), F32)
-    for k in range(4):
-        hits += jnp.where(plane_ref[k] == label, 1.0, 0.0)
-    return hits.astype(BF16)
-
-
-def hits_of(plane_ref, first):
-    return hits_at(plane_ref, iota((QG, 128), 1).astype(F32) + first.astype(F32))
+
+    slot_first = slot_ref[0] * D
+    free_first = slot_first + rep_index * HALF
+    labels = []
+    for part in range(3):
+        target = tgt_buf[pl.ds(3 * lax.axis_index(CLS_REP) + part, 1), :]
+        owner = ((target >> 8) * 21846) >> 16
+        local = (owner - cls_index) * (SLOTS * D) + slot_first + (target - owner * D)
+        labels.append(local.astype(F32))
+    copies[2].wait()
+    for planes, out_ref in ((across_ref, there_ref), (plane_ref, here_ref)):
+        total = jnp.zeros((QG, D), F32)
+        for part in range(3):
+            rows = slice(part * 128, (part + 1) * 128)
+            total += dot(hits_of(planes, free_first + part * 128), free_buf[rows, :])
+            total += dot(hits_at(planes, labels[part]), row_ref[rows, :])
+        out_ref[...] = total.astype(out_ref.dtype)
 
 
 def positive_kernel(slot_ref, flag_ref, plane_ref, lab_ref, out_ref, lab_buf, sems):
@@ -173,31 +201,6 @@
         return carry
 
     lax.fori_loop(0, OLD * 6, body, 0)
-
-
-def share_kernel(
-    slot_ref, tgt_ref, free_ref, row_ref, plane_ref, across_ref, here_ref, there_ref, tgt_buf, sem
-):
-    row, begin = own_target_rows()
-    copy = pltpu.make_async_copy(tgt_ref.at[pl.ds(begin, 16), :], tgt_buf, sem)
-    copy.start()
-    slot_first = slot_ref[0] * D
-    free_first = slot_first + lax.axis_index("rep") * HALF
-    copy.wait()
-    labels = []
-    for part in range(3):
-        target = tgt_buf[pl.ds(row - begin + part, 1), :]
-        owner = ((target >> 8) * 21846) >> 16
-        behind = owner - lax.axis_index(CLS)
-        local = behind * (SLOTS * D) + slot_first + (target - owner * D)
-        labels.append(local.astype(F32))
-    for planes, out_ref in ((plane_ref, here_ref), (across_ref, there_ref)):
-        total = jnp.zeros((QG, D), F32)
-        for part in range(3):
-            rows = slice(part * 128, (part + 1) * 128)
-            total += dot(hits_of(planes, free_first + part * 128), free_ref[rows, :])
-            total += dot(hits_at(planes, labels[part]), row_ref[rows, :])
-        out_ref[...] = total.astype(out_ref.dtype)
 
 
 def quarter_kernel(old_ref, here_ref, came_ref, *out_refs):
@@ -333,7 +336,7 @@
     ring = (iota((QG, 1), 0) >> 1) & 3
     valid = jnp.where(ids_ref[lax.axis_index("rep")] >= 0, 1.0, 0.0)
     column_of = iota((4, QG), 1) - 2 * lax.axis_index(CLS)
-    losses, grads = [], []
+    losses, weights, picks = [], [], []
     for h in range(2):
         mine = odd if h else ~odd
         top = jnp.max(jnp.where(mine, peak, -jnp.inf), axis=0, keepdims=True)
@@ -343,14 +346,23 @@
         inverse = 1.0 / jnp.sum(count, axis=0, keepdims=True)
         chosen = jnp.sum(jnp.where(mine, picked, 0.0), axis=0, keepdims=True)
         losses.append(top + jnp.log(exp_total) - chosen * inverse)
-        scaled = back[:, :D].astype(F32) * (weight / exp_total)
-        parts = []
-        for x in range(4):
-            from_x = jnp.where(mine & (ring == x), tail[:, :QUARTER], 0.0)
-            parts.append(jnp.sum(from_x, axis=0, keepdims=True))
-        positive = jnp.concatenate(parts, axis=1)
-        grads.append(jnp.sum(scaled, axis=0, keepdims=True) - positive * inverse)
+        weights.append(weight / exp_total)
+        picks.append(inverse)
     loss_ref[...] = jnp.concatenate(losses, axis=1)
+    lane = iota((QG, 128), 1)
+    table = jnp.where(lane == 8 + 4 * jnp.where(odd, 1, 0) + ring, 1.0, 0.0)
+    for h in range(2):
+        for at, part in enumerate(three_parts(weights[h])):
+            table = jnp.where(lane == 3 * h + at, part, table)
+    sums = dot_first(table.astype(BF16), back)
+    grads = []
+    for h in range(2):
+        positive = jnp.concatenate(
+            [sums[8 + 4 * h + x : 9 + 4 * h + x, D : D + QUARTER] for x in range(4)], axis=1
+        )
+        scaled = sums[3 * h : 3 * h + 1, :D] + sums[3 * h + 1 : 3 * h + 2, :D]
+        scaled += sums[3 * h + 2 : 3 * h + 3, :D]
+        grads.append(scaled - positive * picks[h])
     grad_ref[...] = jnp.concatenate(grads, axis=0).astype(BF16).reshape(1, 2, D)
 
 
@@ -400,19 +412,27 @@
         in_hbm(target_rows),
         in_hbm(queries),
     )
-    keys, planes, flags, across = pl.pallas_call(
+    keys, planes, flags, here, there = pl.pallas_call(
         place_kernel,
         out_shape=[
             jax.ShapeDtypeStruct((8, QG), F32),
             jax.ShapeDtypeStruct((4, QG, 128), F32),
             jax.ShapeDtypeStruct((1, 128), jnp.int32),
-            jax.ShapeDtypeStruct((4, QG, 128), F32),
-        ],
-        in_specs=[vmem_spec()] * 2,
-        out_specs=[vmem_spec()] * 4,
+            jax.ShapeDtypeStruct((QG, D), F32),
+            jax.ShapeDtypeStruct((QG, D), BF16),
+        ],
+        in_specs=[smem_spec()] + [any_spec] * 3 + [vmem_spec()],
+        out_specs=[vmem_spec()] * 5,
+        scratch_shapes=[
+            pltpu.VMEM((768, 128), jnp.int32),
+            pltpu.VMEM((2, 4, QG), jnp.int32),
+            pltpu.VMEM((HALF, D), BF16),
+            pltpu.VMEM((4, QG, 128), F32),
+            pltpu.SemaphoreType.DMA((3,)),
+        ],
         compiler_params=PARAMS,
         name="place",
-    )(target_rows, ids)
+    )(slot, in_hbm(target_rows), in_hbm(ids), in_hbm(free_vectors), encoded)
     got = lax.all_to_all(sending, CLS, 0, 0, tiled=True)
 
     positive_old = pl.pallas_call(
@@ -428,15 +448,6 @@
         name="positive",
     )(slot, flags, planes, label_vectors)
 
-    here, there = pl.pallas_call(
-        share_kernel,
-        out_shape=[jax.ShapeDtypeStruct((QG, D), F32), jax.ShapeDtypeStruct((QG, D), BF16)],
-        in_specs=[smem_spec(), any_spec] + [vmem_spec()] * 4,
-        out_specs=[vmem_spec()] * 2,
-        scratch_shapes=[pltpu.VMEM((16, 128), jnp.int32), pltpu.SemaphoreType.DMA],
-        compiler_params=PARAMS,
-        name="share",
-    )(slot, in_hbm(target_rows), free_vectors, encoded, planes, across)
     came = lax.ppermute(there, "rep", [(0, 1), (1, 0)])
     quarters = pl.pallas_call(
         quarter_kernel,
@@ -446,19 +457,19 @@
         compiler_params=PARAMS,
         name="quarter",
     )(positive_old, here, came)
-    along_x = [quarters[0]] + [
-        lax.ppermute(quarters[shift], "cls_2", [(x, (x + shift) % 4) for x in range(4)])
-        for shift in (1, 2, 3)
-    ]
+    along_x = [quarters[0]]
+    for shift in (1, 2, 3):
+        pairs = [(x, (x + shift) % 4) for x in range(4)]
+        along_x.append(lax.ppermute(quarters[shift], "cls_2", pairs))
 
     refreshed = pl.pallas_call(
         refresh_kernel,
         out_shape=jax.ShapeDtypeStruct((HALF, D), BF16),
-        in_specs=[vmem_spec()] * 3 + [any_spec] * 4,
+        in_specs=[vmem_spec()] * 3 + [any_spec],
         out_specs=vmem_spec(),
         compiler_params=PARAMS,
         name="refresh",
-    )(keys, got, free_vectors, *along_x)
+    )(keys, got, free_vectors, quarters[0])
     partner = lax.ppermute(refreshed, "rep", [(0, 1), (1, 0)])
 
     own = in_hbm(refreshed)

time: 92.6 us -> 94.4 us (1.019)
  waiting for transfers between devices: 13.4 us -> 20.1 us
  local copies, waits for them, and re-layouts: 2.76 us -> 0.01 us
  blocking collectives: 28.6 us -> 27.1 us
    all_to_all x1, waiting for transfers between devices: 3.42 us -> 20.1 us  [per_device(): got = lax.all_to_all(sending, CLS, 0, 0, tiled=True)]
    ppermute x3, waiting for transfers between devices: 9.94 us -> 0.01 us  [per_device(): along_x.append(lax.ppermute(quarters[shift], 'cls_2', pairs))]
    unnamed x10 -> x4, local copies, waits for them, and re-layouts: 2.76 us -> 0.01 us
    pallas_call x1, Pallas kernels: 0.58 us -> 2.77 us  [per_device(): pl.pallas_call(place_kernel, out_shape=[jax.ShapeDtypeStruct((8, QG), F32...]
    pallas_call x1 -> x0, Pallas kernels: 2.17 us -> none  [per_device(): pl.pallas_call(share_kernel, out_shape=[jax.ShapeDtypeStruct((QG, D), F32...]
    all_to_all x1, blocking collectives: 28.6 us -> 27.1 us  [per_device(): back = lax.all_to_all(leaving, CLS, 0, 0, tiled=True)]
  transfers between devices with their start and end apart: 6 -> 6, of which waited for: 3 -> 1; matrix products, arithmetic and copies ran while one was open for 0% -> 0% of each run, Pallas kernels for 16% -> 17%
where the time goes in v7:
time: 94.4 us; the launch traced here: 94 us
  blocking collectives  27.1 us (29%)
  Pallas kernels  26 us (28%)
  waiting for transfers between devices  20.1 us (21%)
  starting transfers between devices  19.4 us (21%)
  between operations  1.39 us (1%)
    all_to_all x1, blocking collectives, per_device(): back = lax.all_to_all(leaving, CLS, 0, 0, tiled=True)  27.1 us
    all_to_all x1, waiting for transfers between devices, per_device(): got = lax.all_to_all(sending, CLS, 0, 0, tiled=True)  20.1 us
    all_to_all x1, starting transfers between devices, per_device(): got = lax.all_to_all(sending, CLS, 0, 0, tiled=True)  15 us
    pallas_call x1, Pallas kernels, per_device(): pl.pallas_call(old_kernel, out_shape=[jax.ShapeDtypeStruct((QG, 128), F32...  7.88 us
    pallas_call x1, Pallas kernels, per_device(): pl.pallas_call(positive_kernel, out_shape=jax.ShapeDtypeStruct((QG, D), F...  4.52 us
    pallas_call x1, Pallas kernels, per_device(): pl.pallas_call(encode_kernel, out_shape=[jax.ShapeDtypeStruct((N_CLS, 2,...  4.43 us
    ppermute x3, starting transfers between devices, per_device(): along_x.append(lax.ppermute(quarters[shift], 'cls_2', pairs))  4.29 us
    pallas_call x1, Pallas kernels, per_device(): pl.pallas_call(place_kernel, out_shape=[jax.ShapeDtypeStruct((8, QG), F32...  2.77 us
  transfers between devices with their start and end apart: 6, of which 1 were waited for; matrix products, arithmetic and copies ran while one was open for 0% of the time, Pallas kernels for 17%

profile of v7, /device:TPU:32, one launch (start us, length us, event | category | flops | bytes accessed | tf_op | source)
XLA Modules:
  0.0 94.0 jit_solution(8586049551765146291)
XLA Ops:
  0.6 0.0 copy-start
  0.6 4.4 %encode.1 = (bf16[128,2,1920]{2,1,0:T(2,128)(2,1)}, bf16[384,768]{1,0:T(8,128)(2,1)S(1)}) custom-call(bf16[384,768]{1,0:T(8,128)(2,1)} %feat_ref.1, bf16[768,768]{1,0:T(8,128)(2,1)} %weight_ref.1, f32[6,128]{1,0:T(8,128)} %bitcast.12, s32[768,128]{1,0:T(8,128)} %bitcast.10, bf16[1,2,768]{2,1,0:T(2,128)(2,1)} %q_ref.1), custom_call_target="tpu_custom_call" | custom-call | tf_op jit(solution)/shard_map/encode/pallas_call | solution.py:390
  5.1 15.0 %all-to-all-start = ((bf16[128,2,1920]{2,1,0:T(2,128)(2,1)}), bf16[128,2,1920]{2,1,0:T(2,128)(2,1)S(1)}, u32[]{:S(2)}, u32[]{:S(2)}) async-start(bf16[128,2,1920]{2,1,0:T(2,128)(2,1)} %get-tuple-element.25), calls=%async_computation | async-start | bytes 1966080 | tf_op jit(solution)/shard_map/all_to_all | solution.py:436
  20.7 2.8 %place.1 = (f32[8,256]{1,0:T(8,128)S(1)}, f32[4,256,128]{2,1,0:T(8,128)S(1)}, s32[1,128]{1,0:T(1,128)S(1)}, f32[256,768]{1,0:T(8,128)S(1)}, bf16[256,768]{1,0:T(8,128)(2,1)S(1)}) custom-call(s32[1]{0:T(128)} %bitcast.4.slot_ref, s32[768,128]{1,0:T(8,128)} %bitcast.11, s32[2,4,256]{2,1,0:T(4,128)} %bitcast.8, bf16[384,768]{1,0:T(8,128)(2,1)} %free_ref.3, ...), custom_call_target="tpu_custom_call" | custom-call | tf_op jit(solution)/shard_map/place/pallas_call | solution.py:415
  23.5 0.1 collective-permute-start
  23.6 4.5 %positive.1.old_ref.pos_ref = f32[256,768]{1,0:T(8,128)S(1)} custom-call(s32[1]{0:T(128)} %bitcast.5.slot_ref, s32[1,128]{1,0:T(1,128)S(1)} %get-tuple-element.24.flag_ref, f32[4,256,128]{2,1,0:T(8,128)S(1)} %get-tuple-element.27.plane_ref, bf16[6144,768]{1,0:T(8,128)(2,1)} %lab_ref.3), custom_call_target="tpu_custom_call" | custom-call | tf_op jit(solution)/shard_map/positive/pallas_call | solution.py:438
  28.2 0.0 collective-permute-done.came_ref
  28.2 0.6 quarter.1
  28.8 20.1 %all-to-all-done.got_ref = bf16[128,2,1920]{2,1,0:T(2,128)(2,1)S(1)} async-done(((bf16[128,2,1920]{2,1,0:T(2,128)(2,1)}), bf16[128,2,1920]{2,1,0:T(2,128)(2,1)S(1)}, u32[]{:S(2)}, u32[]{:S(2)}) %all-to-all-start) | async-done | bytes 983072 | tf_op jit(solution)/shard_map/all_to_all | solution.py:436
  48.9 0.0 copy-done
  48.9 0.0 copy-start.1
  48.9 1.6 %refresh.1.own_ref = bf16[384,768]{1,0:T(8,128)(2,1)} custom-call(f32[8,256]{1,0:T(8,128)S(1)} %get-tuple-element.26.key_ref, bf16[128,2,1920]{2,1,0:T(2,128)(2,1)S(1)} %all-to-all-done.got_ref, bf16[384,768]{1,0:T(8,128)(2,1)S(1)} %copy-done, bf16[256,256]{1,0:T(8,128)(2,1)S(1)} %get-tuple-element.30.refs_0_), custom_call_target="tpu_custom_call" | custom-call | tf_op jit(solution)/shard_map/refresh/pallas_call | solution.py:465
  50.5 0.0 collective-permute-start.1
  50.6 0.4 collective-permute-start.2
  50.9 2.8 %collective-permute-start.3 = (bf16[256,256]{1,0:T(8,128)(2,1)S(1)}, bf16[256,256]{1,0:T(8,128)(2,1)S(1)}, u32[]{:S(2)}, u32[]{:S(2)}) collective-permute-start(bf16[256,256]{1,0:T(8,128)(2,1)S(1)} %get-tuple-element.39), channel_id=1, source_target_pairs={{0,4},{2,6},{4,0},{6,2},{1,5},{3,7},{5,1},{7,3},{8,12},{10,14},{12... | collective-permute-start | bytes 393224 | tf_op jit(solution)/shard_map/ppermute | solution.py:463
  53.8 1.0 %collective-permute-start.4 = (bf16[256,256]{1,0:T(8,128)(2,1)S(1)}, bf16[256,256]{1,0:T(8,128)(2,1)S(1)}, u32[]{:S(2)}, u32[]{:S(2)}) collective-permute-start(bf16[256,256]{1,0:T(8,128)(2,1)S(1)} %get-tuple-element.40), channel_id=1, source_target_pairs={{0,6},{2,0},{4,2},{6,4},{1,7},{3,1},{5,3},{7,5},{8,14},{10,8},{12,... | collective-permute-start | bytes 393224 | tf_op jit(solution)/shard_map/ppermute | solution.py:463
  54.8 7.9 %old.1 = (f32[256,128]{1,0:T(8,128)S(1)}, f32[256,128]{1,0:T(8,128)S(1)}, f32[256,768]{1,0:T(8,128)S(1)}) custom-call(s32[1]{0:T(128)} %bitcast.6.slot_ref, bf16[128,2,1920]{2,1,0:T(2,128)(2,1)S(1)} %all-to-all-done.got_ref, bf16[384,768]{1,0:T(8,128)(2,1)} %refresh.1.own_ref, bf16[6144,768]{1,0:T(8,128)(2,1)} %lab_ref.3), custom_call_target="tpu_custom_call" | custom-call | tf_op jit(solution)/shard_map/old/pallas_call | solution.py:476
  62.7 0.0 collective-permute-done.1.other_ref
  62.7 0.0 collective-permute-done.2.refs_1_
  62.8 0.0 collective-permute-done.3.refs_2_
  62.8 0.0 collective-permute-done.4.refs_3_
  62.8 2.1 %score.1 = bf16[128,2,1024]{2,1,0:T(2,128)(2,1)S(1)} custom-call(s32[1]{0:T(128)} %bitcast.7.slot_ref, s32[1,128]{1,0:T(1,128)S(1)} %get-tuple-element.24.flag_ref, bf16[128,2,1920]{2,1,0:T(2,128)(2,1)S(1)} %all-to-all-done.got_ref, bf16[384,768]{1,0:T(8,128)(2,1)} %refresh.1.own_ref, bf16[384,768]{1,0:T(8,128)(2,1)S(1)} %collective-permute-done.1.other_ref, ...), custom_call_target="tpu_custom_call" | custom-call | tf_op jit(solution)/shard_map/score/pallas_call | solution.py:494
  64.9 27.1 %all_to_all.10.back_ref = bf16[128,2,1024]{2,1,0:T(2,128)(2,1)S(1)} all-to-all(bf16[128,2,1024]{2,1,0:T(2,128)(2,1)S(1)} %score.1), channel_id=1, replica_groups=mesh['cls_0'=4,'cls_1'=8,'cls_2'=4,'rep'=2] {'cls_0','cls_1','cls_2'}, dimensions={0} | all-to-all | bytes 1048576 | tf_op jit(solution)/shard_map/all_to_all | solution.py:507
  91.9 0.0 copy-done.1
  91.9 2.1 %finish.1 = (f32[1,2]{1,0:T(1,128)}, bf16[1,2,768]{2,1,0:T(2,128)(2,1)}) custom-call(s32[2,4,256]{2,1,0:T(4,128)S(1)} %bitcast.9, bf16[128,2,1024]{2,1,0:T(2,128)(2,1)S(1)} %all_to_all.10.back_ref), custom_call_target="tpu_custom_call" | custom-call | tf_op jit(solution)/shard_map/finish/pallas_call | solution.py:508
Async XLA Ops:
  0.6 48.3 %copy-start = (bf16[384,768]{1,0:T(8,128)(2,1)S(1)}, bf16[384,768]{1,0:T(8,128)(2,1)}, u32[]{:S(2)}) copy-start(bf16[384,768]{1,0:T(8,128)(2,1)} %free_ref.3) | copy-start | bytes 1769476
  5.1 43.8 %all-to-all-start = ((bf16[128,2,1920]{2,1,0:T(2,128)(2,1)}), bf16[128,2,1920]{2,1,0:T(2,128)(2,1)S(1)}, u32[]{:S(2)}, u32[]{:S(2)}) async-start(bf16[128,2,1920]{2,1,0:T(2,128)(2,1)} %get-tuple-element.25), calls=%async_computation | async-start | bytes 1966080 | tf_op jit(solution)/shard_map/all_to_all | solution.py:436
  23.5 4.6 %collective-permute-start = (bf16[256,768]{1,0:T(8,128)(2,1)S(1)}, bf16[256,768]{1,0:T(8,128)(2,1)S(1)}, u32[]{:S(2)}, u32[]{:S(2)}) collective-permute-start(bf16[256,768]{1,0:T(8,128)(2,1)S(1)} %get-tuple-element.29), channel_id=1, source_target_pairs={{0,1},{1,0},{2,3},{3,2},{4,5},{5,4},{6,7},{7,6},{8,9},{9,8},{10,11... | collective-permute-start | bytes 1179656 | tf_op jit(solution)/shard_map/ppermute | solution.py:451
  48.9 43.0 %copy-start.1 = (s32[2,256,4]{1,2,0:T(4,128)S(1)}, s32[2,256,4]{1,2,0:T(4,128)}, u32[]{:S(2)}) copy-start(s32[2,256,4]{1,2,0:T(4,128)} %param.10) | copy-start | bytes 24580
  50.5 12.2 %collective-permute-start.1 = (bf16[384,768]{1,0:T(8,128)(2,1)}, bf16[384,768]{1,0:T(8,128)(2,1)S(1)}, u32[]{:S(2)}, u32[]{:S(2)}) collective-permute-start(bf16[384,768]{1,0:T(8,128)(2,1)} %refresh.1.own_ref), channel_id=1, source_target_pairs={{0,1},{1,0},{2,3},{3,2},{4,5},{5,4},{6,7},{7,6},{8,9},{9,8},{10,11... | collective-permute-start | bytes 1769480 | tf_op jit(solution)/shard_map/ppermute | solution.py:473
  50.6 12.2 %collective-permute-start.2 = (bf16[256,256]{1,0:T(8,128)(2,1)S(1)}, bf16[256,256]{1,0:T(8,128)(2,1)S(1)}, u32[]{:S(2)}, u32[]{:S(2)}) collective-permute-start(bf16[256,256]{1,0:T(8,128)(2,1)S(1)} %get-tuple-element.38), channel_id=1, source_target_pairs={{0,2},{2,4},{4,6},{6,0},{1,3},{3,5},{5,7},{7,1},{8,10},{10,12},{12... | collective-permute-start | bytes 393224 | tf_op jit(solution)/shard_map/ppermute | solution.py:463
  50.9 11.8 %collective-permute-start.3 = (bf16[256,256]{1,0:T(8,128)(2,1)S(1)}, bf16[256,256]{1,0:T(8,128)(2,1)S(1)}, u32[]{:S(2)}, u32[]{:S(2)}) collective-permute-start(bf16[256,256]{1,0:T(8,128)(2,1)S(1)} %get-tuple-element.39), channel_id=1, source_target_pairs={{0,4},{2,6},{4,0},{6,2},{1,5},{3,7},{5,1},{7,3},{8,12},{10,14},{12... | collective-permute-start | bytes 393224 | tf_op jit(solution)/shard_map/ppermute | solution.py:463
  53.8 9.0 %collective-permute-start.4 = (bf16[256,256]{1,0:T(8,128)(2,1)S(1)}, bf16[256,256]{1,0:T(8,128)(2,1)S(1)}, u32[]{:S(2)}, u32[]{:S(2)}) collective-permute-start(bf16[256,256]{1,0:T(8,128)(2,1)S(1)} %get-tuple-element.40), channel_id=1, source_target_pairs={{0,6},{2,0},{4,2},{6,4},{1,7},{3,1},{5,3},{7,5},{8,14},{10,8},{12,... | collective-permute-start | bytes 393224 | tf_op jit(solution)/shard_map/ppermute | solution.py:463

commit v8 on v7

--- a/solution.py
+++ b/solution.py
@@ -64,12 +64,14 @@
 
 def encode_kernel(
     feat_ref, weight_ref, gain_ref, tgt_ref, q_ref, out_ref, row_ref,
-    feat_buf, weight_buf, gain_buf, tgt_buf, q_buf, sems,
+    feat_buf, weight_buf, gain_buf, tgt_buf, q_buf, out_buf, sems,
 ):
     row, begin = own_target_rows()
     pairs = [
-        (tgt_ref.at[pl.ds(begin, 16), :], tgt_buf), (q_ref, q_buf), (weight_ref, weight_buf),
-        (feat_ref, feat_buf), (gain_ref, gain_buf),
+        (tgt_ref.at[pl.ds(begin, 16), :], tgt_buf), (q_ref, q_buf), (feat_ref, feat_buf),
+        (weight_ref.at[pl.ds(0, HALF), :], weight_buf.at[pl.ds(0, HALF), :]),
+        (weight_ref.at[pl.ds(HALF, HALF), :], weight_buf.at[pl.ds(HALF, HALF), :]),
+        (gain_ref, gain_buf),
     ]
     copies = [pltpu.make_async_copy(a, b, sems.at[i]) for i, (a, b) in enumerate(pairs)]
     for copy in copies:
@@ -92,17 +94,34 @@
         hit = rank == first + float(k)
         chosen.append((one_hot(hit & ~odd), one_hot(hit & odd)))
     copies[1].wait()
-    out_ref[..., ROWS:] = jnp.broadcast_to(q_buf[...], (N_CLS, 2, D))
-    for copy in copies[2:]:
-        copy.wait()
-    hidden = dot(feat_buf[...], weight_buf[...])
+    leaving = []
+
+    def send(first, value):
+        window = pl.ds(first, value.shape[2])
+        out_buf[:, :, first : first + value.shape[2]] = value
+        at = 6 + len(leaving)
+        copy = pltpu.make_async_copy(
+            out_buf.at[:, :, window], out_ref.at[:, :, window], sems.at[at]
+        )
+        copy.start()
+        leaving.append(copy)
+
+    send(ROWS, jnp.broadcast_to(q_buf[...], (N_CLS, 2, D)))
+    copies[2].wait()
+    copies[3].wait()
+    hidden = dot(feat_buf[:, :HALF], weight_buf[:HALF, :])
+    copies[4].wait()
+    hidden += dot(feat_buf[:, HALF:], weight_buf[HALF:, :])
+    copies[5].wait()
     mean = jnp.mean(hidden * hidden, axis=1, keepdims=True)
     gain = jnp.concatenate([gain_buf[i : i + 1, :] for i in range(6)], axis=1)
     encoded = (hidden * lax.rsqrt(mean + 1e-06) * gain).astype(BF16)
     row_ref[...] = encoded
     for k, (even_rows, odd_rows) in enumerate(chosen):
         total = dot(even_rows, encoded[:, :HALF]) + dot(odd_rows, encoded[:, HALF:])
-        out_ref[..., k * HALF : (k + 1) * HALF] = total.astype(BF16).reshape(N_CLS, 2, HALF)
+        send(k * HALF, total.astype(BF16).reshape(N_CLS, 2, HALF))
+    for copy in leaving:
+        copy.wait()
 
 
 def hits_at(plane_ref, label):
@@ -264,11 +283,9 @@
 
 
 def old_kernel(
-    slot_ref, got_ref, own_ref, lab_ref, peak_ref, total_ref, grad_ref, own_buf, lab_buf, sems
+    slot_ref, got_ref, own_ref, lab_ref, out_ref, peak_ref, total_ref, grad_ref, lab_buf, sems
 ):
     slot = slot_ref[0]
-    own_copy = pltpu.make_async_copy(own_ref, own_buf, sems.at[OLD])
-    own_copy.start()
     copies = []
     for i in range(OLD):
         source = (i + (i >= slot).astype(jnp.int32)) * D
@@ -276,34 +293,34 @@
             pltpu.make_async_copy(lab_ref.at[pl.ds(source, D), :], lab_buf.at[i], sems.at[i])
         )
         copies[-1].start()
+    out_copy = pltpu.make_async_copy(own_ref, out_ref, sems.at[OLD])
+    out_copy.start()
     start = (jnp.full((QG, 1), -jnp.inf, F32), jnp.zeros((QG, 128), F32), jnp.zeros((QG, D), F32))
     peak, total, grads = absorb_all(
         start,
         got_ref[..., ROWS:].reshape(QG, D),
-        [own_buf] + [lab_buf.at[i] for i in range(OLD)],
-        [[own_copy]] + [[copy] for copy in copies],
+        [own_ref] + [lab_buf.at[i] for i in range(OLD)],
+        [[]] + [[copy] for copy in copies],
     )
     peak_ref[...] = jnp.broadcast_to(peak, (QG, 128))
     total_ref[...] = total
     grad_ref[...] = grads
+    out_copy.wait()
 
 
 def score_kernel(
     slot_ref, flag_ref, got_ref, own_ref, other_ref, peak_ref, total_ref, grad_ref, plane_ref,
     pos_ref, *refs
 ):
-    quarter_refs, (out_ref, own_buf, pos_buf, sem) = refs[:4], refs[4:]
+    quarter_refs, (out_ref, pos_buf) = refs[:4], refs[4:]
     rep = lax.axis_index("rep")
     slot = slot_ref[0]
-    own_copy = pltpu.make_async_copy(own_ref, own_buf, sem)
-    own_copy.start()
     queries = got_ref[..., ROWS:].reshape(QG, D)
     state = (peak_ref[:, :1], total_ref[...], grad_ref[...])
     peak, total, grads = absorb_all(state, queries, [other_ref], [[]])
     out_ref[..., :D] = grads.astype(BF16).reshape(N_CLS, 2, D)
     pos_buf[...] = pos_ref[...]
-    own_copy.wait()
-    for block, half in ((own_buf, rep), (other_ref, 1 - rep)):
+    for block, half in ((own_ref, rep), (other_ref, 1 - rep)):
         for part in range(3):
             tile = slot * 6 + half * 3 + part
 
@@ -390,18 +407,19 @@
     sending, encoded = pl.pallas_call(
         encode_kernel,
         out_shape=[
-            jax.ShapeDtypeStruct((N_CLS, 2, SEND), BF16),
+            pltpu.HBM((N_CLS, 2, SEND), BF16),
             jax.ShapeDtypeStruct((HALF, D), BF16),
         ],
         in_specs=[any_spec] * 5,
-        out_specs=[vmem_spec()] * 2,
+        out_specs=[any_spec, vmem_spec()],
         scratch_shapes=[
             pltpu.VMEM((HALF, D), BF16),
             pltpu.VMEM((D, D), BF16),
             pltpu.VMEM((6, 128), F32),
             pltpu.VMEM((16, 128), jnp.int32),
             pltpu.VMEM((1, 2, D), BF16),
-            pltpu.SemaphoreType.DMA((5,)),
+            pltpu.VMEM((N_CLS, 2, SEND), BF16),
+            pltpu.SemaphoreType.DMA((10,)),
         ],
         compiler_params=PARAMS,
         name="encode",
@@ -462,7 +480,7 @@
         pairs = [(x, (x + shift) % 4) for x in range(4)]
         along_x.append(lax.ppermute(quarters[shift], "cls_2", pairs))
 
-    refreshed = pl.pallas_call(
+    own = pl.pallas_call(
         refresh_kernel,
         out_shape=jax.ShapeDtypeStruct((HALF, D), BF16),
         in_specs=[vmem_spec()] * 3 + [any_spec],
@@ -470,20 +488,19 @@
         compiler_params=PARAMS,
         name="refresh",
     )(keys, got, free_vectors, quarters[0])
-    partner = lax.ppermute(refreshed, "rep", [(0, 1), (1, 0)])
-
-    own = in_hbm(refreshed)
-    state = pl.pallas_call(
+    partner = lax.ppermute(own, "rep", [(0, 1), (1, 0)])
+
+    refreshed, *state = pl.pallas_call(
         old_kernel,
         out_shape=[
+            pltpu.HBM((HALF, D), BF16),
             jax.ShapeDtypeStruct((QG, 128), F32),
             jax.ShapeDtypeStruct((QG, 128), F32),
             jax.ShapeDtypeStruct((QG, D), F32),
         ],
-        in_specs=[smem_spec(), vmem_spec(), any_spec, any_spec],
-        out_specs=[vmem_spec()] * 3,
+        in_specs=[smem_spec(), vmem_spec(), vmem_spec(), any_spec],
+        out_specs=[any_spec] + [vmem_spec()] * 3,
         scratch_shapes=[
-            pltpu.VMEM((HALF, D), BF16),
             pltpu.VMEM((OLD, D, D), BF16),
             pltpu.SemaphoreType.DMA((SLOTS,)),
         ],
@@ -494,12 +511,10 @@
     leaving = pl.pallas_call(
         score_kernel,
         out_shape=jax.ShapeDtypeStruct((N_CLS, 2, BACK), BF16),
-        in_specs=[smem_spec()] * 2 + [vmem_spec(), any_spec] + [vmem_spec()] * 10,
+        in_specs=[smem_spec()] * 2 + [vmem_spec()] * 12,
         out_specs=vmem_spec(),
         scratch_shapes=[
-            pltpu.VMEM((HALF, D), BF16),
             pltpu.VMEM((QG, D), F32),
-            pltpu.SemaphoreType.DMA,
         ],
         compiler_params=PARAMS,
         name="score",

time: 94.4 us -> 93.8 us (level)
  no operation moved by 1% of the time
where the time goes in v8:
time: 93.8 us; the launch traced here: 93.4 us
  blocking collectives  27 us (29%)
  Pallas kernels  25.3 us (27%)
  waiting for transfers between devices  20.1 us (21%)
  starting transfers between devices  19.6 us (21%)
  between operations  1.41 us (2%)
    all_to_all x1, blocking collectives, per_device(): back = lax.all_to_all(leaving, CLS, 0, 0, tiled=True)  27 us
    all_to_all x1, waiting for transfers between devices, per_device(): got = lax.all_to_all(sending, CLS, 0, 0, tiled=True)  20.1 us
    all_to_all x1, starting transfers between devices, per_device(): got = lax.all_to_all(sending, CLS, 0, 0, tiled=True)  15 us
    pallas_call x1, Pallas kernels, per_device(): pl.pallas_call(old_kernel, out_shape=[pltpu.HBM((HALF, D), BF16), jax.Sha...  7.82 us
    pallas_call x1, Pallas kernels, per_device(): pl.pallas_call(encode_kernel, out_shape=[pltpu.HBM((N_CLS, 2, SEND), BF16...  4.65 us
    pallas_call x1, Pallas kernels, per_device(): pl.pallas_call(positive_kernel, out_shape=jax.ShapeDtypeStruct((QG, D), F...  4.56 us
    ppermute x3, starting transfers between devices, per_device(): along_x.append(lax.ppermute(quarters[shift], 'cls_2', pairs))  4.36 us
    pallas_call x1, Pallas kernels, per_device(): pl.pallas_call(place_kernel, out_shape=[jax.ShapeDtypeStruct((8, QG), F32...  2.78 us
  transfers between devices with their start and end apart: 6, of which 1 were waited for; matrix products, arithmetic and copies ran while one was open for 0% of the time, Pallas kernels for 17%

profile of v8, /device:TPU:32, one launch (start us, length us, event | category | flops | bytes accessed | tf_op | source)
XLA Modules:
  0.0 93.4 jit_solution(8579666507615585078)
XLA Ops:
  0.6 0.0 copy-start
  0.6 4.7 %encode.1 = (bf16[128,2,1920]{2,1,0:T(2,128)(2,1)}, bf16[384,768]{1,0:T(8,128)(2,1)S(1)}) custom-call(bf16[384,768]{1,0:T(8,128)(2,1)} %feat_ref.1, bf16[768,768]{1,0:T(8,128)(2,1)} %weight_ref.1, f32[6,128]{1,0:T(8,128)} %bitcast.12, s32[768,128]{1,0:T(8,128)} %bitcast.10, bf16[1,2,768]{2,1,0:T(2,128)(2,1)} %q_ref.1), custom_call_target="tpu_custom_call" | custom-call | tf_op jit(solution)/shard_map/encode/pallas_call | solution.py:407
  5.3 15.0 %all-to-all-start = ((bf16[128,2,1920]{2,1,0:T(2,128)(2,1)}), bf16[128,2,1920]{2,1,0:T(2,128)(2,1)S(1)}, u32[]{:S(2)}, u32[]{:S(2)}) async-start(bf16[128,2,1920]{2,1,0:T(2,128)(2,1)} %get-tuple-element.26), calls=%async_computation | async-start | bytes 1966080 | tf_op jit(solution)/shard_map/all_to_all | solution.py:454
  21.0 2.8 %place.1 = (f32[8,256]{1,0:T(8,128)S(1)}, f32[4,256,128]{2,1,0:T(8,128)S(1)}, s32[1,128]{1,0:T(1,128)S(1)}, f32[256,768]{1,0:T(8,128)S(1)}, bf16[256,768]{1,0:T(8,128)(2,1)S(1)}) custom-call(s32[1]{0:T(128)} %bitcast.4.slot_ref, s32[768,128]{1,0:T(8,128)} %bitcast.11, s32[2,4,256]{2,1,0:T(4,128)} %bitcast.8, bf16[384,768]{1,0:T(8,128)(2,1)} %free_ref.3, ...), custom_call_target="tpu_custom_call" | custom-call | tf_op jit(solution)/shard_map/place/pallas_call | solution.py:433
  23.8 0.1 collective-permute-start
  23.9 4.6 %positive.1.old_ref.pos_ref = f32[256,768]{1,0:T(8,128)S(1)} custom-call(s32[1]{0:T(128)} %bitcast.5.slot_ref, s32[1,128]{1,0:T(1,128)S(1)} %get-tuple-element.25.flag_ref, f32[4,256,128]{2,1,0:T(8,128)S(1)} %get-tuple-element.28.plane_ref, bf16[6144,768]{1,0:T(8,128)(2,1)} %lab_ref.3), custom_call_target="tpu_custom_call" | custom-call | tf_op jit(solution)/shard_map/positive/pallas_call | solution.py:456
  28.4 0.0 collective-permute-done.came_ref
  28.4 0.6 quarter.1
  29.0 20.1 %all-to-all-done.got_ref = bf16[128,2,1920]{2,1,0:T(2,128)(2,1)S(1)} async-done(((bf16[128,2,1920]{2,1,0:T(2,128)(2,1)}), bf16[128,2,1920]{2,1,0:T(2,128)(2,1)S(1)}, u32[]{:S(2)}, u32[]{:S(2)}) %all-to-all-start) | async-done | bytes 983072 | tf_op jit(solution)/shard_map/all_to_all | solution.py:454
  49.1 0.0 copy-done
  49.1 0.0 copy-start.1
  49.1 0.8 refresh.1.own_ref
  49.9 0.1 collective-permute-start.1
  50.0 0.5 collective-permute-start.2
  50.5 2.8 %collective-permute-start.3 = (bf16[256,256]{1,0:T(8,128)(2,1)S(1)}, bf16[256,256]{1,0:T(8,128)(2,1)S(1)}, u32[]{:S(2)}, u32[]{:S(2)}) collective-permute-start(bf16[256,256]{1,0:T(8,128)(2,1)S(1)} %get-tuple-element.40), channel_id=1, source_target_pairs={{0,4},{2,6},{4,0},{6,2},{1,5},{3,7},{5,1},{7,3},{8,12},{10,14},{12... | collective-permute-start | bytes 393224 | tf_op jit(solution)/shard_map/ppermute | solution.py:481
  53.4 1.0 %collective-permute-start.4 = (bf16[256,256]{1,0:T(8,128)(2,1)S(1)}, bf16[256,256]{1,0:T(8,128)(2,1)S(1)}, u32[]{:S(2)}, u32[]{:S(2)}) collective-permute-start(bf16[256,256]{1,0:T(8,128)(2,1)S(1)} %get-tuple-element.41), channel_id=1, source_target_pairs={{0,6},{2,0},{4,2},{6,4},{1,7},{3,1},{5,3},{7,5},{8,14},{10,8},{12,... | collective-permute-start | bytes 393224 | tf_op jit(solution)/shard_map/ppermute | solution.py:481
  54.4 7.8 %old.1 = (bf16[384,768]{1,0:T(8,128)(2,1)}, f32[256,128]{1,0:T(8,128)S(1)}, f32[256,128]{1,0:T(8,128)S(1)}, f32[256,768]{1,0:T(8,128)S(1)}) custom-call(s32[1]{0:T(128)} %bitcast.6.slot_ref, bf16[128,2,1920]{2,1,0:T(2,128)(2,1)S(1)} %all-to-all-done.got_ref, bf16[384,768]{1,0:T(8,128)(2,1)S(1)} %refresh.1.own_ref, bf16[6144,768]{1,0:T(8,128)(2,1)} %lab_ref.3), custom_call_target="tpu_custom_call" | custom-call | tf_op jit(solution)/shard_map/old/pallas_call | solution.py:493
  62.2 0.0 collective-permute-done.1.other_ref
  62.2 0.0 collective-permute-done.2.refs_1_
  62.2 0.0 collective-permute-done.3.refs_2_
  62.3 0.0 collective-permute-done.4.refs_3_
  62.3 2.1 %score.1 = bf16[128,2,1024]{2,1,0:T(2,128)(2,1)S(1)} custom-call(s32[1]{0:T(128)} %bitcast.7.slot_ref, s32[1,128]{1,0:T(1,128)S(1)} %get-tuple-element.25.flag_ref, bf16[128,2,1920]{2,1,0:T(2,128)(2,1)S(1)} %all-to-all-done.got_ref, bf16[384,768]{1,0:T(8,128)(2,1)S(1)} %refresh.1.own_ref, bf16[384,768]{1,0:T(8,128)(2,1)S(1)} %collective-permute-done.1.other_ref, ...), custom_call_target="tpu_custom_call" | custom-call | tf_op jit(solution)/shard_map/score/pallas_call | solution.py:511
  64.4 27.0 %all_to_all.10.back_ref = bf16[128,2,1024]{2,1,0:T(2,128)(2,1)S(1)} all-to-all(bf16[128,2,1024]{2,1,0:T(2,128)(2,1)S(1)} %score.1), channel_id=1, replica_groups=mesh['cls_0'=4,'cls_1'=8,'cls_2'=4,'rep'=2] {'cls_0','cls_1','cls_2'}, dimensions={0} | all-to-all | bytes 1048576 | tf_op jit(solution)/shard_map/all_to_all | solution.py:522
  91.3 0.0 copy-done.1
  91.3 2.1 %finish.1 = (f32[1,2]{1,0:T(1,128)}, bf16[1,2,768]{2,1,0:T(2,128)(2,1)}) custom-call(s32[2,4,256]{2,1,0:T(4,128)S(1)} %bitcast.9, bf16[128,2,1024]{2,1,0:T(2,128)(2,1)S(1)} %all_to_all.10.back_ref), custom_call_target="tpu_custom_call" | custom-call | tf_op jit(solution)/shard_map/finish/pallas_call | solution.py:523
Async XLA Ops:
  0.6 48.5 %copy-start = (bf16[384,768]{1,0:T(8,128)(2,1)S(1)}, bf16[384,768]{1,0:T(8,128)(2,1)}, u32[]{:S(2)}) copy-start(bf16[384,768]{1,0:T(8,128)(2,1)} %free_ref.3) | copy-start | bytes 1769476
  5.3 43.8 %all-to-all-start = ((bf16[128,2,1920]{2,1,0:T(2,128)(2,1)}), bf16[128,2,1920]{2,1,0:T(2,128)(2,1)S(1)}, u32[]{:S(2)}, u32[]{:S(2)}) async-start(bf16[128,2,1920]{2,1,0:T(2,128)(2,1)} %get-tuple-element.26), calls=%async_computation | async-start | bytes 1966080 | tf_op jit(solution)/shard_map/all_to_all | solution.py:454
  23.8 4.7 %collective-permute-start = (bf16[256,768]{1,0:T(8,128)(2,1)S(1)}, bf16[256,768]{1,0:T(8,128)(2,1)S(1)}, u32[]{:S(2)}, u32[]{:S(2)}) collective-permute-start(bf16[256,768]{1,0:T(8,128)(2,1)S(1)} %get-tuple-element.30), channel_id=1, source_target_pairs={{0,1},{1,0},{2,3},{3,2},{4,5},{5,4},{6,7},{7,6},{8,9},{9,8},{10,11... | collective-permute-start | bytes 1179656 | tf_op jit(solution)/shard_map/ppermute | solution.py:469
  49.1 42.2 %copy-start.1 = (s32[2,256,4]{1,2,0:T(4,128)S(1)}, s32[2,256,4]{1,2,0:T(4,128)}, u32[]{:S(2)}) copy-start(s32[2,256,4]{1,2,0:T(4,128)} %param.10) | copy-start | bytes 24580
  49.9 12.3 %collective-permute-start.1 = (bf16[384,768]{1,0:T(8,128)(2,1)S(1)}, bf16[384,768]{1,0:T(8,128)(2,1)S(1)}, u32[]{:S(2)}, u32[]{:S(2)}) collective-permute-start(bf16[384,768]{1,0:T(8,128)(2,1)S(1)} %refresh.1.own_ref), channel_id=1, source_target_pairs={{0,1},{1,0},{2,3},{3,2},{4,5},{5,4},{6,7},{7,6},{8,9},{9,8},{10,11... | collective-permute-start | bytes 1769480 | tf_op jit(solution)/shard_map/ppermute | solution.py:491
  50.0 12.2 %collective-permute-start.2 = (bf16[256,256]{1,0:T(8,128)(2,1)S(1)}, bf16[256,256]{1,0:T(8,128)(2,1)S(1)}, u32[]{:S(2)}, u32[]{:S(2)}) collective-permute-start(bf16[256,256]{1,0:T(8,128)(2,1)S(1)} %get-tuple-element.39), channel_id=1, source_target_pairs={{0,2},{2,4},{4,6},{6,0},{1,3},{3,5},{5,7},{7,1},{8,10},{10,12},{12... | collective-permute-start | bytes 393224 | tf_op jit(solution)/shard_map/ppermute | solution.py:481
  50.5 11.7 %collective-permute-start.3 = (bf16[256,256]{1,0:T(8,128)(2,1)S(1)}, bf16[256,256]{1,0:T(8,128)(2,1)S(1)}, u32[]{:S(2)}, u32[]{:S(2)}) collective-permute-start(bf16[256,256]{1,0:T(8,128)(2,1)S(1)} %get-tuple-element.40), channel_id=1, source_target_pairs={{0,4},{2,6},{4,0},{6,2},{1,5},{3,7},{5,1},{7,3},{8,12},{10,14},{12... | collective-permute-start | bytes 393224 | tf_op jit(solution)/shard_map/ppermute | solution.py:481
  53.4 8.9 %collective-permute-start.4 = (bf16[256,256]{1,0:T(8,128)(2,1)S(1)}, bf16[256,256]{1,0:T(8,128)(2,1)S(1)}, u32[]{:S(2)}, u32[]{:S(2)}) collective-permute-start(bf16[256,256]{1,0:T(8,128)(2,1)S(1)} %get-tuple-element.41), channel_id=1, source_target_pairs={{0,6},{2,0},{4,2},{6,4},{1,7},{3,1},{5,3},{7,5},{8,14},{10,8},{12,... | collective-permute-start | bytes 393224 | tf_op jit(solution)/shard_map/ppermute | solution.py:481

commit v9 on v7

--- a/solution.py
+++ b/solution.py
@@ -264,11 +264,9 @@
 
 
 def old_kernel(
-    slot_ref, got_ref, own_ref, lab_ref, peak_ref, total_ref, grad_ref, own_buf, lab_buf, sems
+    slot_ref, got_ref, own_ref, lab_ref, out_ref, peak_ref, total_ref, grad_ref, lab_buf, sems
 ):
     slot = slot_ref[0]
-    own_copy = pltpu.make_async_copy(own_ref, own_buf, sems.at[OLD])
-    own_copy.start()
     copies = []
     for i in range(OLD):
         source = (i + (i >= slot).astype(jnp.int32)) * D
@@ -276,34 +274,34 @@
             pltpu.make_async_copy(lab_ref.at[pl.ds(source, D), :], lab_buf.at[i], sems.at[i])
         )
         copies[-1].start()
+    out_copy = pltpu.make_async_copy(own_ref, out_ref, sems.at[OLD])
+    out_copy.start()
     start = (jnp.full((QG, 1), -jnp.inf, F32), jnp.zeros((QG, 128), F32), jnp.zeros((QG, D), F32))
     peak, total, grads = absorb_all(
         start,
         got_ref[..., ROWS:].reshape(QG, D),
-        [own_buf] + [lab_buf.at[i] for i in range(OLD)],
-        [[own_copy]] + [[copy] for copy in copies],
+        [own_ref] + [lab_buf.at[i] for i in range(OLD)],
+        [[]] + [[copy] for copy in copies],
     )
     peak_ref[...] = jnp.broadcast_to(peak, (QG, 128))
     total_ref[...] = total
     grad_ref[...] = grads
+    out_copy.wait()
 
 
 def score_kernel(
     slot_ref, flag_ref, got_ref, own_ref, other_ref, peak_ref, total_ref, grad_ref, plane_ref,
     pos_ref, *refs
 ):
-    quarter_refs, (out_ref, own_buf, pos_buf, sem) = refs[:4], refs[4:]
+    quarter_refs, (out_ref, pos_buf) = refs[:4], refs[4:]
     rep = lax.axis_index("rep")
     slot = slot_ref[0]
-    own_copy = pltpu.make_async_copy(own_ref, own_buf, sem)
-    own_copy.start()
     queries = got_ref[..., ROWS:].reshape(QG, D)
     state = (peak_ref[:, :1], total_ref[...], grad_ref[...])
     peak, total, grads = absorb_all(state, queries, [other_ref], [[]])
     out_ref[..., :D] = grads.astype(BF16).reshape(N_CLS, 2, D)
     pos_buf[...] = pos_ref[...]
-    own_copy.wait()
-    for block, half in ((own_buf, rep), (other_ref, 1 - rep)):
+    for block, half in ((own_ref, rep), (other_ref, 1 - rep)):
         for part in range(3):
             tile = slot * 6 + half * 3 + part
 
@@ -462,7 +460,7 @@
         pairs = [(x, (x + shift) % 4) for x in range(4)]
         along_x.append(lax.ppermute(quarters[shift], "cls_2", pairs))
 
-    refreshed = pl.pallas_call(
+    own = pl.pallas_call(
         refresh_kernel,
         out_shape=jax.ShapeDtypeStruct((HALF, D), BF16),
         in_specs=[vmem_spec()] * 3 + [any_spec],
@@ -470,20 +468,19 @@
         compiler_params=PARAMS,
         name="refresh",
     )(keys, got, free_vectors, quarters[0])
-    partner = lax.ppermute(refreshed, "rep", [(0, 1), (1, 0)])
-
-    own = in_hbm(refreshed)
-    state = pl.pallas_call(
+    partner = lax.ppermute(own, "rep", [(0, 1), (1, 0)])
+
+    refreshed, *state = pl.pallas_call(
         old_kernel,
         out_shape=[
+            pltpu.HBM((HALF, D), BF16),
             jax.ShapeDtypeStruct((QG, 128), F32),
             jax.ShapeDtypeStruct((QG, 128), F32),
             jax.ShapeDtypeStruct((QG, D), F32),
         ],
-        in_specs=[smem_spec(), vmem_spec(), any_spec, any_spec],
-        out_specs=[vmem_spec()] * 3,
+        in_specs=[smem_spec(), vmem_spec(), vmem_spec(), any_spec],
+        out_specs=[any_spec] + [vmem_spec()] * 3,
         scratch_shapes=[
-            pltpu.VMEM((HALF, D), BF16),
             pltpu.VMEM((OLD, D, D), BF16),
             pltpu.SemaphoreType.DMA((SLOTS,)),
         ],
@@ -494,12 +491,10 @@
     leaving = pl.pallas_call(
         score_kernel,
         out_shape=jax.ShapeDtypeStruct((N_CLS, 2, BACK), BF16),
-        in_specs=[smem_spec()] * 2 + [vmem_spec(), any_spec] + [vmem_spec()] * 10,
+        in_specs=[smem_spec()] * 2 + [vmem_spec()] * 12,
         out_specs=vmem_spec(),
         scratch_shapes=[
-            pltpu.VMEM((HALF, D), BF16),
             pltpu.VMEM((QG, D), F32),
-            pltpu.SemaphoreType.DMA,
         ],
         compiler_params=PARAMS,
         name="score",

time: 94.4 us -> 93.5 us (level)
  Pallas kernels: 26 us -> 25 us
where the time goes in v9:
time: 93.5 us; the launch traced here: 93.1 us
  blocking collectives  26.9 us (29%)
  Pallas kernels  25 us (27%)
  waiting for transfers between devices  20.2 us (22%)
  starting transfers between devices  19.6 us (21%)
  between operations  1.4 us (1%)
    all_to_all x1, blocking collectives, per_device(): back = lax.all_to_all(leaving, CLS, 0, 0, tiled=True)  26.9 us
    all_to_all x1, waiting for transfers between devices, per_device(): got = lax.all_to_all(sending, CLS, 0, 0, tiled=True)  20.1 us
    all_to_all x1, starting transfers between devices, per_device(): got = lax.all_to_all(sending, CLS, 0, 0, tiled=True)  15 us
    pallas_call x1, Pallas kernels, per_device(): pl.pallas_call(old_kernel, out_shape=[pltpu.HBM((HALF, D), BF16), jax.Sha...  7.83 us
    pallas_call x1, Pallas kernels, per_device(): pl.pallas_call(positive_kernel, out_shape=jax.ShapeDtypeStruct((QG, D), F...  4.52 us
    pallas_call x1, Pallas kernels, per_device(): pl.pallas_call(encode_kernel, out_shape=[jax.ShapeDtypeStruct((N_CLS, 2,...  4.43 us
    ppermute x3, starting transfers between devices, per_device(): along_x.append(lax.ppermute(quarters[shift], 'cls_2', pairs))  4.36 us
    pallas_call x1, Pallas kernels, per_device(): pl.pallas_call(place_kernel, out_shape=[jax.ShapeDtypeStruct((8, QG), F32...  2.76 us
  transfers between devices with their start and end apart: 6, of which 1 were waited for; matrix products, arithmetic and copies ran while one was open for 0% of the time, Pallas kernels for 17%

profile of v9, /device:TPU:32, one launch (start us, length us, event | category | flops | bytes accessed | tf_op | source)
XLA Modules:
  0.0 93.1 jit_solution(15277198006555260823)
XLA Ops:
  0.6 0.0 copy-start
  0.6 4.4 %encode.1 = (bf16[128,2,1920]{2,1,0:T(2,128)(2,1)}, bf16[384,768]{1,0:T(8,128)(2,1)S(1)}) custom-call(bf16[384,768]{1,0:T(8,128)(2,1)} %feat_ref.1, bf16[768,768]{1,0:T(8,128)(2,1)} %weight_ref.1, f32[6,128]{1,0:T(8,128)} %bitcast.12, s32[768,128]{1,0:T(8,128)} %bitcast.10, bf16[1,2,768]{2,1,0:T(2,128)(2,1)} %q_ref.1), custom_call_target="tpu_custom_call" | custom-call | tf_op jit(solution)/shard_map/encode/pallas_call | solution.py:388
  5.1 15.0 %all-to-all-start = ((bf16[128,2,1920]{2,1,0:T(2,128)(2,1)}), bf16[128,2,1920]{2,1,0:T(2,128)(2,1)S(1)}, u32[]{:S(2)}, u32[]{:S(2)}) async-start(bf16[128,2,1920]{2,1,0:T(2,128)(2,1)} %get-tuple-element.26), calls=%async_computation | async-start | bytes 1966080 | tf_op jit(solution)/shard_map/all_to_all | solution.py:434
  20.7 2.8 %place.1 = (f32[8,256]{1,0:T(8,128)S(1)}, f32[4,256,128]{2,1,0:T(8,128)S(1)}, s32[1,128]{1,0:T(1,128)S(1)}, f32[256,768]{1,0:T(8,128)S(1)}, bf16[256,768]{1,0:T(8,128)(2,1)S(1)}) custom-call(s32[1]{0:T(128)} %bitcast.4.slot_ref, s32[768,128]{1,0:T(8,128)} %bitcast.11, s32[2,4,256]{2,1,0:T(4,128)} %bitcast.8, bf16[384,768]{1,0:T(8,128)(2,1)} %free_ref.3, ...), custom_call_target="tpu_custom_call" | custom-call | tf_op jit(solution)/shard_map/place/pallas_call | solution.py:413
  23.5 0.1 collective-permute-start
  23.6 4.5 %positive.1.old_ref.pos_ref = f32[256,768]{1,0:T(8,128)S(1)} custom-call(s32[1]{0:T(128)} %bitcast.5.slot_ref, s32[1,128]{1,0:T(1,128)S(1)} %get-tuple-element.25.flag_ref, f32[4,256,128]{2,1,0:T(8,128)S(1)} %get-tuple-element.28.plane_ref, bf16[6144,768]{1,0:T(8,128)(2,1)} %lab_ref.3), custom_call_target="tpu_custom_call" | custom-call | tf_op jit(solution)/shard_map/positive/pallas_call | solution.py:436
  28.1 0.0 collective-permute-done.came_ref
  28.2 0.6 quarter.1
  28.8 20.1 %all-to-all-done.got_ref = bf16[128,2,1920]{2,1,0:T(2,128)(2,1)S(1)} async-done(((bf16[128,2,1920]{2,1,0:T(2,128)(2,1)}), bf16[128,2,1920]{2,1,0:T(2,128)(2,1)S(1)}, u32[]{:S(2)}, u32[]{:S(2)}) %all-to-all-start) | async-done | bytes 983072 | tf_op jit(solution)/shard_map/all_to_all | solution.py:434
  48.9 0.0 copy-done
  48.9 0.0 copy-start.1
  48.9 0.8 refresh.1.own_ref
  49.7 0.1 collective-permute-start.1
  49.8 0.5 collective-permute-start.2
  50.3 2.8 %collective-permute-start.3 = (bf16[256,256]{1,0:T(8,128)(2,1)S(1)}, bf16[256,256]{1,0:T(8,128)(2,1)S(1)}, u32[]{:S(2)}, u32[]{:S(2)}) collective-permute-start(bf16[256,256]{1,0:T(8,128)(2,1)S(1)} %get-tuple-element.40), channel_id=1, source_target_pairs={{0,4},{2,6},{4,0},{6,2},{1,5},{3,7},{5,1},{7,3},{8,12},{10,14},{12... | collective-permute-start | bytes 393224 | tf_op jit(solution)/shard_map/ppermute | solution.py:461
  53.1 1.0 %collective-permute-start.4 = (bf16[256,256]{1,0:T(8,128)(2,1)S(1)}, bf16[256,256]{1,0:T(8,128)(2,1)S(1)}, u32[]{:S(2)}, u32[]{:S(2)}) collective-permute-start(bf16[256,256]{1,0:T(8,128)(2,1)S(1)} %get-tuple-element.41), channel_id=1, source_target_pairs={{0,6},{2,0},{4,2},{6,4},{1,7},{3,1},{5,3},{7,5},{8,14},{10,8},{12,... | collective-permute-start | bytes 393224 | tf_op jit(solution)/shard_map/ppermute | solution.py:461
  54.2 7.8 %old.1 = (bf16[384,768]{1,0:T(8,128)(2,1)}, f32[256,128]{1,0:T(8,128)S(1)}, f32[256,128]{1,0:T(8,128)S(1)}, f32[256,768]{1,0:T(8,128)S(1)}) custom-call(s32[1]{0:T(128)} %bitcast.6.slot_ref, bf16[128,2,1920]{2,1,0:T(2,128)(2,1)S(1)} %all-to-all-done.got_ref, bf16[384,768]{1,0:T(8,128)(2,1)S(1)} %refresh.1.own_ref, bf16[6144,768]{1,0:T(8,128)(2,1)} %lab_ref.3), custom_call_target="tpu_custom_call" | custom-call | tf_op jit(solution)/shard_map/old/pallas_call | solution.py:473
  62.0 0.0 collective-permute-done.1.other_ref
  62.0 0.0 collective-permute-done.2.refs_1_
  62.0 0.0 collective-permute-done.3.refs_2_
  62.0 0.0 collective-permute-done.4.refs_3_
  62.1 2.1 %score.1 = bf16[128,2,1024]{2,1,0:T(2,128)(2,1)S(1)} custom-call(s32[1]{0:T(128)} %bitcast.7.slot_ref, s32[1,128]{1,0:T(1,128)S(1)} %get-tuple-element.25.flag_ref, bf16[128,2,1920]{2,1,0:T(2,128)(2,1)S(1)} %all-to-all-done.got_ref, bf16[384,768]{1,0:T(8,128)(2,1)S(1)} %refresh.1.own_ref, bf16[384,768]{1,0:T(8,128)(2,1)S(1)} %collective-permute-done.1.other_ref, ...), custom_call_target="tpu_custom_call" | custom-call | tf_op jit(solution)/shard_map/score/pallas_call | solution.py:491
  64.1 26.9 %all_to_all.10.back_ref = bf16[128,2,1024]{2,1,0:T(2,128)(2,1)S(1)} all-to-all(bf16[128,2,1024]{2,1,0:T(2,128)(2,1)S(1)} %score.1), channel_id=1, replica_groups=mesh['cls_0'=4,'cls_1'=8,'cls_2'=4,'rep'=2] {'cls_0','cls_1','cls_2'}, dimensions={0} | all-to-all | bytes 1048576 | tf_op jit(solution)/shard_map/all_to_all | solution.py:502
  91.0 0.0 copy-done.1
  91.0 2.1 %finish.1 = (f32[1,2]{1,0:T(1,128)}, bf16[1,2,768]{2,1,0:T(2,128)(2,1)}) custom-call(s32[2,4,256]{2,1,0:T(4,128)S(1)} %bitcast.9, bf16[128,2,1024]{2,1,0:T(2,128)(2,1)S(1)} %all_to_all.10.back_ref), custom_call_target="tpu_custom_call" | custom-call | tf_op jit(solution)/shard_map/finish/pallas_call | solution.py:503
Async XLA Ops:
  0.6 48.3 %copy-start = (bf16[384,768]{1,0:T(8,128)(2,1)S(1)}, bf16[384,768]{1,0:T(8,128)(2,1)}, u32[]{:S(2)}) copy-start(bf16[384,768]{1,0:T(8,128)(2,1)} %free_ref.3) | copy-start | bytes 1769476
  5.1 43.8 %all-to-all-start = ((bf16[128,2,1920]{2,1,0:T(2,128)(2,1)}), bf16[128,2,1920]{2,1,0:T(2,128)(2,1)S(1)}, u32[]{:S(2)}, u32[]{:S(2)}) async-start(bf16[128,2,1920]{2,1,0:T(2,128)(2,1)} %get-tuple-element.26), calls=%async_computation | async-start | bytes 1966080 | tf_op jit(solution)/shard_map/all_to_all | solution.py:434
  23.5 4.6 %collective-permute-start = (bf16[256,768]{1,0:T(8,128)(2,1)S(1)}, bf16[256,768]{1,0:T(8,128)(2,1)S(1)}, u32[]{:S(2)}, u32[]{:S(2)}) collective-permute-start(bf16[256,768]{1,0:T(8,128)(2,1)S(1)} %get-tuple-element.30), channel_id=1, source_target_pairs={{0,1},{1,0},{2,3},{3,2},{4,5},{5,4},{6,7},{7,6},{8,9},{9,8},{10,11... | collective-permute-start | bytes 1179656 | tf_op jit(solution)/shard_map/ppermute | solution.py:449
  48.9 42.1 %copy-start.1 = (s32[2,256,4]{1,2,0:T(4,128)S(1)}, s32[2,256,4]{1,2,0:T(4,128)}, u32[]{:S(2)}) copy-start(s32[2,256,4]{1,2,0:T(4,128)} %param.10) | copy-start | bytes 24580
  49.7 12.3 %collective-permute-start.1 = (bf16[384,768]{1,0:T(8,128)(2,1)S(1)}, bf16[384,768]{1,0:T(8,128)(2,1)S(1)}, u32[]{:S(2)}, u32[]{:S(2)}) collective-permute-start(bf16[384,768]{1,0:T(8,128)(2,1)S(1)} %refresh.1.own_ref), channel_id=1, source_target_pairs={{0,1},{1,0},{2,3},{3,2},{4,5},{5,4},{6,7},{7,6},{8,9},{9,8},{10,11... | collective-permute-start | bytes 1769480 | tf_op jit(solution)/shard_map/ppermute | solution.py:471
  49.8 12.2 %collective-permute-start.2 = (bf16[256,256]{1,0:T(8,128)(2,1)S(1)}, bf16[256,256]{1,0:T(8,128)(2,1)S(1)}, u32[]{:S(2)}, u32[]{:S(2)}) collective-permute-start(bf16[256,256]{1,0:T(8,128)(2,1)S(1)} %get-tuple-element.39), channel_id=1, source_target_pairs={{0,2},{2,4},{4,6},{6,0},{1,3},{3,5},{5,7},{7,1},{8,10},{10,12},{12... | collective-permute-start | bytes 393224 | tf_op jit(solution)/shard_map/ppermute | solution.py:461
  50.3 11.8 %collective-permute-start.3 = (bf16[256,256]{1,0:T(8,128)(2,1)S(1)}, bf16[256,256]{1,0:T(8,128)(2,1)S(1)}, u32[]{:S(2)}, u32[]{:S(2)}) collective-permute-start(bf16[256,256]{1,0:T(8,128)(2,1)S(1)} %get-tuple-element.40), channel_id=1, source_target_pairs={{0,4},{2,6},{4,0},{6,2},{1,5},{3,7},{5,1},{7,3},{8,12},{10,14},{12... | collective-permute-start | bytes 393224 | tf_op jit(solution)/shard_map/ppermute | solution.py:461
  53.1 8.9 %collective-permute-start.4 = (bf16[256,256]{1,0:T(8,128)(2,1)S(1)}, bf16[256,256]{1,0:T(8,128)(2,1)S(1)}, u32[]{:S(2)}, u32[]{:S(2)}) collective-permute-start(bf16[256,256]{1,0:T(8,128)(2,1)S(1)} %get-tuple-element.41), channel_id=1, source_target_pairs={{0,6},{2,0},{4,2},{6,4},{1,7},{3,1},{5,3},{7,5},{8,14},{10,8},{12,... | collective-permute-start | bytes 393224 | tf_op jit(solution)/shard_map/ppermute | solution.py:461
